TPU v7x, 32 devices: a whole 2x2x4 slice. The times are simulated.
32 devices in a mesh: kpt: 4 (over y, x), pw: 8 (over z, core).
Axes of the slice: x: 2, y: 2, z: 4, core: 2. Of those that a mesh axis runs over, the one named last changes fastest.
Arguments:
- energies: float32 [16, 512], P('kpt', 'pw'), may hold values from 0.5 to 3
- current: float32 [2, 16, 512], P(None, 'kpt', 'pw'), may hold values from -40 to 40
- previous: float32 [2, 16, 512], P(None, 'kpt', 'pw'), may hold values from -6 to 6
- previous_beta: float32 [2], replicated, may hold values from 0.5 to 2
- pair_left: bfloat16 [16, 512, 4096], P('kpt', None, 'pw'), may hold values from -0.09375 to 0.09375
- pair_right: bfloat16 [16, 512, 4096], P('kpt', None, 'pw'), may hold values from -0.25 to 0.25
- screened: bfloat16 [16, 4096, 4096], P('kpt', 'pw'), may hold values from -0.0234375 to 0.0234375
- momentum_index: int32 [16, 16], replicated, may hold values from 0 to 15, each once within a row
Outputs:
- last_vector: float32 [2, 16, 512], P(None, 'kpt', 'pw')
- prior_vector: float32 [2, 16, 512], P(None, 'kpt', 'pw')
- alpha_terms: float32 [2, 3], replicated
- beta_terms: float32 [2, 3], replicated
Inputs may be any that keep to these rules, and one draw needn't show every extreme that they name: Each row of momentum_index names every index from 0 to 15 once.
All inputs are finite; a program needn't handle non-finite values.
Results may differ from a plain program's by a relative error of at most 0.003.
Values may be sent and summed in bfloat16 or wider, within the bound.
No kernel may reach another device: no remote copies, remote signals or barrier semaphores. Data moves between devices by JAX's collectives and lax.ppermute only.
A program may use at most 128 MiB of HBM per device.

v0:
```python
import jax
import jax.numpy as jnp
from jax import lax
from jax.sharding import PartitionSpec as P

STEPS = 3


epsilon = 1e-06


def screened_images(density, screened):
    kpoint_rows = lax.all_gather(density, "kpt", axis=0, tiled=True)
    return jnp.einsum(
        "qsg,kvg->qkvs",
        screened,
        lax.all_gather(kpoint_rows, "pw", axis=2, tiled=True),
        preferred_element_type=jnp.float32,
    )


def on_device(
    energies, current, previous, previous_beta, pair_left, pair_right, screened, momentum_index
):
    kpoint_total = momentum_index.shape[0]
    band_total = pair_left.shape[1]
    entries = kpoint_total * band_total
    qcount = screened.shape[0]
    qpoints = lax.axis_index("kpt") * qcount + jnp.arange(qcount, dtype=jnp.int32)
    selector = (momentum_index[None, :, :] == qpoints[:, None, None]).astype(jnp.float32)
    vector, earlier, levels = (current, previous, energies)
    beta_before = previous_beta
    alpha_list = []
    beta_list = []
    for turn_index in range(STEPS):
        rounded = vector.astype(jnp.bfloat16)
        rounded = lax.all_gather(rounded, "pw", axis=2, tiled=True)
        density = jnp.einsum(
            "kcg,vkc->kvg", pair_right, rounded, preferred_element_type=jnp.float32
        ).astype(jnp.bfloat16)
        images = screened_images(density, screened)
        partial_field = jnp.einsum(
            "qjk,qkvs->jvs",
            selector,
            images,
            precision=lax.Precision.HIGHEST,
            preferred_element_type=jnp.float32,
        )
        potential = lax.psum_scatter(partial_field, "kpt", scatter_dimension=0, tiled=True).astype(
            jnp.bfloat16
        )
        partial_direct = jnp.einsum(
            "kcs,kvs->vkc", pair_left, potential, preferred_element_type=jnp.float32
        )
        direct = lax.psum_scatter(partial_direct, "pw", scatter_dimension=2, tiled=True)
        applied = levels[None] * vector - direct - beta_before[:, None, None] * earlier
        vector_own = vector
        cross_sum, square_sum, vector_sum = lax.psum(
            (
                jnp.sum(vector_own * applied, axis=(1, 2)),
                jnp.sum(applied * applied, axis=(1, 2)),
                jnp.sum(vector_own * vector_own, axis=(1, 2)),
            ),
            ("kpt", "pw"),
        )
        alpha_now = cross_sum / entries
        mean_square = (
            square_sum / entries
            - 2.0 * alpha_now * (cross_sum / entries)
            + alpha_now * alpha_now * (vector_sum / entries)
        )
        beta_now = jnp.sqrt(mean_square + epsilon)
        residual = applied - alpha_now[:, None, None] * vector
        earlier = vector
        vector = residual / beta_now[:, None, None]
        beta_before = beta_now
        alpha_list.append(alpha_now)
        beta_list.append(beta_now)
    return (vector, earlier, jnp.stack(alpha_list, axis=1), jnp.stack(beta_list, axis=1))


def solution(mesh):
    return jax.shard_map(
        on_device,
        mesh=mesh,
        in_specs=(
            P("kpt", "pw"),
            P(None, "kpt", "pw"),
            P(None, "kpt", "pw"),
            P(),
            P("kpt", None, "pw"),
            P("kpt", None, "pw"),
            P("kpt", "pw", None),
            P(),
        ),
        out_specs=(P(None, "kpt", "pw"), P(None, "kpt", "pw"), P(), P()),
        check_vma=False,
    )
```

profile of v0, /device:TPU:0, one launch (start us, length us, event | category | flops | bytes accessed | tf_op | source)
XLA Modules:
  0.0 434.1 jit_solution(2461469843560152316)
XLA Ops:
  7.2 0.0 reduce-scatter.10.cloned.1.call-start
  7.3 0.8 convert_element_type.28
  8.1 0.1 copy.33
  8.2 15.9 %all_gather.27 = bf16[2,4,512]{1,0,2:T(2,128)(2,1)S(1)} all-gather(bf16[2,4,64]{1,0,2:T(2,128)(2,1)S(1)} %copy.33), channel_id=1, replica_groups=mesh['kpt'=4,'pw'=8] {'pw'}, dimensions={2}, use_global_device_ids=true | all-gather | bytes 9216 | tf_op jit(solution)/shard_map/all_gather | solution.py:37
  24.1 0.1 copy.34
  24.3 0.4 convolution_convert_fusion.2
  24.7 8.2 %all_gather.28 = bf16[16,2,512]{2,1,0:T(2,128)(2,1)S(1)} all-gather(bf16[4,2,512]{2,1,0:T(2,128)(2,1)S(1)} %convolution_convert_fusion.2), channel_id=1, replica_groups=mesh['kpt'=4,'pw'=8] {'kpt'}, dimensions={0}, use_global_device_ids=true | all-gather | bytes 40960 | tf_op jit(solution)/shard_map/all_gather | solution.py:13
  32.9 14.3 %all_gather.29 = bf16[16,2,4096]{2,0,1:T(8,128)(2,1)S(1)} all-gather(bf16[16,2,512]{2,0,1:T(8,128)(2,1)S(1)} %copy.35), channel_id=1, replica_groups=mesh['kpt'=4,'pw'=8] {'pw'}, dimensions={2}, use_global_device_ids=true | all-gather | bytes 294912 | tf_op jit(solution)/shard_map/all_gather | solution.py:17
  47.2 10.8 %fusion.6 = f32[4,16,2,512]{3,1,0,2:T(8,128)S(1)} fusion(bf16[4,512,4096]{2,1,0:T(8,128)(2,1)} %param.14, bf16[16,2,4096]{2,0,1:T(8,128)(2,1)S(1)} %all_gather.29), kind=kOutput, calls=%fused_computation.6 | convolution fusion | flops 536870912 | bytes 17301504 | tf_op jit(solution)/shard_map/qsg,kvg->qkvs/dot_general | solution.py:14
  58.0 0.3 convolution_bitcast_fusion.2
  58.3 0.1 copy.36
  58.4 16.0 %all-reduce = bf16[16,2,512]{2,1,0:T(2,128)(2,1)S(1)} all-reduce(f32[16,2,512]{2,1,0:T(2,128)S(1)} %copy.36), channel_id=2, replica_groups=mesh['kpt'=4,'pw'=8] {'kpt'}, use_global_device_ids=true, to_apply=%region_0.0.clone | all-reduce | flops 16384 | bytes 98304
  74.5 0.6 dynamic-slice
  75.8 2.3 convolution_bitcast_fusion.5
  78.0 0.4 copy.56
  78.5 1.2 reshape.29
  79.6 0.0 reduce-scatter.12.cloned.1.call-start
  79.7 30.9 %reduce-scatter.10.cloned.1.call-done = f32[64,8]{1,0:T(8,128)} async-done(((f32[512,8]{1,0:T(8,128)}), f32[64,8]{1,0:T(8,128)}) %reduce-scatter.10.cloned.1.call-update) | async-done | bytes 2064
  110.5 0.9 reshape.30
  111.4 0.1 copy.37
  111.6 0.2 multiply_reduce_fusion.7
  111.7 37.8 %all-reduce.5 = (f32[2]{0:T(128)S(1)}, f32[2]{0:T(128)S(1)}, f32[2]{0:T(128)S(1)}) all-reduce(f32[2]{0:T(128)S(1)} %get-tuple-element.24, f32[2]{0:T(128)S(1)} %get-tuple-element.23, f32[2]{0:T(128)S(1)} %get-tuple-element.22), channel_id=1, replica_groups=mesh['kpt'=4,'pw'=8] {'kpt','pw'}, use_global_device_ids=true, to_apply=%region_7.0 | all-reduce | flops 6 | bytes 48 | tf_op jit(solution)/shard_map/psum | solution.py:58
  149.6 0.1 fusion.37
  149.6 0.1 copy.38
  149.8 14.9 %all_gather.30 = bf16[2,4,512]{1,0,2:T(2,128)(2,1)S(1)} all-gather(bf16[2,4,64]{1,0,2:T(2,128)(2,1)S(1)} %copy.38), channel_id=1, replica_groups=mesh['kpt'=4,'pw'=8] {'pw'}, dimensions={2}, use_global_device_ids=true | all-gather | bytes 9216 | tf_op jit(solution)/shard_map/all_gather | solution.py:37
  164.6 0.1 copy.39
  164.8 0.4 convolution_convert_fusion.1
  165.2 9.0 %all_gather.31 = bf16[16,2,512]{2,1,0:T(2,128)(2,1)S(1)} all-gather(bf16[4,2,512]{2,1,0:T(2,128)(2,1)S(1)} %convolution_convert_fusion.1), channel_id=1, replica_groups=mesh['kpt'=4,'pw'=8] {'kpt'}, dimensions={0}, use_global_device_ids=true | all-gather | bytes 40960 | tf_op jit(solution)/shard_map/all_gather | solution.py:13
  174.1 14.4 %all_gather.32 = bf16[16,2,4096]{2,0,1:T(8,128)(2,1)S(1)} all-gather(bf16[16,2,512]{2,0,1:T(8,128)(2,1)S(1)} %copy.40), channel_id=1, replica_groups=mesh['kpt'=4,'pw'=8] {'pw'}, dimensions={2}, use_global_device_ids=true | all-gather | bytes 294912 | tf_op jit(solution)/shard_map/all_gather | solution.py:17
  188.5 10.8 %fusion.9 = f32[4,16,2,512]{3,1,0,2:T(8,128)S(1)} fusion(bf16[4,512,4096]{2,1,0:T(8,128)(2,1)} %param.14, bf16[16,2,4096]{2,0,1:T(8,128)(2,1)S(1)} %all_gather.32), kind=kOutput, calls=%fused_computation.7 | convolution fusion | flops 536870912 | bytes 17301504 | tf_op jit(solution)/shard_map/qsg,kvg->qkvs/dot_general | solution.py:14
  199.3 0.4 convolution_bitcast_fusion.1
  199.6 0.1 copy.41
  199.7 15.9 %all-reduce.1 = bf16[16,2,512]{2,1,0:T(2,128)(2,1)S(1)} all-reduce(f32[16,2,512]{2,1,0:T(2,128)S(1)} %copy.41), channel_id=4, replica_groups=mesh['kpt'=4,'pw'=8] {'kpt'}, use_global_device_ids=true, to_apply=%region_8.0.clone | all-reduce | flops 16384 | bytes 98304
  215.7 2.2 convolution_bitcast_fusion.4
  217.9 0.4 copy.58
  218.3 1.2 reshape.31
  219.5 0.0 reduce-scatter.14.cloned.1.call-start
  219.6 29.0 %reduce-scatter.12.cloned.1.call-done = f32[64,8]{1,0:T(8,128)} async-done(((f32[512,8]{1,0:T(8,128)}), f32[64,8]{1,0:T(8,128)}) %reduce-scatter.12.cloned.1.call-update) | async-done | bytes 2064
  248.5 0.9 reshape.32
  249.4 0.1 copy.42
  249.5 0.2 multiply_reduce_fusion.4
  249.7 37.8 %all-reduce.4 = (f32[2]{0:T(128)S(1)}, f32[2]{0:T(128)S(1)}, f32[2]{0:T(128)S(1)}) all-reduce(f32[2]{0:T(128)S(1)} %get-tuple-element.21, f32[2]{0:T(128)S(1)} %get-tuple-element.20, f32[2]{0:T(128)S(1)} %get-tuple-element.19), channel_id=1, replica_groups=mesh['kpt'=4,'pw'=8] {'kpt','pw'}, use_global_device_ids=true, to_apply=%region_15.0 | all-reduce | flops 6 | bytes 48 | tf_op jit(solution)/shard_map/psum | solution.py:58
  287.5 0.1 fusion.36
  287.6 0.1 copy.43
  287.7 14.9 %all_gather.33 = bf16[2,4,512]{1,0,2:T(2,128)(2,1)S(1)} all-gather(bf16[2,4,64]{1,0,2:T(2,128)(2,1)S(1)} %copy.43), channel_id=1, replica_groups=mesh['kpt'=4,'pw'=8] {'pw'}, dimensions={2}, use_global_device_ids=true | all-gather | bytes 9216 | tf_op jit(solution)/shard_map/all_gather | solution.py:37
  302.6 0.1 copy.44
  302.8 0.4 convolution_convert_fusion
  303.1 9.0 %all_gather.34 = bf16[16,2,512]{2,1,0:T(2,128)(2,1)S(1)} all-gather(bf16[4,2,512]{2,1,0:T(2,128)(2,1)S(1)} %convolution_convert_fusion), channel_id=1, replica_groups=mesh['kpt'=4,'pw'=8] {'kpt'}, dimensions={0}, use_global_device_ids=true | all-gather | bytes 40960 | tf_op jit(solution)/shard_map/all_gather | solution.py:13
  312.1 14.2 %all_gather.35 = bf16[16,2,4096]{2,0,1:T(8,128)(2,1)S(1)} all-gather(bf16[16,2,512]{2,0,1:T(8,128)(2,1)S(1)} %copy.45), channel_id=1, replica_groups=mesh['kpt'=4,'pw'=8] {'pw'}, dimensions={2}, use_global_device_ids=true | all-gather | bytes 294912 | tf_op jit(solution)/shard_map/all_gather | solution.py:17
  326.3 10.8 %fusion.12 = f32[4,16,2,512]{3,1,0,2:T(8,128)S(1)} fusion(bf16[4,512,4096]{2,1,0:T(8,128)(2,1)} %param.14, bf16[16,2,4096]{2,0,1:T(8,128)(2,1)S(1)} %all_gather.35), kind=kOutput, calls=%fused_computation.8 | convolution fusion | flops 536870912 | bytes 17301504 | tf_op jit(solution)/shard_map/qsg,kvg->qkvs/dot_general | solution.py:14
  337.1 0.4 convolution_bitcast_fusion
  337.4 0.1 copy.46
  337.5 16.1 %all-reduce.2 = bf16[16,2,512]{2,1,0:T(2,128)(2,1)S(1)} all-reduce(f32[16,2,512]{2,1,0:T(2,128)S(1)} %copy.46), channel_id=6, replica_groups=mesh['kpt'=4,'pw'=8] {'kpt'}, use_global_device_ids=true, to_apply=%region_16.0.clone | all-reduce | flops 16384 | bytes 98304
  353.6 2.2 convolution_bitcast_fusion.3
  355.9 0.4 copy.60
  356.3 1.2 reshape.33
  357.5 29.0 %reduce-scatter.14.cloned.1.call-done = f32[64,8]{1,0:T(8,128)} async-done(((f32[512,8]{1,0:T(8,128)}), f32[64,8]{1,0:T(8,128)}) %reduce-scatter.14.cloned.1.call-update) | async-done | bytes 2064
  386.5 0.9 reshape.34
  387.4 0.1 copy.47
  387.5 0.2 multiply_reduce_fusion.1
  387.7 37.9 %all-reduce.3 = (f32[2]{0:T(128)S(1)}, f32[2]{0:T(128)S(1)}, f32[2]{0:T(128)S(1)}) all-reduce(f32[2]{0:T(128)S(1)} %get-tuple-element.18, f32[2]{0:T(128)S(1)} %get-tuple-element.17, f32[2]{0:T(128)S(1)} %get-tuple-element.16), channel_id=1, replica_groups=mesh['kpt'=4,'pw'=8] {'kpt','pw'}, use_global_device_ids=true, to_apply=%region_23.0 | all-reduce | flops 6 | bytes 48 | tf_op jit(solution)/shard_map/psum | solution.py:58
  425.6 0.6 copy.48
  426.3 0.6 copy.49
  426.9 0.7 subtract_divide_fusion
  (28 shorter events, 0.2 us)
Async XLA Ops:
  7.2 17.1 %copy-start = (bf16[4,512,512]{2,1,0:T(8,128)(2,1)S(1)}, bf16[4,512,512]{2,1,0:T(8,128)(2,1)}, u32[]{:S(2)}) copy-start(bf16[4,512,512]{2,1,0:T(8,128)(2,1)} %param.13) | copy-start | bytes 6291460
  7.2 103.4 %reduce-scatter.10.cloned.1.call-start = ((), (), s32[]{:S(2)}) async-start(), calls=%async_computation.3 | async-start | bytes 294912
  47.2 10.8 %copy-start.1 = (s32[16,16]{1,0:T(8,128)S(1)}, s32[16,16]{1,0:T(8,128)}, u32[]{:S(2)}) copy-start(s32[16,16]{1,0:T(8,128)} %param.15) | copy-start | bytes 3076
  47.2 27.3 %copy-start.7 = (u32[32]{0:T(128)S(1)}, u32[32]{0:T(128)}, u32[]{:S(2)}) copy-start(u32[32]{0:T(128)} %constant.29) | copy-start | bytes 388
  75.7 35.8 %copy-start.2 = (f32[2,4,64]{2,1,0:T(4,128)S(1)}, f32[2,4,64]{2,1,0:T(4,128)}, u32[]{:S(2)}) copy-start(f32[2,4,64]{2,1,0:T(4,128)} %param.9) | copy-start | bytes 6148
  75.7 35.8 %copy-start.4 = (f32[4,64]{1,0:T(4,128)S(1)}, f32[4,64]{1,0:T(4,128)}, u32[]{:S(2)}) copy-start(f32[4,64]{1,0:T(4,128)} %param.8) | copy-start | bytes 3076
  75.7 35.8 %copy-start.5 = (f32[2,4,64]{2,1,0:T(4,128)S(1)}, f32[2,4,64]{2,1,0:T(4,128)}, u32[]{:S(2)}) copy-start(f32[2,4,64]{2,1,0:T(4,128)} %param.10) | copy-start | bytes 6148
  75.8 35.8 %copy-start.6 = (f32[2]{0:T(128)S(1)}, f32[2]{0:T(128)}, u32[]{:S(2)}) copy-start(f32[2]{0:T(128)} %param.11) | copy-start | bytes 28
  79.6 168.9 %reduce-scatter.12.cloned.1.call-start = ((), (), s32[]{:S(2)}) async-start(), calls=%async_computation.4 | async-start | bytes 294912
  219.5 167.0 %reduce-scatter.14.cloned.1.call-start = ((), (), s32[]{:S(2)}) async-start(), calls=%async_computation.5 | async-start | bytes 294912
  287.6 139.3 %copy-start.3 = (f32[2,4,64]{2,1,0:T(4,128)}, f32[2,4,64]{2,1,0:T(4,128)S(1)}, u32[]{:S(2)}) copy-start(f32[2,4,64]{2,1,0:T(4,128)S(1)} %get-tuple-element.36) | copy-start | bytes 6148
Sparse Core Ops, SparseCore 0:
  79.8 30.7 reduce-scatter.9
  219.6 28.8 reduce-scatter.11
  357.6 28.8 reduce-scatter.13
where the time goes:
time: 436 us; the launch traced here: 434 us
  blocking collectives  276 us (63%)
  waiting for transfers between devices  88.9 us (20%)
  matrix products  41.3 us (9%)
  between operations  14.7 us (3%)
  local copies, waits for them, and re-layouts  10.6 us (2%)
    psum x3, blocking collectives, on_device(): lax.psum((jnp.sum(vector_own * applied, axis=(1, 2)), jnp.sum(applied * a...  114 us
    unnamed x6, waiting for transfers between devices  88.9 us
    unnamed x3, blocking collectives  48.1 us
    all_gather x3, blocking collectives, on_device(): rounded = lax.all_gather(rounded, 'pw', axis=2, tiled=True)  45.6 us
    all_gather x3, blocking collectives, screened_images(): lax.all_gather(kpoint_rows, 'pw', axis=2, tiled=True)  42.9 us
    dot_general x3, matrix products, screened_images(): jnp.einsum('qsg,kvg->qkvs', screened, lax.all_gather(kpoint_rows, 'pw', a...  32.4 us
    all_gather x3, blocking collectives, screened_images(): kpoint_rows = lax.all_gather(density, 'kpt', axis=0, tiled=True)  26.1 us
    unnamed x28, local copies, waits for them, and re-layouts  9.32 us
  transfers between devices with their start and end apart: 3, of which 3 were waited for; matrix products, arithmetic and copies ran while one was open for 0% of the time, Pallas kernels for 0%

commit v1 on v0

v1 whole, which is shorter than its diff:
```python
import functools

import jax
import jax.numpy as jnp
from jax import lax
from jax.experimental import pallas as pl
from jax.experimental.pallas import tpu as pltpu
from jax.sharding import PartitionSpec as P

STEPS = 3
EPSILON = 1e-06
LANES = 128
BF, F32 = jnp.bfloat16, jnp.float32


def iota(shape, axis):
    return lax.broadcasted_iota(jnp.int32, shape, axis)


def high_low(x):
    high = x.astype(BF)
    return high, (x - high.astype(F32)).astype(BF)


def three_pieces(x):
    high = x.astype(BF).astype(F32)
    rest = x - high
    middle = rest.astype(BF).astype(F32)
    return high, middle, (rest - middle).astype(BF).astype(F32)


def chain_rows(x, chains):
    rows = x.shape[0] // chains
    parts = []
    for n in range(chains):
        part = jnp.sum(x[n * rows : (n + 1) * rows], axis=(0, 1), keepdims=True)
        parts.append(jnp.broadcast_to(part, (rows, 1)))
    return jnp.concatenate(parts, axis=0)


def begin_kernel(s, mi_ref, current_ref, previous_ref, energies_ref, pick_ref, out_ref):
    rows = s.rows
    bands = energies_ref.shape[1]
    mi = mi_ref[...].astype(F32).astype(BF)
    total, nk = s.groups * rows, mi.shape[0]

    def kpoint(r):
        return (r // rows) * s.kpoints + r % s.kpoints

    def chain(r):
        return (r % rows) // s.kpoints

    left = (kpoint(iota((total, nk), 0)) == iota((total, nk), 1)).astype(F32).astype(BF)
    right = (iota((nk, total), 0) == kpoint(iota((nk, total), 1))).astype(F32).astype(BF)
    spread = jnp.dot(left, mi, preferred_element_type=F32)
    spread = jnp.dot(spread.astype(BF), right, preferred_element_type=F32)
    same = chain(iota((total, total), 0)) == chain(iota((total, total), 1))
    for q in range(s.transfers):
        wanted = (lax.axis_index("kpt") * s.transfers + q).astype(F32)
        one = jnp.where(jnp.logical_and(spread == wanted, same), 1.0, 0.0).astype(BF)
        for piece in range(3):
            at = (q * 3 + piece) * total
            pick_ref[:, at : at + total] = one
    k = s.kpoints
    for b in range(s.parts):
        for n in range(s.chains):
            out_ref[b, n * k : (n + 1) * k, :] = current_ref[n]
            out_ref[b, rows + n * k : rows + (n + 1) * k, :] = previous_ref[n]
            out_ref[b, 2 * rows + n * k : 2 * rows + (n + 1) * k, :] = energies_ref[...]


def unpack_kernel(s, gathered_ref, right_ref, packet_ref, vector_ref, earlier_ref, levels_ref):
    rows = s.rows
    for at, ref in enumerate((vector_ref, earlier_ref, levels_ref)):
        ref[...] = jnp.concatenate(
            [gathered_ref[b, at * rows : (at + 1) * rows, :] for b in range(s.parts)], axis=1
        )
    density = project(s, vector_ref[...].astype(BF), right_ref)
    send(s, density, jnp.zeros((rows, LANES), F32), packet_ref)


def project(s, x, right_ref):
    rows, bands = x.shape
    total = None
    for k in range(s.kpoints):
        own = iota((rows, bands), 0) % s.kpoints == k
        masked = jnp.where(own, x.astype(F32), 0.0).astype(BF)
        part = jnp.dot(masked, right_ref[k], preferred_element_type=F32)
        total = part if total is None else total + part
    return total


def send(s, density, sums, packet_ref):
    width = density.shape[1]
    density = density.astype(BF)
    sums = sums.astype(BF)
    for d in range(s.groups * s.parts):
        packet_ref[d, :, :width] = density
        packet_ref[d, :, width:] = sums


def apply_step(s, partial_ref, vector, earlier, levels, beta):
    direct = partial_ref[0]
    for b in range(1, s.parts):
        direct = direct + partial_ref[b]
    applied = levels * vector - direct - beta * earlier
    square = chain_rows(vector * vector, s.chains)
    cross = chain_rows(vector * applied, s.chains)
    shift = jnp.where(square > 0.0, cross / jnp.where(square > 0.0, square, 1.0), 0.0)
    shift = shift.astype(BF).astype(F32)
    work = applied - shift * vector
    sums = (
        square,
        chain_rows(work * vector, s.chains),
        chain_rows(work * work, s.chains),
        shift,
    )
    lane = iota((s.rows, LANES), 1)
    value = jnp.zeros((s.rows, LANES), F32)
    for at, item in enumerate(sums):
        value = jnp.where(lane % 4 == at, item, value)
    high, middle, low = three_pieces(value)
    packed = jnp.where(lane < 4, high, jnp.where(lane < 8, middle, low))
    return work, packed


def read_sums(s, tiles):
    square, cross, work, shift = [], [], [], []
    for tile in tiles:
        value = tile[:, 0:4] + tile[:, 4:8] + tile[:, 8:12]
        for at, into in enumerate((square, cross, work, shift)):
            into.append(value[:, at : at + 1])
    alpha = sum(c + h * q for c, h, q in zip(cross, shift, square)) / s.entries
    offsets = [h - alpha for h in shift]
    mean = sum(
        w + 2.0 * o * c + o * (o * q) for w, o, c, q in zip(work, offsets, cross, square)
    )
    beta = jnp.sqrt(jnp.maximum(mean / s.entries, 0.0) + EPSILON)
    return alpha, beta, offsets


def later_kernel(
    s, partial_ref, work_ref, vector_ref, levels_ref, scalars_ref, right_ref,
    packet_ref, new_work_ref, new_vector_ref
):
    vector, beta = advance(work_ref, vector_ref, scalars_ref)
    new_vector_ref[...] = vector
    work, packed = apply_step(s, partial_ref, vector, vector_ref[...], levels_ref[...], beta)
    new_work_ref[...] = work
    finish_packet(s, work, packed, right_ref, packet_ref)


def first_kernel(
    s, partial_ref, vector_ref, earlier_ref, levels_ref, beta_ref, right_ref,
    packet_ref, new_work_ref
):
    beta = first_beta(s, beta_ref)
    work, packed = apply_step(
        s, partial_ref, vector_ref[...], earlier_ref[...], levels_ref[...], beta
    )
    new_work_ref[...] = work
    finish_packet(s, work, packed, right_ref, packet_ref)


def first_beta(s, beta_ref):
    row = iota((s.rows, 1), 0) // s.kpoints
    beta = jnp.zeros((s.rows, 1), F32)
    for n in range(s.chains):
        beta = jnp.where(row == n, beta_ref[n], beta)
    return beta


def advance(work_ref, vector_ref, scalars_ref):
    beta = scalars_ref[:, 1:2]
    offset = scalars_ref[:, 2:3]
    return (work_ref[...] + offset * vector_ref[...]) / beta, beta


def finish_packet(s, work, packed, right_ref, packet_ref):
    high, low = high_low(work)
    density = project(s, high, right_ref) + project(s, low, right_ref)
    send(s, density, packed, packet_ref)


def last_kernel(
    s, partial_ref, work_ref, vector_ref, levels_ref, scalars_ref,
    packet_ref, new_work_ref, new_vector_ref
):
    vector, beta = advance(work_ref, vector_ref, scalars_ref)
    new_vector_ref[...] = vector
    work, packed = apply_step(s, partial_ref, vector, vector_ref[...], levels_ref[...], beta)
    new_work_ref[...] = work
    for a in range(s.groups):
        packet_ref[a] = packed


def end_kernel(s, sums_ref, work_ref, vector_ref, *refs):
    scalar_refs, (last_ref, prior_ref, alphas_ref, betas_ref) = refs[:-4], refs[-4:]
    alpha, beta, offsets = read_sums(s, [sums_ref[a] for a in range(s.groups)])
    offset = own_offset(s, offsets)
    vector = vector_ref[...]
    last = (work_ref[...] + offset * vector) / beta
    width = last_ref.shape[2]
    me = lax.axis_index("pw")
    k = s.kpoints
    for value, ref in ((last, last_ref), (vector, prior_ref)):
        own = jnp.zeros((s.rows, width), F32)
        for b in range(s.parts):
            own = jnp.where(me == b, value[:, b * width : (b + 1) * width], own)
        for n in range(s.chains):
            ref[n] = own[n * k : (n + 1) * k]
    alphas = [ref[:, 0:1] for ref in scalar_refs] + [alpha]
    betas = [ref[:, 1:2] for ref in scalar_refs] + [beta]
    for n in range(s.chains):
        at = slice(n * k, n * k + 1)
        alphas_ref[n : n + 1, :] = jnp.concatenate([x[at] for x in alphas], axis=1)
        betas_ref[n : n + 1, :] = jnp.concatenate([x[at] for x in betas], axis=1)


def own_offset(s, offsets):
    me = lax.axis_index("kpt")
    own = jnp.zeros_like(offsets[0])
    for a in range(s.groups):
        own = jnp.where(me == a, offsets[a], own)
    return own


def screen_kernel(s, first, keep, *refs):
    refs = list(refs)
    packet_ref = refs.pop(0)
    before_ref = None if first else refs.pop(0)
    screened_ref, pick_ref, out_ref = refs[:3]
    refs = refs[3:]
    scalars_ref = None if first else refs.pop(0)
    density_ref = refs.pop(0) if keep else None
    (columns_ref,) = refs
    rows, total = s.rows, s.groups * s.rows
    width = packet_ref.shape[2] - LANES
    if not first:
        tiles = [packet_ref[a * s.parts, :, width:].astype(F32) for a in range(s.groups)]
        alpha, beta, offsets = read_sums(s, tiles)
        scale = 1.0 / beta
        lane = iota((rows, LANES), 1)
        scalars_ref[...] = jnp.where(
            lane == 0, alpha, jnp.where(lane == 1, beta, own_offset(s, offsets))
        )
    for a in range(s.groups):
        for b in range(s.parts):
            block = packet_ref[a * s.parts + b, :, :width]
            at = (slice(a * rows, (a + 1) * rows), slice(b * width, (b + 1) * width))
            if first:
                value = block.astype(F32)
            else:
                value = (block.astype(F32) + offsets[a] * before_ref[at]) * scale
            if keep:
                density_ref[at] = value
            high = value.astype(BF)
            columns_ref[at] = high.astype(F32)
            if not first:
                low = (slice(total + a * rows, total + (a + 1) * rows), at[1])
                columns_ref[low] = value - high.astype(F32)
    columns = columns_ref[...].astype(BF)
    pieces = []
    for q in range(s.transfers):
        image = lax.dot_general(
            screened_ref[q], columns, (((1,), (1,)), ((), ())), preferred_element_type=F32
        )
        image = image.T
        if not first:
            image = image[:total] + image[total:]
        pieces.extend(three_pieces(image))
    stacked = jnp.concatenate([piece.astype(BF) for piece in pieces], axis=0)
    field = jnp.dot(pick_ref[...], stacked, preferred_element_type=F32)
    for a in range(s.groups):
        out_ref[a] = field[a * rows : (a + 1) * rows]


def field_kernel(s, first, pieces_ref, left_ref, out_ref):
    field = pieces_ref[0]
    for a in range(1, s.groups):
        field = field + pieces_ref[a]
    parts = (field.astype(BF),) if first else high_low(field)
    stacked = jnp.concatenate([p.astype(F32) for p in parts], axis=0).astype(BF)
    rows = s.rows
    direct = None
    for k in range(s.kpoints):
        image = lax.dot_general(
            stacked, left_ref[k], (((1,), (1,)), ((), ())), preferred_element_type=F32
        )
        if not first:
            image = image[:rows] + image[rows:]
        own = iota(image.shape, 0) % s.kpoints == k
        direct = jnp.where(own, image, 0.0 if direct is None else direct)
    for b in range(s.parts):
        out_ref[b] = direct


class Sizes:
    pass


VMEM = pl.BlockSpec(memory_space=pltpu.VMEM)
SMEM = pl.BlockSpec(memory_space=pltpu.SMEM)


def call(body, args, outs, name, specs=None, scratch=(), limit=24):
    return pl.pallas_call(
        body,
        out_shape=[jax.ShapeDtypeStruct(shape, dtype) for shape, dtype in outs],
        in_specs=specs or [VMEM] * len(args),
        out_specs=[VMEM] * len(outs),
        scratch_shapes=list(scratch),
        compiler_params=pltpu.CompilerParams(vmem_limit_bytes=limit * 1024 * 1024),
        name=name,
    )(*args)


def on_device(
    groups, parts,
    energies, current, previous, previous_beta, pair_left, pair_right, screened, momentum_index
):
    s = Sizes()
    s.groups, s.parts = groups, parts
    s.chains, s.kpoints, band_block = current.shape
    s.rows = s.chains * s.kpoints
    s.transfers, width, waves = screened.shape
    bands = pair_left.shape[1]
    nk = momentum_index.shape[0]
    s.entries = float(nk * bands)
    total = groups * s.rows
    state = ((s.rows, bands), F32)
    packet = ((groups * parts, s.rows, width + LANES), BF)
    both = ("kpt", "pw")

    def exchange(x, axes):
        return lax.all_to_all(x, axes, 0, 0, tiled=True)

    screened = pltpu.with_memory_space_constraint(screened, pltpu.VMEM)
    pick, start = call(
        functools.partial(begin_kernel, s),
        (momentum_index, current, previous, energies),
        [((total, s.transfers * 3 * total), BF), ((parts, 3 * s.rows, band_block), F32)],
        "begin",
    )
    start = exchange(start, "pw")
    sent, vector, earlier, levels = call(
        functools.partial(unpack_kernel, s),
        (start, pair_right),
        [packet, state, state, state],
        "unpack",
    )
    scalars = []
    density = work = None
    for step in range(STEPS):
        first, keep = step == 0, step < STEPS - 1
        got = exchange(sent, both)
        args = (got,) + (() if first else (density,)) + (screened, pick)
        outs = [((groups, s.rows, width), F32)]
        outs += [] if first else [((s.rows, LANES), F32)]
        outs += [((total, waves), F32)] if keep else []
        results = call(
            functools.partial(screen_kernel, s, first, keep),
            args,
            outs,
            "screen",
            scratch=[pltpu.VMEM((total if first else 2 * total, waves), F32)],
        )
        field = results[0]
        if not first:
            scalars.append(results[1])
        if keep:
            density = results[-1]
        (direct,) = call(
            functools.partial(field_kernel, s, first),
            (exchange(field, "kpt"), pair_left),
            [((parts, s.rows, bands), F32)],
            "field",
        )
        direct = exchange(direct, "pw")
        if first:
            sent, work = call(
                functools.partial(first_kernel, s),
                (direct, vector, earlier, levels, previous_beta, pair_right),
                [packet, state],
                "apply",
                specs=[VMEM] * 4 + [SMEM, VMEM],
            )
        elif keep:
            sent, work, vector = call(
                functools.partial(later_kernel, s),
                (direct, work, vector, levels, scalars[-1], pair_right),
                [packet, state, state],
                "apply",
            )
        else:
            sent, work, vector = call(
                functools.partial(last_kernel, s),
                (direct, work, vector, levels, scalars[-1]),
                [((groups, s.rows, LANES), F32), state, state],
                "apply",
            )
    sums = exchange(sent, "kpt")
    own = (current.shape, F32)
    terms = ((s.chains, STEPS), F32)
    return tuple(
        call(
            functools.partial(end_kernel, s),
            (sums, work, vector, *scalars),
            [own, own, terms, terms],
            "end",
        )
    )


def solution(mesh):
    return jax.shard_map(
        functools.partial(on_device, mesh.shape["kpt"], mesh.shape["pw"]),
        mesh=mesh,
        in_specs=(
            P("kpt", "pw"),
            P(None, "kpt", "pw"),
            P(None, "kpt", "pw"),
            P(),
            P("kpt", None, "pw"),
            P("kpt", None, "pw"),
            P("kpt", "pw", None),
            P(),
        ),
        out_specs=(P(None, "kpt", "pw"), P(None, "kpt", "pw"), P(), P()),
        check_vma=False,
    )
```

time: 436 us -> 146 us (0.33)
  blocking collectives: 276 us -> 111 us
  waiting for transfers between devices: 88.9 us -> 0 us
  matrix products: 41.3 us -> 0 us
  Pallas kernels: 0 us -> 22.3 us
  between operations: 14.7 us -> 0.74 us
    all_gather x9 -> x0, blocking collectives: 115 us -> none  [the longest x3 45.6 us: on_device(): rounded = lax.all_gather(rounded, 'pw', axis=2, tiled=True)]
    psum x3 -> x0, blocking collectives: 114 us -> none  [on_device(): lax.psum((jnp.sum(vector_own * applied, axis=(1, 2)), jnp.sum(applied * a...]
    all_to_all x0 -> x11, blocking collectives: none -> 111 us  [exchange(): return lax.all_to_all(x, axes, 0, 0, tiled=True)]
    unnamed x6 -> x0, waiting for transfers between devices: 88.9 us -> none
    unnamed x3 -> x0, blocking collectives: 48.1 us -> none
    dot_general x12 -> x0, matrix products: 41.3 us -> none  [the longest x3 32.4 us: screened_images(): jnp.einsum('qsg,kvg->qkvs', screened, lax.all_gather(kpoint_rows, 'pw', a...]
    pallas_call x0 -> x12, Pallas kernels: none -> 22.3 us  [call(): pl.pallas_call(body, out_shape=[jax.ShapeDtypeStruct(shape, dtype) for sh...]
    unnamed x28 -> x22, local copies, waits for them, and re-layouts: 9.32 us -> 10.3 us
  transfers between devices with their start and end apart: 3 -> 0, of which waited for: 3 -> 0; matrix products, arithmetic and copies ran while one was open for 0% -> 0% of each run, Pallas kernels for 0% -> 0%
where the time goes in v1:
time: 146 us; the launch traced here: 145 us
  blocking collectives  111 us (76%)
  Pallas kernels  22.3 us (15%)
  local copies, waits for them, and re-layouts  10.8 us (7%)
    all_to_all x11, blocking collectives, exchange(): return lax.all_to_all(x, axes, 0, 0, tiled=True)  111 us
    pallas_call x12, Pallas kernels, call(): pl.pallas_call(body, out_shape=[jax.ShapeDtypeStruct(shape, dtype) for sh...  22.3 us
    unnamed x22, local copies, waits for them, and re-layouts  10.3 us

profile of v1, /device:TPU:0, one launch (start us, length us, event | category | flops | bytes accessed | tf_op | source)
XLA Modules:
  0.0 145.2 jit_solution(5277613068862723560)
XLA Ops:
  0.6 0.0 copy-start.5
  0.6 0.7 copy-done.5
  1.3 0.0 copy-start.6
  1.3 0.7 copy-done.6
  2.0 0.0 copy-start.7
  2.0 0.7 copy-done.7
  2.7 0.0 copy-start.8
  2.7 0.7 copy-done.8
  3.4 0.3 begin.1
  3.7 0.1 reshape.8
  3.8 12.0 %all_to_all.55 = f32[8,1,1536]{2,1,0:T(1,128)S(1)} all-to-all(f32[8,1,1536]{2,1,0:T(1,128)S(1)} %reshape.8), channel_id=1, replica_groups=mesh['kpt'=4,'pw'=8] {'pw'}, dimensions={0} | all-to-all | bytes 98304 | tf_op jit(solution)/shard_map/all_to_all | solution.py:336
  15.8 0.5 broadcast
  16.3 0.8 reduce
  17.1 0.1 reshape.9.gathered_ref
  17.2 0.0 copy-start.2
  17.2 1.6 %copy-done.2 = bf16[4,512,512]{2,1,0:T(8,128)(2,1)S(1)} copy-done((bf16[4,512,512]{2,1,0:T(8,128)(2,1)S(1)}, bf16[4,512,512]{2,1,0:T(8,128)(2,1)}, u32[]{:S(2)}) %copy-start.2) | copy-done | bytes 2097176
  18.8 0.0 copy-start.4
  18.8 0.4 unpack.1
  19.2 14.8 %all_to_all.56.refs_0_ = bf16[32,8,640]{2,1,0:T(8,128)(2,1)S(1)} all-to-all(bf16[32,8,640]{2,1,0:T(8,128)(2,1)S(1)} %get-tuple-element.26), channel_id=1, replica_groups=mesh['kpt'=4,'pw'=8] {'kpt','pw'}, dimensions={0} | all-to-all | bytes 655360 | tf_op jit(solution)/shard_map/all_to_all | solution.py:336
  34.0 0.0 copy-start
  34.0 5.8 %copy-done = bf16[4,512,4096]{2,1,0:T(8,128)(2,1)S(1)} copy-done((bf16[4,512,4096]{2,1,0:T(8,128)(2,1)S(1)}, bf16[4,512,4096]{2,1,0:T(8,128)(2,1)}, u32[]{:S(2)}) %copy-start) | copy-done | bytes 16777240
  39.8 0.0 copy-start.1
  39.8 4.7 %screen.3 = (f32[4,8,512]{2,1,0:T(8,128)S(1)}, f32[32,4096]{1,0:T(8,128)S(1)}) custom-call(bf16[32,8,640]{2,1,0:T(8,128)(2,1)S(1)} %all_to_all.56.refs_0_, bf16[4,512,4096]{2,1,0:T(8,128)(2,1)S(1)} %copy-done, bf16[32,384]{1,0:T(8,128)(2,1)S(1)} %get-tuple-element.27.refs_2_.refs_3_), custom_call_target="tpu_custom_call" | custom-call | tf_op jit(solution)/shard_map/screen/pallas_call | solution.py:307
  44.5 0.0 copy-start.3
  44.5 0.0 copy-start.9
  44.5 7.3 %all_to_all.57.pieces_ref = f32[4,8,512]{2,1,0:T(8,128)S(1)} all-to-all(f32[4,8,512]{2,1,0:T(8,128)S(1)} %get-tuple-element.28), channel_id=1, replica_groups=mesh['kpt'=4,'pw'=8] {'kpt'}, dimensions={0} | all-to-all | bytes 131072 | tf_op jit(solution)/shard_map/all_to_all | solution.py:336
  51.8 0.0 copy-done.4
  51.8 0.7 field.3
  52.5 9.1 %all_to_all.58.partial_ref = f32[8,8,512]{2,1,0:T(8,128)S(1)} all-to-all(f32[8,8,512]{2,1,0:T(8,128)S(1)} %field.3), channel_id=1, replica_groups=mesh['kpt'=4,'pw'=8] {'pw'}, dimensions={0} | all-to-all | bytes 262144 | tf_op jit(solution)/shard_map/all_to_all | solution.py:336
  61.6 0.0 copy-done.3
  61.6 0.0 copy-done.9
  61.6 1.4 apply.3
  63.1 13.8 %all_to_all.59.refs_0_ = bf16[32,8,640]{2,1,0:T(8,128)(2,1)S(1)} all-to-all(bf16[32,8,640]{2,1,0:T(8,128)(2,1)S(1)} %get-tuple-element.32), channel_id=1, replica_groups=mesh['kpt'=4,'pw'=8] {'kpt','pw'}, dimensions={0} | all-to-all | bytes 655360 | tf_op jit(solution)/shard_map/all_to_all | solution.py:336
  76.9 0.0 copy-done.1
  76.9 5.2 %screen.4 = (f32[4,8,512]{2,1,0:T(8,128)S(1)}, f32[8,128]{1,0:T(8,128)S(1)}, f32[32,4096]{1,0:T(8,128)S(1)}) custom-call(bf16[32,8,640]{2,1,0:T(8,128)(2,1)S(1)} %all_to_all.59.refs_0_, f32[32,4096]{1,0:T(8,128)S(1)} %get-tuple-element.33.refs_1_, bf16[4,512,4096]{2,1,0:T(8,128)(2,1)S(1)} %copy-done.1, bf16[32,384]{1,0:T(8,128)(2,1)S(1)} %get-tuple-element.27.refs_2_.refs_3_), custom_call_target="tpu_custom_call" | custom-call | tf_op jit(solution)/shard_map/screen/pallas_call | solution.py:307
  82.0 7.2 %all_to_all.60.pieces_ref = f32[4,8,512]{2,1,0:T(8,128)S(1)} all-to-all(f32[4,8,512]{2,1,0:T(8,128)S(1)} %get-tuple-element.34), channel_id=1, replica_groups=mesh['kpt'=4,'pw'=8] {'kpt'}, dimensions={0} | all-to-all | bytes 131072 | tf_op jit(solution)/shard_map/all_to_all | solution.py:336
  89.3 0.7 field.4
  89.9 9.1 %all_to_all.61.partial_ref = f32[8,8,512]{2,1,0:T(8,128)S(1)} all-to-all(f32[8,8,512]{2,1,0:T(8,128)S(1)} %field.4), channel_id=1, replica_groups=mesh['kpt'=4,'pw'=8] {'pw'}, dimensions={0} | all-to-all | bytes 262144 | tf_op jit(solution)/shard_map/all_to_all | solution.py:336
  99.1 0.9 apply.4
  100.0 13.8 %all_to_all.62.refs_0_ = bf16[32,8,640]{2,1,0:T(8,128)(2,1)S(1)} all-to-all(bf16[32,8,640]{2,1,0:T(8,128)(2,1)S(1)} %get-tuple-element.37), channel_id=1, replica_groups=mesh['kpt'=4,'pw'=8] {'kpt','pw'}, dimensions={0} | all-to-all | bytes 655360 | tf_op jit(solution)/shard_map/all_to_all | solution.py:336
  113.8 5.2 %screen.5 = (f32[4,8,512]{2,1,0:T(8,128)S(1)}, f32[8,128]{1,0:T(8,128)S(1)}) custom-call(bf16[32,8,640]{2,1,0:T(8,128)(2,1)S(1)} %all_to_all.62.refs_0_, f32[32,4096]{1,0:T(8,128)S(1)} %get-tuple-element.38.refs_1_, bf16[4,512,4096]{2,1,0:T(8,128)(2,1)S(1)} %copy-done.1, bf16[32,384]{1,0:T(8,128)(2,1)S(1)} %get-tuple-element.27.refs_2_.refs_3_), custom_call_target="tpu_custom_call" | custom-call | tf_op jit(solution)/shard_map/screen/pallas_call | solution.py:307
  119.0 7.2 %all_to_all.63.pieces_ref = f32[4,8,512]{2,1,0:T(8,128)S(1)} all-to-all(f32[4,8,512]{2,1,0:T(8,128)S(1)} %get-tuple-element.39), channel_id=1, replica_groups=mesh['kpt'=4,'pw'=8] {'kpt'}, dimensions={0} | all-to-all | bytes 131072 | tf_op jit(solution)/shard_map/all_to_all | solution.py:336
  126.2 0.7 field.5
  126.9 9.1 %all_to_all.64.partial_ref = f32[8,8,512]{2,1,0:T(8,128)S(1)} all-to-all(f32[8,8,512]{2,1,0:T(8,128)S(1)} %field.5), channel_id=1, replica_groups=mesh['kpt'=4,'pw'=8] {'pw'}, dimensions={0} | all-to-all | bytes 262144 | tf_op jit(solution)/shard_map/all_to_all | solution.py:336
  136.0 0.5 apply.5
  136.5 7.1 %all_to_all.65.sums_ref = f32[4,8,128]{2,1,0:T(8,128)S(1)} all-to-all(f32[4,8,128]{2,1,0:T(8,128)S(1)} %get-tuple-element.43), channel_id=1, replica_groups=mesh['kpt'=4,'pw'=8] {'kpt'}, dimensions={0} | all-to-all | bytes 32768 | tf_op jit(solution)/shard_map/all_to_all | solution.py:336
  143.6 1.6 %end.1 = (f32[2,4,64]{2,1,0:T(4,128)}, f32[2,4,64]{2,1,0:T(4,128)}, f32[2,3]{1,0:T(2,128)}, f32[2,3]{1,0:T(2,128)}) custom-call(f32[4,8,128]{2,1,0:T(8,128)S(1)} %all_to_all.65.sums_ref, f32[8,512]{1,0:T(8,128)S(1)} %get-tuple-element.44.work_ref, f32[8,512]{1,0:T(8,128)S(1)} %get-tuple-element.45.vector_ref, ...), custom_call_target="tpu_custom_call" | custom-call | tf_op jit(solution)/shard_map/end/pallas_call | solution.py:307
Async XLA Ops:
  0.6 0.7 copy-start.5
  1.3 0.7 copy-start.6
  2.0 0.7 copy-start.7
  2.7 0.7 copy-start.8
  17.2 1.6 %copy-start.2 = (bf16[4,512,512]{2,1,0:T(8,128)(2,1)S(1)}, bf16[4,512,512]{2,1,0:T(8,128)(2,1)}, u32[]{:S(2)}) copy-start(bf16[4,512,512]{2,1,0:T(8,128)(2,1)} %right_ref.5) | copy-start | bytes 6291460
  18.8 33.0 %copy-start.4 = (bf16[4,512,512]{2,1,0:T(8,128)(2,1)S(1)}, bf16[4,512,512]{2,1,0:T(8,128)(2,1)}, u32[]{:S(2)}) copy-start(bf16[4,512,512]{2,1,0:T(8,128)(2,1)} %left_ref.5) | copy-start | bytes 6291460
  34.0 5.8 %copy-start = (bf16[4,512,4096]{2,1,0:T(8,128)(2,1)S(1)}, bf16[4,512,4096]{2,1,0:T(8,128)(2,1)}, u32[]{:S(2)}) copy-start(bf16[4,512,4096]{2,1,0:T(8,128)(2,1)} %refs_2_.3) | copy-start | bytes 50331652
  39.8 37.1 %copy-start.1 = (bf16[4,512,4096]{2,1,0:T(8,128)(2,1)S(1)}, bf16[4,512,4096]{2,1,0:T(8,128)(2,1)}, u32[]{:S(2)}) copy-start(bf16[4,512,4096]{2,1,0:T(8,128)(2,1)} %refs_2_.3) | copy-start | bytes 50331652
  44.5 17.2 %copy-start.3 = (bf16[4,512,512]{2,1,0:T(8,128)(2,1)S(1)}, bf16[4,512,512]{2,1,0:T(8,128)(2,1)}, u32[]{:S(2)}) copy-start(bf16[4,512,512]{2,1,0:T(8,128)(2,1)} %right_ref.5) | copy-start | bytes 6291460
  44.5 17.2 %copy-start.9 = (f32[2]{0:T(128)S(1)}, f32[2]{0:T(128)}, u32[]{:S(2)}) copy-start(f32[2]{0:T(128)} %beta_ref.1) | copy-start | bytes 28

commit v2 on v1

--- a/solution.py
+++ b/solution.py
@@ -9,6 +9,7 @@
 
 STEPS = 3
 EPSILON = 1e-06
+COVER = 5_000_000_000
 LANES = 128
 BF, F32 = jnp.bfloat16, jnp.float32
 
@@ -38,9 +39,28 @@
     return jnp.concatenate(parts, axis=0)
 
 
-def begin_kernel(s, mi_ref, current_ref, previous_ref, energies_ref, pick_ref, out_ref):
+def begin_kernel(s, *refs):
+    sources, held, sems = refs[:4], refs[6:10], refs[10]
+    pick_ref, out_ref = refs[4:6]
+    started = [
+        pltpu.make_async_copy(source, target, sems.at[at])
+        for at, (source, target) in enumerate(zip(sources, held))
+    ]
+    for copy in started:
+        copy.start()
+    for copy in started:
+        copy.wait()
+    mi_ref, current_ref, previous_ref, energies_ref = held
     rows = s.rows
-    bands = energies_ref.shape[1]
+    both = []
+    for ref in (current_ref, previous_ref):
+        both.append(jnp.concatenate([ref[n] for n in range(s.chains)], axis=0))
+    levels = jnp.concatenate([energies_ref[...]] * s.chains, axis=0)
+    piece = jnp.concatenate(
+        [jnp.concatenate(both, axis=1), jnp.concatenate([levels] * 2, axis=1)], axis=0
+    )
+    for b in range(s.parts):
+        out_ref[b] = piece
     mi = mi_ref[...].astype(F32).astype(BF)
     total, nk = s.groups * rows, mi.shape[0]
 
@@ -61,19 +81,18 @@
         for piece in range(3):
             at = (q * 3 + piece) * total
             pick_ref[:, at : at + total] = one
-    k = s.kpoints
-    for b in range(s.parts):
-        for n in range(s.chains):
-            out_ref[b, n * k : (n + 1) * k, :] = current_ref[n]
-            out_ref[b, rows + n * k : rows + (n + 1) * k, :] = previous_ref[n]
-            out_ref[b, 2 * rows + n * k : 2 * rows + (n + 1) * k, :] = energies_ref[...]
 
 
 def unpack_kernel(s, gathered_ref, right_ref, packet_ref, vector_ref, earlier_ref, levels_ref):
     rows = s.rows
-    for at, ref in enumerate((vector_ref, earlier_ref, levels_ref)):
+    width = gathered_ref.shape[2] // 2
+    for ref, row, lane in ((vector_ref, 0, 0), (earlier_ref, 0, width), (levels_ref, rows, 0)):
         ref[...] = jnp.concatenate(
-            [gathered_ref[b, at * rows : (at + 1) * rows, :] for b in range(s.parts)], axis=1
+            [
+                gathered_ref[b, row : row + rows, lane : lane + width]
+                for b in range(s.parts)
+            ],
+            axis=1,
         )
     density = project(s, vector_ref[...].astype(BF), right_ref)
     send(s, density, jnp.zeros((rows, LANES), F32), packet_ref)
@@ -100,9 +119,9 @@
 
 
 def apply_step(s, partial_ref, vector, earlier, levels, beta):
-    direct = partial_ref[0]
+    direct = partial_ref[0].astype(F32)
     for b in range(1, s.parts):
-        direct = direct + partial_ref[b]
+        direct = direct + partial_ref[b].astype(F32)
     applied = levels * vector - direct - beta * earlier
     square = chain_rows(vector * vector, s.chains)
     cross = chain_rows(vector * applied, s.chains)
@@ -292,7 +311,7 @@
         own = iota(image.shape, 0) % s.kpoints == k
         direct = jnp.where(own, image, 0.0 if direct is None else direct)
     for b in range(s.parts):
-        out_ref[b] = direct
+        out_ref[b] = direct.astype(BF)
 
 
 class Sizes:
@@ -300,10 +319,11 @@
 
 
 VMEM = pl.BlockSpec(memory_space=pltpu.VMEM)
+HBM = pl.BlockSpec(memory_space=pltpu.HBM)
 SMEM = pl.BlockSpec(memory_space=pltpu.SMEM)
 
 
-def call(body, args, outs, name, specs=None, scratch=(), limit=24):
+def call(body, args, outs, name, specs=None, scratch=(), limit=24, cost=0):
     return pl.pallas_call(
         body,
         out_shape=[jax.ShapeDtypeStruct(shape, dtype) for shape, dtype in outs],
@@ -312,6 +332,9 @@
         scratch_shapes=list(scratch),
         compiler_params=pltpu.CompilerParams(vmem_limit_bytes=limit * 1024 * 1024),
         name=name,
+        cost_estimate=pl.CostEstimate(
+            flops=cost, bytes_accessed=cost // 256, transcendentals=0
+        ),
     )(*args)
 
 
@@ -336,11 +359,22 @@
         return lax.all_to_all(x, axes, 0, 0, tiled=True)
 
     screened = pltpu.with_memory_space_constraint(screened, pltpu.VMEM)
+    inputs = tuple(
+        pltpu.with_memory_space_constraint(x, pltpu.HBM)
+        for x in (momentum_index, current, previous, energies)
+    )
     pick, start = call(
         functools.partial(begin_kernel, s),
-        (momentum_index, current, previous, energies),
-        [((total, s.transfers * 3 * total), BF), ((parts, 3 * s.rows, band_block), F32)],
+        inputs,
+        [
+            ((total, s.transfers * 3 * total), BF),
+            ((parts, 2 * s.rows, 2 * band_block), F32),
+        ],
         "begin",
+        specs=[HBM] * len(inputs),
+        scratch=[pltpu.VMEM(x.shape, x.dtype) for x in inputs]
+        + [pltpu.SemaphoreType.DMA((len(inputs),))],
+        cost=COVER,
     )
     start = exchange(start, "pw")
     sent, vector, earlier, levels = call(
@@ -348,6 +382,7 @@
         (start, pair_right),
         [packet, state, state, state],
         "unpack",
+        cost=COVER,
     )
     scalars = []
     density = work = None
@@ -373,7 +408,7 @@
         (direct,) = call(
             functools.partial(field_kernel, s, first),
             (exchange(field, "kpt"), pair_left),
-            [((parts, s.rows, bands), F32)],
+            [((parts, s.rows, bands), BF)],
             "field",
         )
         direct = exchange(direct, "pw")

time: 146 us -> 133 us (0.911)
  local copies, waits for them, and re-layouts: 10.8 us -> 0.03 us
  blocking collectives: 111 us -> 108 us
    unnamed x22 -> x14, local copies, waits for them, and re-layouts: 10.3 us -> 0.03 us
    all_to_all x11, blocking collectives: 111 us -> 108 us  [exchange(): return lax.all_to_all(x, axes, 0, 0, tiled=True)]
where the time goes in v2:
time: 133 us; the launch traced here: 132 us
  blocking collectives  108 us (81%)
  Pallas kernels  23.1 us (17%)
    all_to_all x11, blocking collectives, exchange(): return lax.all_to_all(x, axes, 0, 0, tiled=True)  108 us
    pallas_call x12, Pallas kernels, call(): pl.pallas_call(body, out_shape=[jax.ShapeDtypeStruct(shape, dtype) for sh...  23.1 us

profile of v2, /device:TPU:0, one launch (start us, length us, event | category | flops | bytes accessed | tf_op | source)
XLA Modules:
  0.0 132.4 jit_solution(15792473006834882926)
XLA Ops:
  0.6 0.0 copy-start.1
  0.6 0.0 slice-start
  0.7 0.0 slice-start.1
  0.7 1.3 begin.1
  1.9 12.3 %all_to_all.55.gathered_ref = f32[8,16,128]{2,1,0:T(8,128)S(1)} all-to-all(f32[8,16,128]{2,1,0:T(8,128)S(1)} %get-tuple-element.25), channel_id=1, replica_groups=mesh['kpt'=4,'pw'=8] {'pw'}, dimensions={0} | all-to-all | bytes 131072 | tf_op jit(solution)/shard_map/all_to_all | solution.py:359
  14.3 0.0 copy-done.1
  14.3 0.0 slice-start.2
  14.3 0.0 slice-start.3
  14.3 0.4 unpack.1
  14.7 14.9 %all_to_all.56.refs_0_ = bf16[32,8,640]{2,1,0:T(8,128)(2,1)S(1)} all-to-all(bf16[32,8,640]{2,1,0:T(8,128)(2,1)S(1)} %get-tuple-element.26), channel_id=1, replica_groups=mesh['kpt'=4,'pw'=8] {'kpt','pw'}, dimensions={0} | all-to-all | bytes 655360 | tf_op jit(solution)/shard_map/all_to_all | solution.py:359
  29.7 0.0 slice-done
  29.7 0.0 slice-done.1
  29.7 0.0 slice-done.2
  29.7 0.0 slice-done.3
  29.7 0.0 copy-start
  29.7 4.7 %screen.3 = (f32[4,8,512]{2,1,0:T(8,128)S(1)}, f32[32,4096]{1,0:T(8,128)S(1)}) custom-call(bf16[32,8,640]{2,1,0:T(8,128)(2,1)S(1)} %all_to_all.56.refs_0_, bf16[4,512,4096]{2,1,0:T(8,128)(2,1)S(1)} %bitcast.1, bf16[32,384]{1,0:T(8,128)(2,1)S(1)} %get-tuple-element.27.refs_2_.refs_3_), custom_call_target="tpu_custom_call" | custom-call | tf_op jit(solution)/shard_map/screen/pallas_call | solution.py:327
  34.4 0.0 copy-start.2
  34.4 7.3 %all_to_all.57.pieces_ref = f32[4,8,512]{2,1,0:T(8,128)S(1)} all-to-all(f32[4,8,512]{2,1,0:T(8,128)S(1)} %get-tuple-element.28), channel_id=1, replica_groups=mesh['kpt'=4,'pw'=8] {'kpt'}, dimensions={0} | all-to-all | bytes 131072 | tf_op jit(solution)/shard_map/all_to_all | solution.py:359
  41.8 0.0 copy-done
  41.8 0.7 field.3
  42.4 8.3 %all_to_all.58.partial_ref = bf16[8,8,512]{2,1,0:T(8,128)(2,1)S(1)} all-to-all(bf16[8,8,512]{2,1,0:T(8,128)(2,1)S(1)} %field.3), channel_id=1, replica_groups=mesh['kpt'=4,'pw'=8] {'pw'}, dimensions={0} | all-to-all | bytes 131072 | tf_op jit(solution)/shard_map/all_to_all | solution.py:359
  50.7 0.0 copy-done.2
  50.7 1.4 %apply.3 = (bf16[32,8,640]{2,1,0:T(8,128)(2,1)S(1)}, f32[8,512]{1,0:T(8,128)S(1)}) custom-call(bf16[8,8,512]{2,1,0:T(8,128)(2,1)S(1)} %all_to_all.58.partial_ref, f32[8,512]{1,0:T(8,128)S(1)} %get-tuple-element.29.vector_ref, f32[8,512]{1,0:T(8,128)S(1)} %get-tuple-element.30.earlier_ref, f32[8,512]{1,0:T(8,128)S(1)} %get-tuple-element.31.levels_ref, ...), custom_call_target="tpu_custom_call" | custom-call | tf_op jit(solution)/shard_map/apply/pallas_call | solution.py:327
  52.1 13.7 %all_to_all.59.refs_0_ = bf16[32,8,640]{2,1,0:T(8,128)(2,1)S(1)} all-to-all(bf16[32,8,640]{2,1,0:T(8,128)(2,1)S(1)} %get-tuple-element.32), channel_id=1, replica_groups=mesh['kpt'=4,'pw'=8] {'kpt','pw'}, dimensions={0} | all-to-all | bytes 655360 | tf_op jit(solution)/shard_map/all_to_all | solution.py:359
  65.9 5.2 %screen.4 = (f32[4,8,512]{2,1,0:T(8,128)S(1)}, f32[8,128]{1,0:T(8,128)S(1)}, f32[32,4096]{1,0:T(8,128)S(1)}) custom-call(bf16[32,8,640]{2,1,0:T(8,128)(2,1)S(1)} %all_to_all.59.refs_0_, f32[32,4096]{1,0:T(8,128)S(1)} %get-tuple-element.33.refs_1_, bf16[4,512,4096]{2,1,0:T(8,128)(2,1)S(1)} %bitcast.1, bf16[32,384]{1,0:T(8,128)(2,1)S(1)} %get-tuple-element.27.refs_2_.refs_3_), custom_call_target="tpu_custom_call" | custom-call | tf_op jit(solution)/shard_map/screen/pallas_call | solution.py:327
  71.0 7.2 %all_to_all.60.pieces_ref = f32[4,8,512]{2,1,0:T(8,128)S(1)} all-to-all(f32[4,8,512]{2,1,0:T(8,128)S(1)} %get-tuple-element.34), channel_id=1, replica_groups=mesh['kpt'=4,'pw'=8] {'kpt'}, dimensions={0} | all-to-all | bytes 131072 | tf_op jit(solution)/shard_map/all_to_all | solution.py:359
  78.3 0.7 field.4
  78.9 8.3 %all_to_all.61.partial_ref = bf16[8,8,512]{2,1,0:T(8,128)(2,1)S(1)} all-to-all(bf16[8,8,512]{2,1,0:T(8,128)(2,1)S(1)} %field.4), channel_id=1, replica_groups=mesh['kpt'=4,'pw'=8] {'pw'}, dimensions={0} | all-to-all | bytes 131072 | tf_op jit(solution)/shard_map/all_to_all | solution.py:359
  87.2 0.9 apply.4
  88.2 13.7 %all_to_all.62.refs_0_ = bf16[32,8,640]{2,1,0:T(8,128)(2,1)S(1)} all-to-all(bf16[32,8,640]{2,1,0:T(8,128)(2,1)S(1)} %get-tuple-element.37), channel_id=1, replica_groups=mesh['kpt'=4,'pw'=8] {'kpt','pw'}, dimensions={0} | all-to-all | bytes 655360 | tf_op jit(solution)/shard_map/all_to_all | solution.py:359
  101.9 5.2 %screen.5 = (f32[4,8,512]{2,1,0:T(8,128)S(1)}, f32[8,128]{1,0:T(8,128)S(1)}) custom-call(bf16[32,8,640]{2,1,0:T(8,128)(2,1)S(1)} %all_to_all.62.refs_0_, f32[32,4096]{1,0:T(8,128)S(1)} %get-tuple-element.38.refs_1_, bf16[4,512,4096]{2,1,0:T(8,128)(2,1)S(1)} %bitcast.1, bf16[32,384]{1,0:T(8,128)(2,1)S(1)} %get-tuple-element.27.refs_2_.refs_3_), custom_call_target="tpu_custom_call" | custom-call | tf_op jit(solution)/shard_map/screen/pallas_call | solution.py:327
  107.1 7.2 %all_to_all.63.pieces_ref = f32[4,8,512]{2,1,0:T(8,128)S(1)} all-to-all(f32[4,8,512]{2,1,0:T(8,128)S(1)} %get-tuple-element.39), channel_id=1, replica_groups=mesh['kpt'=4,'pw'=8] {'kpt'}, dimensions={0} | all-to-all | bytes 131072 | tf_op jit(solution)/shard_map/all_to_all | solution.py:359
  114.3 0.7 field.5
  114.9 8.3 %all_to_all.64.partial_ref = bf16[8,8,512]{2,1,0:T(8,128)(2,1)S(1)} all-to-all(bf16[8,8,512]{2,1,0:T(8,128)(2,1)S(1)} %field.5), channel_id=1, replica_groups=mesh['kpt'=4,'pw'=8] {'pw'}, dimensions={0} | all-to-all | bytes 131072 | tf_op jit(solution)/shard_map/all_to_all | solution.py:359
  123.2 0.5 apply.5
  123.7 7.1 %all_to_all.65.sums_ref = f32[4,8,128]{2,1,0:T(8,128)S(1)} all-to-all(f32[4,8,128]{2,1,0:T(8,128)S(1)} %get-tuple-element.43), channel_id=1, replica_groups=mesh['kpt'=4,'pw'=8] {'kpt'}, dimensions={0} | all-to-all | bytes 32768 | tf_op jit(solution)/shard_map/all_to_all | solution.py:359
  130.8 1.6 %end.1 = (f32[2,4,64]{2,1,0:T(4,128)}, f32[2,4,64]{2,1,0:T(4,128)}, f32[2,3]{1,0:T(2,128)}, f32[2,3]{1,0:T(2,128)}) custom-call(f32[4,8,128]{2,1,0:T(8,128)S(1)} %all_to_all.65.sums_ref, f32[8,512]{1,0:T(8,128)S(1)} %get-tuple-element.44.work_ref, f32[8,512]{1,0:T(8,128)S(1)} %get-tuple-element.45.vector_ref, ...), custom_call_target="tpu_custom_call" | custom-call | tf_op jit(solution)/shard_map/end/pallas_call | solution.py:327
  (1 shorter events, 0.0 us)
Async XLA Ops:
  0.6 13.6 %copy-start.1 = (bf16[4,512,512]{2,1,0:T(8,128)(2,1)S(1)}, bf16[4,512,512]{2,1,0:T(8,128)(2,1)}, u32[]{:S(2)}) copy-start(bf16[4,512,512]{2,1,0:T(8,128)(2,1)} %right_ref.5) | copy-start | bytes 6291460
  0.6 29.0 %slice-start = ((s8[16777216]{0:T(1024)(128)(4,1)}), s8[4194304]{0:T(1024)(128)(4,1)S(1)}, s32[]{:S(2)}) async-start(s8[16777216]{0:T(1024)(128)(4,1)} %bitcast), calls=%async_computation.11 | async-start | bytes 8388608
  0.7 29.0 %slice-start.1 = ((s8[16777216]{0:T(1024)(128)(4,1)}), s8[4194304]{0:T(1024)(128)(4,1)S(1)}, s32[]{:S(2)}) async-start(s8[16777216]{0:T(1024)(128)(4,1)} %bitcast), calls=%async_computation.12 | async-start | bytes 8388608
  14.3 15.4 %slice-start.2 = ((s8[16777216]{0:T(1024)(128)(4,1)}), s8[4194304]{0:T(1024)(128)(4,1)S(1)}, s32[]{:S(2)}) async-start(s8[16777216]{0:T(1024)(128)(4,1)} %bitcast), calls=%async_computation.13 | async-start | bytes 8388608
  14.3 15.4 %slice-start.3 = ((s8[16777216]{0:T(1024)(128)(4,1)}), s8[4194304]{0:T(1024)(128)(4,1)S(1)}, s32[]{:S(2)}) async-start(s8[16777216]{0:T(1024)(128)(4,1)} %bitcast), calls=%async_computation.14 | async-start | bytes 8388608
  29.7 12.1 %copy-start = (bf16[4,512,512]{2,1,0:T(8,128)(2,1)S(1)}, bf16[4,512,512]{2,1,0:T(8,128)(2,1)}, u32[]{:S(2)}) copy-start(bf16[4,512,512]{2,1,0:T(8,128)(2,1)} %left_ref.5) | copy-start | bytes 6291460
  34.4 16.3 %copy-start.2 = (f32[2]{0:T(128)S(1)}, f32[2]{0:T(128)}, u32[]{:S(2)}) copy-start(f32[2]{0:T(128)} %beta_ref.1) | copy-start | bytes 28

commit v3 on v2

--- a/solution.py
+++ b/solution.py
@@ -11,6 +11,7 @@
 EPSILON = 1e-06
 COVER = 5_000_000_000
 LANES = 128
+CORES = 2
 BF, F32 = jnp.bfloat16, jnp.float32
 
 
@@ -113,7 +114,7 @@
     width = density.shape[1]
     density = density.astype(BF)
     sums = sums.astype(BF)
-    for d in range(s.groups * s.parts):
+    for d in range(packet_ref.shape[0]):
         packet_ref[d, :, :width] = density
         packet_ref[d, :, width:] = sums
 
@@ -209,18 +210,26 @@
     new_vector_ref[...] = vector
     work, packed = apply_step(s, partial_ref, vector, vector_ref[...], levels_ref[...], beta)
     new_work_ref[...] = work
+    packet_ref[...] = packed
+
+
+def end_kernel(s, *refs):
+    sums, refs = [ref[...] for ref in refs[: s.groups]], refs[s.groups :]
+    work_ref, vector_ref = refs[:2]
+    scalar_refs, (last_ref, prior_ref, alphas_ref, betas_ref) = refs[2:-4], refs[-4:]
+    mine = lax.axis_index("kpt")
+    tiles = []
     for a in range(s.groups):
-        packet_ref[a] = packed
-
-
-def end_kernel(s, sums_ref, work_ref, vector_ref, *refs):
-    scalar_refs, (last_ref, prior_ref, alphas_ref, betas_ref) = refs[:-4], refs[-4:]
-    alpha, beta, offsets = read_sums(s, [sums_ref[a] for a in range(s.groups)])
+        tile = sums[0]
+        for other in range(1, s.groups):
+            tile = jnp.where((mine ^ a) == other, sums[other], tile)
+        tiles.append(tile)
+    alpha, beta, offsets = read_sums(s, tiles)
     offset = own_offset(s, offsets)
     vector = vector_ref[...]
     last = (work_ref[...] + offset * vector) / beta
     width = last_ref.shape[2]
-    me = lax.axis_index("pw")
+    me = lax.axis_index("z") * CORES + lax.axis_index("core")
     k = s.kpoints
     for value, ref in ((last, last_ref), (vector, prior_ref)):
         own = jnp.zeros((s.rows, width), F32)
@@ -246,17 +255,24 @@
 
 def screen_kernel(s, first, keep, *refs):
     refs = list(refs)
-    packet_ref = refs.pop(0)
+    packet_refs = refs[:CORES]
+    del refs[:CORES]
     before_ref = None if first else refs.pop(0)
-    screened_ref, pick_ref, out_ref = refs[:3]
-    refs = refs[3:]
+    screened_ref, pick_ref = refs[:2]
+    out_refs = refs[2 : 2 + s.groups]
+    del refs[: 2 + s.groups]
     scalars_ref = None if first else refs.pop(0)
     density_ref = refs.pop(0) if keep else None
-    (columns_ref,) = refs
+    columns_ref, field_ref = refs
     rows, total = s.rows, s.groups * s.rows
-    width = packet_ref.shape[2] - LANES
+    chips = s.parts // CORES
+    width = packet_refs[0].shape[2] - LANES
+    core = lax.axis_index("core")
     if not first:
-        tiles = [packet_ref[a * s.parts, :, width:].astype(F32) for a in range(s.groups)]
+        tiles = [
+            jnp.where(core == 0, *(ref[a * chips, :, width:].astype(F32) for ref in packet_refs))
+            for a in range(s.groups)
+        ]
         alpha, beta, offsets = read_sums(s, tiles)
         scale = 1.0 / beta
         lane = iota((rows, LANES), 1)
@@ -264,20 +280,22 @@
             lane == 0, alpha, jnp.where(lane == 1, beta, own_offset(s, offsets))
         )
     for a in range(s.groups):
-        for b in range(s.parts):
-            block = packet_ref[a * s.parts + b, :, :width]
-            at = (slice(a * rows, (a + 1) * rows), slice(b * width, (b + 1) * width))
-            if first:
-                value = block.astype(F32)
-            else:
-                value = (block.astype(F32) + offsets[a] * before_ref[at]) * scale
-            if keep:
-                density_ref[at] = value
-            high = value.astype(BF)
-            columns_ref[at] = high.astype(F32)
-            if not first:
-                low = (slice(total + a * rows, total + (a + 1) * rows), at[1])
-                columns_ref[low] = value - high.astype(F32)
+        for z in range(chips):
+            for c in range(CORES):
+                block = packet_refs[c][a * chips + z, :, :width].astype(F32)
+                part = z * CORES + (core ^ c)
+                lanes = pl.ds(pl.multiple_of(part * width, width), width)
+                at = (slice(a * rows, (a + 1) * rows), lanes)
+                value = block
+                if not first:
+                    value = (value + offsets[a] * before_ref[at]) * scale
+                if keep:
+                    density_ref[at] = value
+                high = value.astype(BF).astype(F32)
+                columns_ref[at] = high
+                if not first:
+                    low = (slice(total + a * rows, total + (a + 1) * rows), lanes)
+                    columns_ref[low] = value - high
     columns = columns_ref[...].astype(BF)
     pieces = []
     for q in range(s.transfers):
@@ -289,15 +307,17 @@
             image = image[:total] + image[total:]
         pieces.extend(three_pieces(image))
     stacked = jnp.concatenate([piece.astype(BF) for piece in pieces], axis=0)
-    field = jnp.dot(pick_ref[...], stacked, preferred_element_type=F32)
+    field_ref[...] = jnp.dot(pick_ref[...], stacked, preferred_element_type=F32)
+    mine = lax.axis_index("kpt")
     for a in range(s.groups):
-        out_ref[a] = field[a * rows : (a + 1) * rows]
-
-
-def field_kernel(s, first, pieces_ref, left_ref, out_ref):
-    field = pieces_ref[0]
-    for a in range(1, s.groups):
-        field = field + pieces_ref[a]
+        out_refs[a][...] = field_ref[pl.ds(pl.multiple_of((mine ^ a) * rows, rows), rows), :]
+
+
+def field_kernel(s, first, *refs):
+    left_ref, out_ref = refs[-2:]
+    field = refs[0][...]
+    for ref in refs[1:-2]:
+        field = field + ref[...]
     parts = (field.astype(BF),) if first else high_low(field)
     stacked = jnp.concatenate([p.astype(F32) for p in parts], axis=0).astype(BF)
     rows = s.rows
@@ -352,11 +372,19 @@
     s.entries = float(nk * bands)
     total = groups * s.rows
     state = ((s.rows, bands), F32)
-    packet = ((groups * parts, s.rows, width + LANES), BF)
-    both = ("kpt", "pw")
+    packet = ((groups * parts // CORES, s.rows, width + LANES), BF)
+    chip = ("z", "core")
 
     def exchange(x, axes):
         return lax.all_to_all(x, axes, 0, 0, tiled=True)
+
+    def across(x, axis, size, distance):
+        return lax.ppermute(x, axis, [(i, i ^ distance) for i in range(size)])
+
+    def swap(pieces):
+        return [pieces[0]] + [
+            across(piece, "kpt", groups, a) for a, piece in enumerate(pieces) if a
+        ]
 
     screened = pltpu.with_memory_space_constraint(screened, pltpu.VMEM)
     inputs = tuple(
@@ -376,7 +404,7 @@
         + [pltpu.SemaphoreType.DMA((len(inputs),))],
         cost=COVER,
     )
-    start = exchange(start, "pw")
+    start = exchange(start, chip)
     sent, vector, earlier, levels = call(
         functools.partial(unpack_kernel, s),
         (start, pair_right),
@@ -388,9 +416,9 @@
     density = work = None
     for step in range(STEPS):
         first, keep = step == 0, step < STEPS - 1
-        got = exchange(sent, both)
-        args = (got,) + (() if first else (density,)) + (screened, pick)
-        outs = [((groups, s.rows, width), F32)]
+        got = exchange(sent, ("kpt", "z"))
+        args = (got, across(got, "core", CORES, 1)) + (() if first else (density,)) + (screened, pick)
+        outs = [((s.rows, width), F32)] * groups
         outs += [] if first else [((s.rows, LANES), F32)]
         outs += [((total, waves), F32)] if keep else []
         results = call(
@@ -398,20 +426,22 @@
             args,
             outs,
             "screen",
-            scratch=[pltpu.VMEM((total if first else 2 * total, waves), F32)],
-        )
-        field = results[0]
+            scratch=[
+                pltpu.VMEM((total if first else 2 * total, waves), F32),
+                pltpu.VMEM((total, width), F32),
+            ],
+        )
         if not first:
-            scalars.append(results[1])
+            scalars.append(results[groups])
         if keep:
             density = results[-1]
         (direct,) = call(
             functools.partial(field_kernel, s, first),
-            (exchange(field, "kpt"), pair_left),
+            (*swap(results[:groups]), pair_left),
             [((parts, s.rows, bands), BF)],
             "field",
         )
-        direct = exchange(direct, "pw")
+        direct = exchange(direct, chip)
         if first:
             sent, work = call(
                 functools.partial(first_kernel, s),
@@ -431,16 +461,16 @@
             sent, work, vector = call(
                 functools.partial(last_kernel, s),
                 (direct, work, vector, levels, scalars[-1]),
-                [((groups, s.rows, LANES), F32), state, state],
+                [((s.rows, LANES), F32), state, state],
                 "apply",
             )
-    sums = exchange(sent, "kpt")
+    sums = swap([sent] * groups)
     own = (current.shape, F32)
     terms = ((s.chains, STEPS), F32)
     return tuple(
         call(
             functools.partial(end_kernel, s),
-            (sums, work, vector, *scalars),
+            (*sums, work, vector, *scalars),
             [own, own, terms, terms],
             "end",
         )
@@ -448,19 +478,22 @@
 
 
 def solution(mesh):
+    groups, parts = mesh.shape["kpt"], mesh.shape["pw"]
+    devices = mesh.devices.reshape(groups, parts // CORES, CORES)
+    pw = ("z", "core")
     return jax.shard_map(
-        functools.partial(on_device, mesh.shape["kpt"], mesh.shape["pw"]),
-        mesh=mesh,
+        functools.partial(on_device, groups, parts),
+        mesh=jax.sharding.Mesh(devices, ("kpt", *pw)),
         in_specs=(
-            P("kpt", "pw"),
-            P(None, "kpt", "pw"),
-            P(None, "kpt", "pw"),
+            P("kpt", pw),
+            P(None, "kpt", pw),
+            P(None, "kpt", pw),
             P(),
-            P("kpt", None, "pw"),
-            P("kpt", None, "pw"),
-            P("kpt", "pw", None),
+            P("kpt", None, pw),
+            P("kpt", None, pw),
+            P("kpt", pw, None),
             P(),
         ),
-        out_specs=(P(None, "kpt", "pw"), P(None, "kpt", "pw"), P(), P()),
+        out_specs=(P(None, "kpt", pw), P(None, "kpt", pw), P(), P()),
         check_vma=False,
     )

time: 133 us -> 127 us (0.955)
  blocking collectives: 108 us -> 74.4 us
  starting transfers between devices: 0 us -> 14.2 us
  waiting for transfers between devices: 0 us -> 13.9 us
    all_to_all x11 -> x7, blocking collectives: 108 us -> 74.4 us  [exchange(): return lax.all_to_all(x, axes, 0, 0, tiled=True)]
    ppermute x0 -> x15, starting transfers between devices: none -> 14.2 us  [across(): return lax.ppermute(x, axis, [(i, i ^ distance) for i in range(size)])]
    ppermute x0 -> x15, waiting for transfers between devices: none -> 13.9 us  [across(): return lax.ppermute(x, axis, [(i, i ^ distance) for i in range(size)])]
  transfers between devices with their start and end apart: 0 -> 15, of which waited for: 0 -> 15; matrix products, arithmetic and copies ran while one was open for 0% -> 0% of each run, Pallas kernels for 0% -> 0%
where the time goes in v3:
time: 127 us
  blocking collectives  74.4 us (59%)
  Pallas kernels  23.4 us (18%)
  starting transfers between devices  14.2 us (11%)
  waiting for transfers between devices  13.9 us (11%)
    all_to_all x7, blocking collectives, exchange(): return lax.all_to_all(x, axes, 0, 0, tiled=True)  74.4 us
    pallas_call x12, Pallas kernels, call(): pl.pallas_call(body, out_shape=[jax.ShapeDtypeStruct(shape, dtype) for sh...  23.4 us
    ppermute x15, starting transfers between devices, across(): return lax.ppermute(x, axis, [(i, i ^ distance) for i in range(size)])  14.2 us
    ppermute x15, waiting for transfers between devices, across(): return lax.ppermute(x, axis, [(i, i ^ distance) for i in range(size)])  13.9 us
  transfers between devices with their start and end apart: 15, of which 15 were waited for; matrix products, arithmetic and copies ran while one was open for 0% of the time, Pallas kernels for 0%

profile of v3, /device:TPU:0, one launch (start us, length us, event | category | flops | bytes accessed | tf_op | source)
XLA Modules:
  0.0 126.7 jit_solution(7908884800030689416)
XLA Ops:
  0.6 0.0 copy-start.1
  0.6 0.0 slice-start
  0.7 0.0 slice-start.1
  0.7 1.3 begin.1
  1.9 12.3 %all_to_all.35.gathered_ref = f32[8,16,128]{2,1,0:T(8,128)S(1)} all-to-all(f32[8,16,128]{2,1,0:T(8,128)S(1)} %get-tuple-element.34), channel_id=1, replica_groups=mesh['kpt'=4,'z'=4,'core'=2] {'z','core'}, dimensions={0} | all-to-all | bytes 131072 | tf_op jit(solution)/shard_map/all_to_all | solution.py:379
  14.3 0.0 copy-done.1
  14.3 0.0 slice-start.2
  14.3 0.0 slice-start.3
  14.3 0.4 unpack.1
  14.7 12.6 %all_to_all.36.refs_0_ = bf16[16,8,640]{2,1,0:T(8,128)(2,1)S(1)} all-to-all(bf16[16,8,640]{2,1,0:T(8,128)(2,1)S(1)} %get-tuple-element.35), channel_id=1, replica_groups=mesh['kpt'=4,'z'=4,'core'=2] {'kpt','z'}, dimensions={0} | all-to-all | bytes 327680 | tf_op jit(solution)/shard_map/all_to_all | solution.py:379
  27.3 0.0 collective-permute-start
  27.3 1.4 %collective-permute-done.refs_1_ = bf16[16,8,640]{2,1,0:T(8,128)(2,1)S(1)} collective-permute-done((bf16[16,8,640]{2,1,0:T(8,128)(2,1)S(1)}, bf16[16,8,640]{2,1,0:T(8,128)(2,1)S(1)}, u32[]{:S(2)}, u32[]{:S(2)}) %collective-permute-start) | collective-permute-done | bytes 163872 | tf_op jit(solution)/shard_map/ppermute | solution.py:382
  28.7 0.0 slice-done
  28.7 0.0 slice-done.1
  28.7 0.0 slice-done.2
  28.7 0.0 slice-done.3
  28.7 0.0 copy-start
  28.7 4.8 %screen.3 = (f32[8,512]{1,0:T(8,128)S(1)}, f32[8,512]{1,0:T(8,128)S(1)}, f32[8,512]{1,0:T(8,128)S(1)}, f32[8,512]{1,0:T(8,128)S(1)}, f32[32,4096]{1,0:T(8,128)S(1)}) custom-call(bf16[16,8,640]{2,1,0:T(8,128)(2,1)S(1)} %all_to_all.36.refs_0_, bf16[16,8,640]{2,1,0:T(8,128)(2,1)S(1)} %collective-permute-done.refs_1_, bf16[4,512,4096]{2,1,0:T(8,128)(2,1)S(1)} %bitcast.1, ...), custom_call_target="tpu_custom_call" | custom-call | tf_op jit(solution)/shard_map/screen/pallas_call | solution.py:347
  33.5 0.0 copy-start.2
  33.5 0.4 collective-permute-start.1
  33.9 0.8 collective-permute-start.2
  34.7 2.4 %collective-permute-start.3 = (f32[8,512]{1,0:T(8,128)S(1)}, f32[8,512]{1,0:T(8,128)S(1)}, u32[]{:S(2)}, u32[]{:S(2)}) collective-permute-start(f32[8,512]{1,0:T(8,128)S(1)} %get-tuple-element.40), channel_id=1, source_target_pairs={{0,24},{8,16},{16,8},{24,0},{1,25},{9,17},{17,9},{25,1},{2,26},{10... | collective-permute-start | bytes 49160 | tf_op jit(solution)/shard_map/ppermute | solution.py:382
  37.1 0.2 collective-permute-done.1.refs_1_
  37.3 0.3 collective-permute-done.2.refs_2_
  37.7 1.7 %collective-permute-done.3.refs_3_ = f32[8,512]{1,0:T(8,128)S(1)} collective-permute-done((f32[8,512]{1,0:T(8,128)S(1)}, f32[8,512]{1,0:T(8,128)S(1)}, u32[]{:S(2)}, u32[]{:S(2)}) %collective-permute-start.3) | collective-permute-done | bytes 16416 | tf_op jit(solution)/shard_map/ppermute | solution.py:382
  39.4 0.0 copy-done
  39.4 0.6 field.3
  40.0 8.4 %all_to_all.37.partial_ref = bf16[8,8,512]{2,1,0:T(8,128)(2,1)S(1)} all-to-all(bf16[8,8,512]{2,1,0:T(8,128)(2,1)S(1)} %field.3), channel_id=1, replica_groups=mesh['kpt'=4,'z'=4,'core'=2] {'z','core'}, dimensions={0} | all-to-all | bytes 131072 | tf_op jit(solution)/shard_map/all_to_all | solution.py:379
  48.4 0.0 copy-done.2
  48.4 1.4 %apply.3 = (bf16[16,8,640]{2,1,0:T(8,128)(2,1)S(1)}, f32[8,512]{1,0:T(8,128)S(1)}) custom-call(bf16[8,8,512]{2,1,0:T(8,128)(2,1)S(1)} %all_to_all.37.partial_ref, f32[8,512]{1,0:T(8,128)S(1)} %get-tuple-element.41.vector_ref, f32[8,512]{1,0:T(8,128)S(1)} %get-tuple-element.42.earlier_ref, f32[8,512]{1,0:T(8,128)S(1)} %get-tuple-element.43.levels_ref, ...), custom_call_target="tpu_custom_call" | custom-call | tf_op jit(solution)/shard_map/apply/pallas_call | solution.py:347
  49.9 12.1 %all_to_all.38.refs_0_ = bf16[16,8,640]{2,1,0:T(8,128)(2,1)S(1)} all-to-all(bf16[16,8,640]{2,1,0:T(8,128)(2,1)S(1)} %get-tuple-element.44), channel_id=1, replica_groups=mesh['kpt'=4,'z'=4,'core'=2] {'kpt','z'}, dimensions={0} | all-to-all | bytes 327680 | tf_op jit(solution)/shard_map/all_to_all | solution.py:379
  62.0 0.0 collective-permute-start.4
  62.0 1.4 %collective-permute-done.4.refs_1_ = bf16[16,8,640]{2,1,0:T(8,128)(2,1)S(1)} collective-permute-done((bf16[16,8,640]{2,1,0:T(8,128)(2,1)S(1)}, bf16[16,8,640]{2,1,0:T(8,128)(2,1)S(1)}, u32[]{:S(2)}, u32[]{:S(2)}) %collective-permute-start.4) | collective-permute-done | bytes 163872 | tf_op jit(solution)/shard_map/ppermute | solution.py:382
  63.4 5.3 %screen.4 = (f32[8,512]{1,0:T(8,128)S(1)}, f32[8,512]{1,0:T(8,128)S(1)}, f32[8,512]{1,0:T(8,128)S(1)}, f32[8,512]{1,0:T(8,128)S(1)}, f32[8,128]{1,0:T(8,128)S(1)}, /*index=5*/f32[32,4096]{1,0:T(8,128)S(1)}) custom-call(bf16[16,8,640]{2,1,0:T(8,128)(2,1)S(1)} %all_to_all.38.refs_0_, bf16[16,8,640]{2,1,0:T(8,128)(2,1)S(1)} %collective-permute-done.4.refs_1_, ...), custom_call_target="tpu_custom_call" | custom-call | tf_op jit(solution)/shard_map/screen/pallas_call | solution.py:347
  68.7 0.4 collective-permute-start.5
  69.0 0.8 collective-permute-start.6
  69.8 2.4 %collective-permute-start.7 = (f32[8,512]{1,0:T(8,128)S(1)}, f32[8,512]{1,0:T(8,128)S(1)}, u32[]{:S(2)}, u32[]{:S(2)}) collective-permute-start(f32[8,512]{1,0:T(8,128)S(1)} %get-tuple-element.49), channel_id=1, source_target_pairs={{0,24},{8,16},{16,8},{24,0},{1,25},{9,17},{17,9},{25,1},{2,26},{10... | collective-permute-start | bytes 49160 | tf_op jit(solution)/shard_map/ppermute | solution.py:382
  72.2 0.2 collective-permute-done.5.refs_1_
  72.5 0.3 collective-permute-done.6.refs_2_
  72.8 1.7 %collective-permute-done.7.refs_3_ = f32[8,512]{1,0:T(8,128)S(1)} collective-permute-done((f32[8,512]{1,0:T(8,128)S(1)}, f32[8,512]{1,0:T(8,128)S(1)}, u32[]{:S(2)}, u32[]{:S(2)}) %collective-permute-start.7) | collective-permute-done | bytes 16416 | tf_op jit(solution)/shard_map/ppermute | solution.py:382
  74.5 0.7 field.4
  75.1 8.4 %all_to_all.39.partial_ref = bf16[8,8,512]{2,1,0:T(8,128)(2,1)S(1)} all-to-all(bf16[8,8,512]{2,1,0:T(8,128)(2,1)S(1)} %field.4), channel_id=1, replica_groups=mesh['kpt'=4,'z'=4,'core'=2] {'z','core'}, dimensions={0} | all-to-all | bytes 131072 | tf_op jit(solution)/shard_map/all_to_all | solution.py:379
  83.6 0.9 apply.4
  84.5 12.1 %all_to_all.40.refs_0_ = bf16[16,8,640]{2,1,0:T(8,128)(2,1)S(1)} all-to-all(bf16[16,8,640]{2,1,0:T(8,128)(2,1)S(1)} %get-tuple-element.52), channel_id=1, replica_groups=mesh['kpt'=4,'z'=4,'core'=2] {'kpt','z'}, dimensions={0} | all-to-all | bytes 327680 | tf_op jit(solution)/shard_map/all_to_all | solution.py:379
  96.6 0.0 collective-permute-start.8
  96.6 1.4 %collective-permute-done.8.refs_1_ = bf16[16,8,640]{2,1,0:T(8,128)(2,1)S(1)} collective-permute-done((bf16[16,8,640]{2,1,0:T(8,128)(2,1)S(1)}, bf16[16,8,640]{2,1,0:T(8,128)(2,1)S(1)}, u32[]{:S(2)}, u32[]{:S(2)}) %collective-permute-start.8) | collective-permute-done | bytes 163872 | tf_op jit(solution)/shard_map/ppermute | solution.py:382
  98.0 5.3 %screen.5 = (f32[8,512]{1,0:T(8,128)S(1)}, f32[8,512]{1,0:T(8,128)S(1)}, f32[8,512]{1,0:T(8,128)S(1)}, f32[8,512]{1,0:T(8,128)S(1)}, f32[8,128]{1,0:T(8,128)S(1)}) custom-call(bf16[16,8,640]{2,1,0:T(8,128)(2,1)S(1)} %all_to_all.40.refs_0_, bf16[16,8,640]{2,1,0:T(8,128)(2,1)S(1)} %collective-permute-done.8.refs_1_, f32[32,4096]{1,0:T(8,128)S(1)} %get-tuple-element.53.refs_2_, ...), custom_call_target="tpu_custom_call" | custom-call | tf_op jit(solution)/shard_map/screen/pallas_call | solution.py:347
  103.3 0.4 collective-permute-start.9
  103.7 0.8 collective-permute-start.10
  104.5 2.4 %collective-permute-start.11 = (f32[8,512]{1,0:T(8,128)S(1)}, f32[8,512]{1,0:T(8,128)S(1)}, u32[]{:S(2)}, u32[]{:S(2)}) collective-permute-start(f32[8,512]{1,0:T(8,128)S(1)} %get-tuple-element.57), channel_id=1, source_target_pairs={{0,24},{8,16},{16,8},{24,0},{1,25},{9,17},{17,9},{25,1},{2,26},{10... | collective-permute-start | bytes 49160 | tf_op jit(solution)/shard_map/ppermute | solution.py:382
  106.8 0.2 collective-permute-done.9.refs_1_
  107.1 0.3 collective-permute-done.10.refs_2_
  107.4 1.7 %collective-permute-done.11.refs_3_ = f32[8,512]{1,0:T(8,128)S(1)} collective-permute-done((f32[8,512]{1,0:T(8,128)S(1)}, f32[8,512]{1,0:T(8,128)S(1)}, u32[]{:S(2)}, u32[]{:S(2)}) %collective-permute-start.11) | collective-permute-done | bytes 16416 | tf_op jit(solution)/shard_map/ppermute | solution.py:382
  109.1 0.7 field.5
  109.8 8.4 %all_to_all.41.partial_ref = bf16[8,8,512]{2,1,0:T(8,128)(2,1)S(1)} all-to-all(bf16[8,8,512]{2,1,0:T(8,128)(2,1)S(1)} %field.5), channel_id=1, replica_groups=mesh['kpt'=4,'z'=4,'core'=2] {'z','core'}, dimensions={0} | all-to-all | bytes 131072 | tf_op jit(solution)/shard_map/all_to_all | solution.py:379
  118.2 0.5 apply.5
  118.7 2.3 %collective-permute-start.14 = (f32[8,128]{1,0:T(8,128)S(1)}, f32[8,128]{1,0:T(8,128)S(1)}, u32[]{:S(2)}, u32[]{:S(2)}) collective-permute-start(f32[8,128]{1,0:T(8,128)S(1)} %get-tuple-element.61.refs_0_), channel_id=1, source_target_pairs={{0,24},{8,16},{16,8},{24,0},{1,25},{9,17},{17,9},{25,1},{2,26},{10... | collective-permute-start | bytes 12296 | tf_op jit(solution)/shard_map/ppermute | solution.py:382
  121.0 0.6 collective-permute-start.13
  121.5 0.7 collective-permute-start.12
  122.2 1.0 collective-permute-done.14.refs_3_
  123.2 1.3 %collective-permute-done.13.refs_2_ = f32[8,128]{1,0:T(8,128)S(1)} collective-permute-done((f32[8,128]{1,0:T(8,128)S(1)}, f32[8,128]{1,0:T(8,128)S(1)}, u32[]{:S(2)}, u32[]{:S(2)}) %collective-permute-start.13) | collective-permute-done | bytes 4128 | tf_op jit(solution)/shard_map/ppermute | solution.py:382
  124.6 0.6 collective-permute-done.12.refs_1_
  125.1 1.6 %end.1 = (f32[2,4,64]{2,1,0:T(4,128)}, f32[2,4,64]{2,1,0:T(4,128)}, f32[2,3]{1,0:T(2,128)}, f32[2,3]{1,0:T(2,128)}) custom-call(f32[8,128]{1,0:T(8,128)S(1)} %get-tuple-element.61.refs_0_, f32[8,128]{1,0:T(8,128)S(1)} %collective-permute-done.12.refs_1_, f32[8,128]{1,0:T(8,128)S(1)} %collective-permute-done.13.refs_2_, ...), custom_call_target="tpu_custom_call" | custom-call | tf_op jit(solution)/shard_map/end/pallas_call | solution.py:347
  (1 shorter events, 0.0 us)
Async XLA Ops:
  0.6 13.6 %copy-start.1 = (bf16[4,512,512]{2,1,0:T(8,128)(2,1)S(1)}, bf16[4,512,512]{2,1,0:T(8,128)(2,1)}, u32[]{:S(2)}) copy-start(bf16[4,512,512]{2,1,0:T(8,128)(2,1)} %right_ref.5) | copy-start | bytes 6291460
  0.6 28.1 %slice-start = ((s8[16777216]{0:T(1024)(128)(4,1)}), s8[4194304]{0:T(1024)(128)(4,1)S(1)}, s32[]{:S(2)}) async-start(s8[16777216]{0:T(1024)(128)(4,1)} %bitcast), calls=%async_computation.7 | async-start | bytes 8388608
  0.7 28.0 %slice-start.1 = ((s8[16777216]{0:T(1024)(128)(4,1)}), s8[4194304]{0:T(1024)(128)(4,1)S(1)}, s32[]{:S(2)}) async-start(s8[16777216]{0:T(1024)(128)(4,1)} %bitcast), calls=%async_computation.8 | async-start | bytes 8388608
  14.3 14.4 %slice-start.2 = ((s8[16777216]{0:T(1024)(128)(4,1)}), s8[4194304]{0:T(1024)(128)(4,1)S(1)}, s32[]{:S(2)}) async-start(s8[16777216]{0:T(1024)(128)(4,1)} %bitcast), calls=%async_computation.9 | async-start | bytes 8388608
  14.3 14.4 %slice-start.3 = ((s8[16777216]{0:T(1024)(128)(4,1)}), s8[4194304]{0:T(1024)(128)(4,1)S(1)}, s32[]{:S(2)}) async-start(s8[16777216]{0:T(1024)(128)(4,1)} %bitcast), calls=%async_computation.10 | async-start | bytes 8388608
  27.3 1.4 %collective-permute-start = (bf16[16,8,640]{2,1,0:T(8,128)(2,1)S(1)}, bf16[16,8,640]{2,1,0:T(8,128)(2,1)S(1)}, u32[]{:S(2)}, u32[]{:S(2)}) collective-permute-start(bf16[16,8,640]{2,1,0:T(8,128)(2,1)S(1)} %all_to_all.36.refs_0_), channel_id=1, source_target_pairs={{0,1},{1,0},{2,3},{3,2},{4,5},{5,4},{6,7},{7,6},{8,9},{9,8},{10,11... | collective-permute-start | bytes 491528 | tf_op jit(solution)/shard_map/ppermute | solution.py:382
  28.7 10.6 %copy-start = (bf16[4,512,512]{2,1,0:T(8,128)(2,1)S(1)}, bf16[4,512,512]{2,1,0:T(8,128)(2,1)}, u32[]{:S(2)}) copy-start(bf16[4,512,512]{2,1,0:T(8,128)(2,1)} %refs_4_.5) | copy-start | bytes 6291460
  33.5 14.9 %copy-start.2 = (f32[2]{0:T(128)S(1)}, f32[2]{0:T(128)}, u32[]{:S(2)}) copy-start(f32[2]{0:T(128)} %beta_ref.1) | copy-start | bytes 28
  33.5 3.8 %collective-permute-start.1 = (f32[8,512]{1,0:T(8,128)S(1)}, f32[8,512]{1,0:T(8,128)S(1)}, u32[]{:S(2)}, u32[]{:S(2)}) collective-permute-start(f32[8,512]{1,0:T(8,128)S(1)} %get-tuple-element.38), channel_id=1, source_target_pairs={{0,8},{8,0},{16,24},{24,16},{1,9},{9,1},{17,25},{25,17},{2,10},{10... | collective-permute-start | bytes 49160 | tf_op jit(solution)/shard_map/ppermute | solution.py:382
  33.9 3.7 %collective-permute-start.2 = (f32[8,512]{1,0:T(8,128)S(1)}, f32[8,512]{1,0:T(8,128)S(1)}, u32[]{:S(2)}, u32[]{:S(2)}) collective-permute-start(f32[8,512]{1,0:T(8,128)S(1)} %get-tuple-element.39), channel_id=1, source_target_pairs={{0,16},{8,24},{16,0},{24,8},{1,17},{9,25},{17,1},{25,9},{2,18},{10... | collective-permute-start | bytes 49160 | tf_op jit(solution)/shard_map/ppermute | solution.py:382
  34.7 4.6 %collective-permute-start.3 = (f32[8,512]{1,0:T(8,128)S(1)}, f32[8,512]{1,0:T(8,128)S(1)}, u32[]{:S(2)}, u32[]{:S(2)}) collective-permute-start(f32[8,512]{1,0:T(8,128)S(1)} %get-tuple-element.40), channel_id=1, source_target_pairs={{0,24},{8,16},{16,8},{24,0},{1,25},{9,17},{17,9},{25,1},{2,26},{10... | collective-permute-start | bytes 49160 | tf_op jit(solution)/shard_map/ppermute | solution.py:382
  62.0 1.4 %collective-permute-start.4 = (bf16[16,8,640]{2,1,0:T(8,128)(2,1)S(1)}, bf16[16,8,640]{2,1,0:T(8,128)(2,1)S(1)}, u32[]{:S(2)}, u32[]{:S(2)}) collective-permute-start(bf16[16,8,640]{2,1,0:T(8,128)(2,1)S(1)} %all_to_all.38.refs_0_), channel_id=1, source_target_pairs={{0,1},{1,0},{2,3},{3,2},{4,5},{5,4},{6,7},{7,6},{8,9},{9,8},{10,11... | collective-permute-start | bytes 491528 | tf_op jit(solution)/shard_map/ppermute | solution.py:382
  68.7 3.8 %collective-permute-start.5 = (f32[8,512]{1,0:T(8,128)S(1)}, f32[8,512]{1,0:T(8,128)S(1)}, u32[]{:S(2)}, u32[]{:S(2)}) collective-permute-start(f32[8,512]{1,0:T(8,128)S(1)} %get-tuple-element.47), channel_id=1, source_target_pairs={{0,8},{8,0},{16,24},{24,16},{1,9},{9,1},{17,25},{25,17},{2,10},{10... | collective-permute-start | bytes 49160 | tf_op jit(solution)/shard_map/ppermute | solution.py:382
  69.0 3.7 %collective-permute-start.6 = (f32[8,512]{1,0:T(8,128)S(1)}, f32[8,512]{1,0:T(8,128)S(1)}, u32[]{:S(2)}, u32[]{:S(2)}) collective-permute-start(f32[8,512]{1,0:T(8,128)S(1)} %get-tuple-element.48), channel_id=1, source_target_pairs={{0,16},{8,24},{16,0},{24,8},{1,17},{9,25},{17,1},{25,9},{2,18},{10... | collective-permute-start | bytes 49160 | tf_op jit(solution)/shard_map/ppermute | solution.py:382
  69.8 4.6 %collective-permute-start.7 = (f32[8,512]{1,0:T(8,128)S(1)}, f32[8,512]{1,0:T(8,128)S(1)}, u32[]{:S(2)}, u32[]{:S(2)}) collective-permute-start(f32[8,512]{1,0:T(8,128)S(1)} %get-tuple-element.49), channel_id=1, source_target_pairs={{0,24},{8,16},{16,8},{24,0},{1,25},{9,17},{17,9},{25,1},{2,26},{10... | collective-permute-start | bytes 49160 | tf_op jit(solution)/shard_map/ppermute | solution.py:382
  96.6 1.4 %collective-permute-start.8 = (bf16[16,8,640]{2,1,0:T(8,128)(2,1)S(1)}, bf16[16,8,640]{2,1,0:T(8,128)(2,1)S(1)}, u32[]{:S(2)}, u32[]{:S(2)}) collective-permute-start(bf16[16,8,640]{2,1,0:T(8,128)(2,1)S(1)} %all_to_all.40.refs_0_), channel_id=1, source_target_pairs={{0,1},{1,0},{2,3},{3,2},{4,5},{5,4},{6,7},{7,6},{8,9},{9,8},{10,11... | collective-permute-start | bytes 491528 | tf_op jit(solution)/shard_map/ppermute | solution.py:382
  103.3 3.8 %collective-permute-start.9 = (f32[8,512]{1,0:T(8,128)S(1)}, f32[8,512]{1,0:T(8,128)S(1)}, u32[]{:S(2)}, u32[]{:S(2)}) collective-permute-start(f32[8,512]{1,0:T(8,128)S(1)} %get-tuple-element.55), channel_id=1, source_target_pairs={{0,8},{8,0},{16,24},{24,16},{1,9},{9,1},{17,25},{25,17},{2,10},{10... | collective-permute-start | bytes 49160 | tf_op jit(solution)/shard_map/ppermute | solution.py:382
  103.7 3.7 %collective-permute-start.10 = (f32[8,512]{1,0:T(8,128)S(1)}, f32[8,512]{1,0:T(8,128)S(1)}, u32[]{:S(2)}, u32[]{:S(2)}) collective-permute-start(f32[8,512]{1,0:T(8,128)S(1)} %get-tuple-element.56), channel_id=1, source_target_pairs={{0,16},{8,24},{16,0},{24,8},{1,17},{9,25},{17,1},{25,9},{2,18},{10... | collective-permute-start | bytes 49160 | tf_op jit(solution)/shard_map/ppermute | solution.py:382
  104.5 4.6 %collective-permute-start.11 = (f32[8,512]{1,0:T(8,128)S(1)}, f32[8,512]{1,0:T(8,128)S(1)}, u32[]{:S(2)}, u32[]{:S(2)}) collective-permute-start(f32[8,512]{1,0:T(8,128)S(1)} %get-tuple-element.57), channel_id=1, source_target_pairs={{0,24},{8,16},{16,8},{24,0},{1,25},{9,17},{17,9},{25,1},{2,26},{10... | collective-permute-start | bytes 49160 | tf_op jit(solution)/shard_map/ppermute | solution.py:382
  118.7 4.5 %collective-permute-start.14 = (f32[8,128]{1,0:T(8,128)S(1)}, f32[8,128]{1,0:T(8,128)S(1)}, u32[]{:S(2)}, u32[]{:S(2)}) collective-permute-start(f32[8,128]{1,0:T(8,128)S(1)} %get-tuple-element.61.refs_0_), channel_id=1, source_target_pairs={{0,24},{8,16},{16,8},{24,0},{1,25},{9,17},{17,9},{25,1},{2,26},{10... | collective-permute-start | bytes 12296 | tf_op jit(solution)/shard_map/ppermute | solution.py:382
  121.0 3.6 %collective-permute-start.13 = (f32[8,128]{1,0:T(8,128)S(1)}, f32[8,128]{1,0:T(8,128)S(1)}, u32[]{:S(2)}, u32[]{:S(2)}) collective-permute-start(f32[8,128]{1,0:T(8,128)S(1)} %get-tuple-element.61.refs_0_), channel_id=1, source_target_pairs={{0,16},{8,24},{16,0},{24,8},{1,17},{9,25},{17,1},{25,9},{2,18},{10... | collective-permute-start | bytes 12296 | tf_op jit(solution)/shard_map/ppermute | solution.py:382
  121.5 3.6 %collective-permute-start.12 = (f32[8,128]{1,0:T(8,128)S(1)}, f32[8,128]{1,0:T(8,128)S(1)}, u32[]{:S(2)}, u32[]{:S(2)}) collective-permute-start(f32[8,128]{1,0:T(8,128)S(1)} %get-tuple-element.61.refs_0_), channel_id=1, source_target_pairs={{0,8},{8,0},{16,24},{24,16},{1,9},{9,1},{17,25},{25,17},{2,10},{10... | collective-permute-start | bytes 12296 | tf_op jit(solution)/shard_map/ppermute | solution.py:382

commit v4 on v3

--- a/solution.py
+++ b/solution.py
@@ -40,17 +40,21 @@
     return jnp.concatenate(parts, axis=0)
 
 
-def begin_kernel(s, *refs):
-    sources, held, sems = refs[:4], refs[6:10], refs[10]
-    pick_ref, out_ref = refs[4:6]
+def copy_all(sources, targets, sems):
     started = [
         pltpu.make_async_copy(source, target, sems.at[at])
-        for at, (source, target) in enumerate(zip(sources, held))
+        for at, (source, target) in enumerate(zip(sources, targets))
     ]
     for copy in started:
         copy.start()
     for copy in started:
         copy.wait()
+
+
+def begin_kernel(s, *refs):
+    sources, held, sems = refs[:4], refs[6:10], refs[10]
+    pick_ref, out_ref = refs[4:6]
+    copy_all(sources, held, sems)
     mi_ref, current_ref, previous_ref, energies_ref = held
     rows = s.rows
     both = []
@@ -95,19 +99,19 @@
             ],
             axis=1,
         )
-    density = project(s, vector_ref[...].astype(BF), right_ref)
+    density = project(s, (vector_ref[...].astype(BF),), right_ref)
     send(s, density, jnp.zeros((rows, LANES), F32), packet_ref)
 
 
-def project(s, x, right_ref):
-    rows, bands = x.shape
+def project(s, parts, right_ref):
+    x = jnp.concatenate([part.astype(F32) for part in parts], axis=0)
     total = None
     for k in range(s.kpoints):
-        own = iota((rows, bands), 0) % s.kpoints == k
-        masked = jnp.where(own, x.astype(F32), 0.0).astype(BF)
+        own = iota(x.shape, 0) % s.kpoints == k
+        masked = jnp.where(own, x, 0.0).astype(BF)
         part = jnp.dot(masked, right_ref[k], preferred_element_type=F32)
         total = part if total is None else total + part
-    return total
+    return sum(total[at : at + s.rows] for at in range(0, x.shape[0], s.rows))
 
 
 def send(s, density, sums, packet_ref):
@@ -119,10 +123,13 @@
         packet_ref[d, :, width:] = sums
 
 
-def apply_step(s, partial_ref, vector, earlier, levels, beta):
-    direct = partial_ref[0].astype(F32)
-    for b in range(1, s.parts):
-        direct = direct + partial_ref[b].astype(F32)
+def pair_kernel(s, own_ref, other_ref, out_ref):
+    out_ref[...] = (own_ref[...] + other_ref[...]).astype(BF)
+
+
+def apply_step(s, refs, vector, earlier, levels, beta):
+    pieces = [ref[...].astype(F32) for ref in refs]
+    direct = sum(in_order(lax.axis_index("z"), pieces))
     applied = levels * vector - direct - beta * earlier
     square = chain_rows(vector * vector, s.chains)
     cross = chain_rows(vector * applied, s.chains)
@@ -159,24 +166,24 @@
     return alpha, beta, offsets
 
 
-def later_kernel(
-    s, partial_ref, work_ref, vector_ref, levels_ref, scalars_ref, right_ref,
-    packet_ref, new_work_ref, new_vector_ref
-):
+def later_kernel(s, *refs):
+    direct_refs, refs = refs[: s.chips], refs[s.chips :]
+    work_ref, vector_ref, levels_ref, scalars_ref, right_ref = refs[:5]
+    packet_ref, new_work_ref, new_vector_ref = refs[5:]
     vector, beta = advance(work_ref, vector_ref, scalars_ref)
     new_vector_ref[...] = vector
-    work, packed = apply_step(s, partial_ref, vector, vector_ref[...], levels_ref[...], beta)
+    work, packed = apply_step(s, direct_refs, vector, vector_ref[...], levels_ref[...], beta)
     new_work_ref[...] = work
     finish_packet(s, work, packed, right_ref, packet_ref)
 
 
-def first_kernel(
-    s, partial_ref, vector_ref, earlier_ref, levels_ref, beta_ref, right_ref,
-    packet_ref, new_work_ref
-):
+def first_kernel(s, *refs):
+    direct_refs, refs = refs[: s.chips], refs[s.chips :]
+    vector_ref, earlier_ref, levels_ref, beta_ref, right_ref = refs[:5]
+    packet_ref, new_work_ref = refs[5:]
     beta = first_beta(s, beta_ref)
     work, packed = apply_step(
-        s, partial_ref, vector_ref[...], earlier_ref[...], levels_ref[...], beta
+        s, direct_refs, vector_ref[...], earlier_ref[...], levels_ref[...], beta
     )
     new_work_ref[...] = work
     finish_packet(s, work, packed, right_ref, packet_ref)
@@ -186,7 +193,7 @@
     row = iota((s.rows, 1), 0) // s.kpoints
     beta = jnp.zeros((s.rows, 1), F32)
     for n in range(s.chains):
-        beta = jnp.where(row == n, beta_ref[n], beta)
+        beta = jnp.where(row == n, beta_ref[:, n : n + 1], beta)
     return beta
 
 
@@ -197,34 +204,36 @@
 
 
 def finish_packet(s, work, packed, right_ref, packet_ref):
-    high, low = high_low(work)
-    density = project(s, high, right_ref) + project(s, low, right_ref)
-    send(s, density, packed, packet_ref)
-
-
-def last_kernel(
-    s, partial_ref, work_ref, vector_ref, levels_ref, scalars_ref,
-    packet_ref, new_work_ref, new_vector_ref
-):
+    send(s, project(s, high_low(work), right_ref), packed, packet_ref)
+
+
+def last_kernel(s, *refs):
+    direct_refs, refs = refs[: s.chips], refs[s.chips :]
+    work_ref, vector_ref, levels_ref, scalars_ref = refs[:4]
+    packet_ref, new_work_ref, new_vector_ref = refs[4:]
     vector, beta = advance(work_ref, vector_ref, scalars_ref)
     new_vector_ref[...] = vector
-    work, packed = apply_step(s, partial_ref, vector, vector_ref[...], levels_ref[...], beta)
+    work, packed = apply_step(s, direct_refs, vector, vector_ref[...], levels_ref[...], beta)
     new_work_ref[...] = work
     packet_ref[...] = packed
+
+
+def in_order(me, pieces):
+    ordered = []
+    for source in range(len(pieces)):
+        piece = pieces[0]
+        for distance in range(1, len(pieces)):
+            piece = jnp.where((me ^ source) == distance, pieces[distance], piece)
+        ordered.append(piece)
+    return ordered
 
 
 def end_kernel(s, *refs):
     sums, refs = [ref[...] for ref in refs[: s.groups]], refs[s.groups :]
     work_ref, vector_ref = refs[:2]
-    scalar_refs, (last_ref, prior_ref, alphas_ref, betas_ref) = refs[2:-4], refs[-4:]
-    mine = lax.axis_index("kpt")
-    tiles = []
-    for a in range(s.groups):
-        tile = sums[0]
-        for other in range(1, s.groups):
-            tile = jnp.where((mine ^ a) == other, sums[other], tile)
-        tiles.append(tile)
-    alpha, beta, offsets = read_sums(s, tiles)
+    scalar_refs, targets, held, sems = refs[2:-9], refs[-9:-5], refs[-5:-1], refs[-1]
+    last_ref, prior_ref, alphas_ref, betas_ref = held
+    alpha, beta, offsets = read_sums(s, in_order(lax.axis_index("kpt"), sums))
     offset = own_offset(s, offsets)
     vector = vector_ref[...]
     last = (work_ref[...] + offset * vector) / beta
@@ -243,6 +252,7 @@
         at = slice(n * k, n * k + 1)
         alphas_ref[n : n + 1, :] = jnp.concatenate([x[at] for x in alphas], axis=1)
         betas_ref[n : n + 1, :] = jnp.concatenate([x[at] for x in betas], axis=1)
+    copy_all(held, targets, sems)
 
 
 def own_offset(s, offsets):
@@ -253,8 +263,40 @@
     return own
 
 
+def images(s, packet_ref, screened_ref, other):
+    width = packet_ref.shape[2] - LANES
+    rows, core = s.rows, lax.axis_index("core") ^ other
+    columns = []
+    for z in range(s.chips):
+        blocks = [
+            packet_ref[a * s.chips + z, :, :width].astype(F32) for a in range(s.groups)
+        ]
+        columns.append(jnp.concatenate(blocks, axis=0).astype(BF))
+    result = []
+    for q in range(s.transfers):
+        image = None
+        for z in range(s.chips):
+            part = z * CORES + core
+            lanes = pl.ds(pl.multiple_of(part * width, width), width)
+            piece = lax.dot_general(
+                screened_ref[q, :, lanes],
+                columns[z],
+                (((1,), (1,)), ((), ())),
+                preferred_element_type=F32,
+            )
+            image = piece if image is None else image + piece
+        result.append(image.T)
+    return result
+
+
+def half_kernel(s, packet_ref, screened_ref, image_ref):
+    for q, image in enumerate(images(s, packet_ref, screened_ref, 0)):
+        image_ref[q] = image
+
+
 def screen_kernel(s, first, keep, *refs):
     refs = list(refs)
+    half_ref = refs.pop(0)
     packet_refs = refs[:CORES]
     del refs[:CORES]
     before_ref = None if first else refs.pop(0)
@@ -262,15 +304,16 @@
     out_refs = refs[2 : 2 + s.groups]
     del refs[: 2 + s.groups]
     scalars_ref = None if first else refs.pop(0)
-    density_ref = refs.pop(0) if keep else None
-    columns_ref, field_ref = refs
-    rows, total = s.rows, s.groups * s.rows
-    chips = s.parts // CORES
+    image_ref = refs.pop(0) if keep else None
+    (field_ref,) = refs
+    rows = s.rows
     width = packet_refs[0].shape[2] - LANES
     core = lax.axis_index("core")
     if not first:
         tiles = [
-            jnp.where(core == 0, *(ref[a * chips, :, width:].astype(F32) for ref in packet_refs))
+            jnp.where(
+                core == 0, *(ref[a * s.chips, :, width:].astype(F32) for ref in packet_refs)
+            )
             for a in range(s.groups)
         ]
         alpha, beta, offsets = read_sums(s, tiles)
@@ -279,32 +322,15 @@
         scalars_ref[...] = jnp.where(
             lane == 0, alpha, jnp.where(lane == 1, beta, own_offset(s, offsets))
         )
-    for a in range(s.groups):
-        for z in range(chips):
-            for c in range(CORES):
-                block = packet_refs[c][a * chips + z, :, :width].astype(F32)
-                part = z * CORES + (core ^ c)
-                lanes = pl.ds(pl.multiple_of(part * width, width), width)
-                at = (slice(a * rows, (a + 1) * rows), lanes)
-                value = block
-                if not first:
-                    value = (value + offsets[a] * before_ref[at]) * scale
-                if keep:
-                    density_ref[at] = value
-                high = value.astype(BF).astype(F32)
-                columns_ref[at] = high
-                if not first:
-                    low = (slice(total + a * rows, total + (a + 1) * rows), lanes)
-                    columns_ref[low] = value - high
-    columns = columns_ref[...].astype(BF)
+        shifts = jnp.concatenate(offsets, axis=0)
+        scales = jnp.concatenate([scale] * s.groups, axis=0)
     pieces = []
-    for q in range(s.transfers):
-        image = lax.dot_general(
-            screened_ref[q], columns, (((1,), (1,)), ((), ())), preferred_element_type=F32
-        )
-        image = image.T
+    for q, image in enumerate(images(s, packet_refs[1], screened_ref, 1)):
+        image = image + half_ref[q]
         if not first:
-            image = image[:total] + image[total:]
+            image = (image + shifts * before_ref[q]) * scales
+        if keep:
+            image_ref[q] = image
         pieces.extend(three_pieces(image))
     stacked = jnp.concatenate([piece.astype(BF) for piece in pieces], axis=0)
     field_ref[...] = jnp.dot(pick_ref[...], stacked, preferred_element_type=F32)
@@ -330,8 +356,7 @@
             image = image[:rows] + image[rows:]
         own = iota(image.shape, 0) % s.kpoints == k
         direct = jnp.where(own, image, 0.0 if direct is None else direct)
-    for b in range(s.parts):
-        out_ref[b] = direct.astype(BF)
+    out_ref[...] = direct
 
 
 class Sizes:
@@ -340,15 +365,14 @@
 
 VMEM = pl.BlockSpec(memory_space=pltpu.VMEM)
 HBM = pl.BlockSpec(memory_space=pltpu.HBM)
-SMEM = pl.BlockSpec(memory_space=pltpu.SMEM)
-
-
-def call(body, args, outs, name, specs=None, scratch=(), limit=24, cost=0):
+
+
+def call(body, args, outs, name, specs=None, out_specs=None, scratch=(), limit=24, cost=0):
     return pl.pallas_call(
         body,
         out_shape=[jax.ShapeDtypeStruct(shape, dtype) for shape, dtype in outs],
         in_specs=specs or [VMEM] * len(args),
-        out_specs=[VMEM] * len(outs),
+        out_specs=out_specs or [VMEM] * len(outs),
         scratch_shapes=list(scratch),
         compiler_params=pltpu.CompilerParams(vmem_limit_bytes=limit * 1024 * 1024),
         name=name,
@@ -363,7 +387,7 @@
     energies, current, previous, previous_beta, pair_left, pair_right, screened, momentum_index
 ):
     s = Sizes()
-    s.groups, s.parts = groups, parts
+    s.groups, s.parts, s.chips = groups, parts, parts // CORES
     s.chains, s.kpoints, band_block = current.shape
     s.rows = s.chains * s.kpoints
     s.transfers, width, waves = screened.shape
@@ -381,9 +405,9 @@
     def across(x, axis, size, distance):
         return lax.ppermute(x, axis, [(i, i ^ distance) for i in range(size)])
 
-    def swap(pieces):
+    def swap(pieces, axis="kpt"):
         return [pieces[0]] + [
-            across(piece, "kpt", groups, a) for a, piece in enumerate(pieces) if a
+            across(piece, axis, len(pieces), at) for at, piece in enumerate(pieces) if at
         ]
 
     screened = pltpu.with_memory_space_constraint(screened, pltpu.VMEM)
@@ -413,54 +437,61 @@
         cost=COVER,
     )
     scalars = []
-    density = work = None
+    before = work = None
     for step in range(STEPS):
         first, keep = step == 0, step < STEPS - 1
         got = exchange(sent, ("kpt", "z"))
-        args = (got, across(got, "core", CORES, 1)) + (() if first else (density,)) + (screened, pick)
+        other = across(got, "core", CORES, 1)
+        image = ((s.transfers, total, width), F32)
+        (half,) = call(
+            functools.partial(half_kernel, s), (got, screened), [image], "half", cost=COVER
+        )
+        args = (half, got, other) + (() if first else (before,)) + (screened, pick)
         outs = [((s.rows, width), F32)] * groups
         outs += [] if first else [((s.rows, LANES), F32)]
-        outs += [((total, waves), F32)] if keep else []
+        outs += [image] if keep else []
         results = call(
             functools.partial(screen_kernel, s, first, keep),
             args,
             outs,
             "screen",
-            scratch=[
-                pltpu.VMEM((total if first else 2 * total, waves), F32),
-                pltpu.VMEM((total, width), F32),
-            ],
+            scratch=[pltpu.VMEM((total, width), F32)],
         )
         if not first:
             scalars.append(results[groups])
         if keep:
-            density = results[-1]
+            before = results[-1]
         (direct,) = call(
             functools.partial(field_kernel, s, first),
             (*swap(results[:groups]), pair_left),
-            [((parts, s.rows, bands), BF)],
+            [state],
             "field",
         )
-        direct = exchange(direct, chip)
+        (direct,) = call(
+            functools.partial(pair_kernel, s),
+            (direct, across(direct, "core", CORES, 1)),
+            [((s.rows, bands), BF)],
+            "pair",
+        )
+        direct = swap([direct] * s.chips, "z")
         if first:
             sent, work = call(
                 functools.partial(first_kernel, s),
-                (direct, vector, earlier, levels, previous_beta, pair_right),
+                (*direct, vector, earlier, levels, previous_beta[None], pair_right),
                 [packet, state],
                 "apply",
-                specs=[VMEM] * 4 + [SMEM, VMEM],
             )
         elif keep:
             sent, work, vector = call(
                 functools.partial(later_kernel, s),
-                (direct, work, vector, levels, scalars[-1], pair_right),
+                (*direct, work, vector, levels, scalars[-1], pair_right),
                 [packet, state, state],
                 "apply",
             )
         else:
             sent, work, vector = call(
                 functools.partial(last_kernel, s),
-                (direct, work, vector, levels, scalars[-1]),
+                (*direct, work, vector, levels, scalars[-1]),
                 [((s.rows, LANES), F32), state, state],
                 "apply",
             )
@@ -473,6 +504,9 @@
             (*sums, work, vector, *scalars),
             [own, own, terms, terms],
             "end",
+            out_specs=[HBM] * 4,
+            scratch=[pltpu.VMEM(*x) for x in (own, own, terms, terms)]
+            + [pltpu.SemaphoreType.DMA((4,))],
         )
     )
 

time: 127 us -> 121 us (0.953)
  blocking collectives: 74.4 us -> 50.3 us
  starting transfers between devices: 14.2 us -> 27.4 us
  waiting for transfers between devices: 13.9 us -> 19.6 us
  Pallas kernels: 23.4 us -> 22 us
    all_to_all x7 -> x4, blocking collectives: 74.4 us -> 50.3 us  [exchange(): return lax.all_to_all(x, axes, 0, 0, tiled=True)]
    ppermute x15 -> x27, starting transfers between devices: 14.2 us -> 27.4 us  [across(): return lax.ppermute(x, axis, [(i, i ^ distance) for i in range(size)])]
    ppermute x15 -> x27, waiting for transfers between devices: 13.9 us -> 19.6 us  [across(): return lax.ppermute(x, axis, [(i, i ^ distance) for i in range(size)])]
    pallas_call x12 -> x18, Pallas kernels: 23.4 us -> 22 us  [call(): pl.pallas_call(body, out_shape=[jax.ShapeDtypeStruct(shape, dtype) for sh...]
  transfers between devices with their start and end apart: 15 -> 27, of which waited for: 15 -> 24; matrix products, arithmetic and copies ran while one was open for 0% -> 0% of each run, Pallas kernels for 0% -> 6%
where the time goes in v4:
time: 121 us; the launch traced here: 120 us
  blocking collectives  50.3 us (42%)
  starting transfers between devices  27.4 us (23%)
  Pallas kernels  22 us (18%)
  waiting for transfers between devices  19.6 us (16%)
    all_to_all x4, blocking collectives, exchange(): return lax.all_to_all(x, axes, 0, 0, tiled=True)  50.3 us
    ppermute x27, starting transfers between devices, across(): return lax.ppermute(x, axis, [(i, i ^ distance) for i in range(size)])  27.4 us
    pallas_call x18, Pallas kernels, call(): pl.pallas_call(body, out_shape=[jax.ShapeDtypeStruct(shape, dtype) for sh...  22 us
    ppermute x27, waiting for transfers between devices, across(): return lax.ppermute(x, axis, [(i, i ^ distance) for i in range(size)])  19.6 us
  transfers between devices with their start and end apart: 27, of which 24 were waited for; matrix products, arithmetic and copies ran while one was open for 0% of the time, Pallas kernels for 6%

profile of v4, /device:TPU:0, one launch (start us, length us, event | category | flops | bytes accessed | tf_op | source)
XLA Modules:
  0.0 120.3 jit_solution(18065827546906258607)
XLA Ops:
  0.7 1.3 %begin.1 = (bf16[32,384]{1,0:T(8,128)(2,1)S(1)}, f32[8,16,128]{2,1,0:T(8,128)S(1)}) custom-call(s32[16,16]{1,0:T(8,128)} %refs_0_.1, f32[2,4,64]{2,1,0:T(4,128)} %refs_1_.1, f32[2,4,64]{2,1,0:T(4,128)} %refs_2_.1, f32[4,64]{1,0:T(4,128)} %refs_3_.2), custom_call_target="tpu_custom_call" | custom-call | flops 5000000000 | bytes 19531250 | tf_op jit(solution)/shard_map/begin/pallas_call | solution.py:371
  1.9 12.3 %all_to_all.20.gathered_ref = f32[8,16,128]{2,1,0:T(8,128)S(1)} all-to-all(f32[8,16,128]{2,1,0:T(8,128)S(1)} %get-tuple-element.34), channel_id=1, replica_groups=mesh['kpt'=4,'z'=4,'core'=2] {'z','core'}, dimensions={0} | all-to-all | bytes 131072 | tf_op jit(solution)/shard_map/all_to_all | solution.py:403
  14.3 0.4 unpack.1
  14.7 12.6 %all_to_all.21.packet_ref.refs_1_ = bf16[16,8,640]{2,1,0:T(8,128)(2,1)S(1)} all-to-all(bf16[16,8,640]{2,1,0:T(8,128)(2,1)S(1)} %get-tuple-element.35), channel_id=1, replica_groups=mesh['kpt'=4,'z'=4,'core'=2] {'kpt','z'}, dimensions={0} | all-to-all | bytes 327680 | tf_op jit(solution)/shard_map/all_to_all | solution.py:403
  27.3 2.4 %half.3.refs_0_ = f32[4,32,512]{2,1,0:T(8,128)S(1)} custom-call(bf16[16,8,640]{2,1,0:T(8,128)(2,1)S(1)} %all_to_all.21.packet_ref.refs_1_, bf16[4,512,4096]{2,1,0:T(8,128)(2,1)S(1)} %bitcast.2), custom_call_target="tpu_custom_call" | custom-call | flops 5000000000 | bytes 19531250 | tf_op jit(solution)/shard_map/half/pallas_call | solution.py:371
  29.7 2.6 %screen.3 = (f32[8,512]{1,0:T(8,128)S(1)}, f32[8,512]{1,0:T(8,128)S(1)}, f32[8,512]{1,0:T(8,128)S(1)}, f32[8,512]{1,0:T(8,128)S(1)}, f32[4,32,512]{2,1,0:T(8,128)S(1)}) custom-call(f32[4,32,512]{2,1,0:T(8,128)S(1)} %half.3.refs_0_, bf16[16,8,640]{2,1,0:T(8,128)(2,1)S(1)} %all_to_all.21.packet_ref.refs_1_, ...), custom_call_target="tpu_custom_call" | custom-call | tf_op jit(solution)/shard_map/screen/pallas_call | solution.py:371
  32.3 0.4 collective-permute-start.1
  32.7 0.8 collective-permute-start.2
  33.5 2.4 %collective-permute-start.3 = (f32[8,512]{1,0:T(8,128)S(1)}, f32[8,512]{1,0:T(8,128)S(1)}, u32[]{:S(2)}, u32[]{:S(2)}) collective-permute-start(f32[8,512]{1,0:T(8,128)S(1)} %get-tuple-element.40), channel_id=1, source_target_pairs={{0,24},{8,16},{16,8},{24,0},{1,25},{9,17},{17,9},{25,1},{2,26},{10... | collective-permute-start | bytes 49160 | tf_op jit(solution)/shard_map/ppermute | solution.py:406
  35.9 0.2 collective-permute-done.1.refs_1_
  36.1 0.3 collective-permute-done.2.refs_2_
  36.4 1.7 %collective-permute-done.3.refs_3_ = f32[8,512]{1,0:T(8,128)S(1)} collective-permute-done((f32[8,512]{1,0:T(8,128)S(1)}, f32[8,512]{1,0:T(8,128)S(1)}, u32[]{:S(2)}, u32[]{:S(2)}) %collective-permute-start.3) | collective-permute-done | bytes 16416 | tf_op jit(solution)/shard_map/ppermute | solution.py:406
  38.1 0.6 field.3.own_ref
  38.8 1.2 collective-permute-done.4.other_ref
  40.0 1.4 %collective-permute-start.7 = (bf16[8,512]{1,0:T(8,128)(2,1)S(1)}, bf16[8,512]{1,0:T(8,128)(2,1)S(1)}, u32[]{:S(2)}, u32[]{:S(2)}) collective-permute-start(bf16[8,512]{1,0:T(8,128)(2,1)S(1)} %pair.3.refs_0_), channel_id=1, source_target_pairs={{0,6},{2,4},{4,2},{6,0},{1,7},{3,5},{5,3},{7,1},{8,14},{10,12},{12... | collective-permute-start | bytes 24584 | tf_op jit(solution)/shard_map/ppermute | solution.py:406
  41.4 0.8 collective-permute-start.6
  42.2 2.2 %collective-permute-start.5 = (bf16[8,512]{1,0:T(8,128)(2,1)S(1)}, bf16[8,512]{1,0:T(8,128)(2,1)S(1)}, u32[]{:S(2)}, u32[]{:S(2)}) collective-permute-start(bf16[8,512]{1,0:T(8,128)(2,1)S(1)} %pair.3.refs_0_), channel_id=1, source_target_pairs={{0,2},{2,0},{4,6},{6,4},{1,3},{3,1},{5,7},{7,5},{8,10},{10,8},{12,... | collective-permute-start | bytes 24584 | tf_op jit(solution)/shard_map/ppermute | solution.py:406
  44.4 1.1 collective-permute-done.7.refs_3_
  45.4 0.6 collective-permute-done.6.refs_2_
  46.0 0.1 collective-permute-done.5.refs_1_
  46.1 0.7 apply.3
  46.8 13.0 %all_to_all.22.packet_ref.refs_1_ = bf16[16,8,640]{2,1,0:T(8,128)(2,1)S(1)} all-to-all(bf16[16,8,640]{2,1,0:T(8,128)(2,1)S(1)} %get-tuple-element.44), channel_id=1, replica_groups=mesh['kpt'=4,'z'=4,'core'=2] {'kpt','z'}, dimensions={0} | all-to-all | bytes 327680 | tf_op jit(solution)/shard_map/all_to_all | solution.py:403
  59.8 2.4 %half.4.refs_0_ = f32[4,32,512]{2,1,0:T(8,128)S(1)} custom-call(bf16[16,8,640]{2,1,0:T(8,128)(2,1)S(1)} %all_to_all.22.packet_ref.refs_1_, bf16[4,512,4096]{2,1,0:T(8,128)(2,1)S(1)} %bitcast.2), custom_call_target="tpu_custom_call" | custom-call | flops 5000000000 | bytes 19531250 | tf_op jit(solution)/shard_map/half/pallas_call | solution.py:371
  62.1 2.6 %screen.4 = (f32[8,512]{1,0:T(8,128)S(1)}, f32[8,512]{1,0:T(8,128)S(1)}, f32[8,512]{1,0:T(8,128)S(1)}, f32[8,512]{1,0:T(8,128)S(1)}, f32[8,128]{1,0:T(8,128)S(1)}, /*index=5*/f32[4,32,512]{2,1,0:T(8,128)S(1)}) custom-call(f32[4,32,512]{2,1,0:T(8,128)S(1)} %half.4.refs_0_, bf16[16,8,640]{2,1,0:T(8,128)(2,1)S(1)} %all_to_all.22.packet_ref.refs_1_, ...), custom_call_target="tpu_custom_call" | custom-call | tf_op jit(solution)/shard_map/screen/pallas_call | solution.py:371
  64.7 1.1 collective-permute-start.9
  65.8 0.8 collective-permute-start.10
  66.6 1.7 %collective-permute-start.11 = (f32[8,512]{1,0:T(8,128)S(1)}, f32[8,512]{1,0:T(8,128)S(1)}, u32[]{:S(2)}, u32[]{:S(2)}) collective-permute-start(f32[8,512]{1,0:T(8,128)S(1)} %get-tuple-element.49), channel_id=1, source_target_pairs={{0,24},{8,16},{16,8},{24,0},{1,25},{9,17},{17,9},{25,1},{2,26},{10... | collective-permute-start | bytes 49160 | tf_op jit(solution)/shard_map/ppermute | solution.py:406
  68.3 0.2 collective-permute-done.9.refs_1_
  68.5 1.0 collective-permute-done.10.refs_2_
  69.5 1.7 %collective-permute-done.11.refs_3_ = f32[8,512]{1,0:T(8,128)S(1)} collective-permute-done((f32[8,512]{1,0:T(8,128)S(1)}, f32[8,512]{1,0:T(8,128)S(1)}, u32[]{:S(2)}, u32[]{:S(2)}) %collective-permute-start.11) | collective-permute-done | bytes 16416 | tf_op jit(solution)/shard_map/ppermute | solution.py:406
  71.2 0.6 field.4.own_ref
  71.9 1.2 collective-permute-done.12.other_ref
  73.1 1.2 %collective-permute-start.15 = (bf16[8,512]{1,0:T(8,128)(2,1)S(1)}, bf16[8,512]{1,0:T(8,128)(2,1)S(1)}, u32[]{:S(2)}, u32[]{:S(2)}) collective-permute-start(bf16[8,512]{1,0:T(8,128)(2,1)S(1)} %pair.4.refs_0_), channel_id=1, source_target_pairs={{0,6},{2,4},{4,2},{6,0},{1,7},{3,5},{5,3},{7,1},{8,14},{10,12},{12... | collective-permute-start | bytes 24584 | tf_op jit(solution)/shard_map/ppermute | solution.py:406
  74.3 1.0 collective-permute-start.14
  75.3 2.1 %collective-permute-start.13 = (bf16[8,512]{1,0:T(8,128)(2,1)S(1)}, bf16[8,512]{1,0:T(8,128)(2,1)S(1)}, u32[]{:S(2)}, u32[]{:S(2)}) collective-permute-start(bf16[8,512]{1,0:T(8,128)(2,1)S(1)} %pair.4.refs_0_), channel_id=1, source_target_pairs={{0,2},{2,0},{4,6},{6,4},{1,3},{3,1},{5,7},{7,5},{8,10},{10,8},{12,... | collective-permute-start | bytes 24584 | tf_op jit(solution)/shard_map/ppermute | solution.py:406
  77.5 1.1 collective-permute-done.15.refs_3_
  78.5 0.3 collective-permute-done.14.refs_2_
  78.8 0.3 collective-permute-done.13.refs_1_
  79.1 0.7 apply.4
  79.8 12.4 %all_to_all.23.packet_ref.refs_1_ = bf16[16,8,640]{2,1,0:T(8,128)(2,1)S(1)} all-to-all(bf16[16,8,640]{2,1,0:T(8,128)(2,1)S(1)} %get-tuple-element.52), channel_id=1, replica_groups=mesh['kpt'=4,'z'=4,'core'=2] {'kpt','z'}, dimensions={0} | all-to-all | bytes 327680 | tf_op jit(solution)/shard_map/all_to_all | solution.py:403
  92.2 2.4 %half.5.refs_0_ = f32[4,32,512]{2,1,0:T(8,128)S(1)} custom-call(bf16[16,8,640]{2,1,0:T(8,128)(2,1)S(1)} %all_to_all.23.packet_ref.refs_1_, bf16[4,512,4096]{2,1,0:T(8,128)(2,1)S(1)} %bitcast.2), custom_call_target="tpu_custom_call" | custom-call | flops 5000000000 | bytes 19531250 | tf_op jit(solution)/shard_map/half/pallas_call | solution.py:371
  94.6 2.6 %screen.5 = (f32[8,512]{1,0:T(8,128)S(1)}, f32[8,512]{1,0:T(8,128)S(1)}, f32[8,512]{1,0:T(8,128)S(1)}, f32[8,512]{1,0:T(8,128)S(1)}, f32[8,128]{1,0:T(8,128)S(1)}) custom-call(f32[4,32,512]{2,1,0:T(8,128)S(1)} %half.5.refs_0_, bf16[16,8,640]{2,1,0:T(8,128)(2,1)S(1)} %all_to_all.23.packet_ref.refs_1_, ...), custom_call_target="tpu_custom_call" | custom-call | tf_op jit(solution)/shard_map/screen/pallas_call | solution.py:371
  97.2 1.1 collective-permute-start.17
  98.2 0.8 collective-permute-start.18
  99.0 1.7 %collective-permute-start.19 = (f32[8,512]{1,0:T(8,128)S(1)}, f32[8,512]{1,0:T(8,128)S(1)}, u32[]{:S(2)}, u32[]{:S(2)}) collective-permute-start(f32[8,512]{1,0:T(8,128)S(1)} %get-tuple-element.57), channel_id=1, source_target_pairs={{0,24},{8,16},{16,8},{24,0},{1,25},{9,17},{17,9},{25,1},{2,26},{10... | collective-permute-start | bytes 49160 | tf_op jit(solution)/shard_map/ppermute | solution.py:406
  100.7 0.2 collective-permute-done.17.refs_1_
  101.0 1.0 collective-permute-done.18.refs_2_
  102.0 1.7 %collective-permute-done.19.refs_3_ = f32[8,512]{1,0:T(8,128)S(1)} collective-permute-done((f32[8,512]{1,0:T(8,128)S(1)}, f32[8,512]{1,0:T(8,128)S(1)}, u32[]{:S(2)}, u32[]{:S(2)}) %collective-permute-start.19) | collective-permute-done | bytes 16416 | tf_op jit(solution)/shard_map/ppermute | solution.py:406
  103.7 0.6 field.5.own_ref
  104.3 1.2 collective-permute-done.20.other_ref
  105.5 1.2 %collective-permute-start.23 = (bf16[8,512]{1,0:T(8,128)(2,1)S(1)}, bf16[8,512]{1,0:T(8,128)(2,1)S(1)}, u32[]{:S(2)}, u32[]{:S(2)}) collective-permute-start(bf16[8,512]{1,0:T(8,128)(2,1)S(1)} %pair.5.refs_0_), channel_id=1, source_target_pairs={{0,6},{2,4},{4,2},{6,0},{1,7},{3,5},{5,3},{7,1},{8,14},{10,12},{12... | collective-permute-start | bytes 24584 | tf_op jit(solution)/shard_map/ppermute | solution.py:406
  106.7 1.0 collective-permute-start.22
  107.8 2.2 %collective-permute-start.21 = (bf16[8,512]{1,0:T(8,128)(2,1)S(1)}, bf16[8,512]{1,0:T(8,128)(2,1)S(1)}, u32[]{:S(2)}, u32[]{:S(2)}) collective-permute-start(bf16[8,512]{1,0:T(8,128)(2,1)S(1)} %pair.5.refs_0_), channel_id=1, source_target_pairs={{0,2},{2,0},{4,6},{6,4},{1,3},{3,1},{5,7},{7,5},{8,10},{10,8},{12,... | collective-permute-start | bytes 24584 | tf_op jit(solution)/shard_map/ppermute | solution.py:406
  109.9 1.1 collective-permute-done.23.refs_3_
  111.0 0.3 collective-permute-done.22.refs_2_
  111.3 0.2 collective-permute-done.21.refs_1_
  111.5 0.5 apply.5
  112.0 2.3 %collective-permute-start.26 = (f32[8,128]{1,0:T(8,128)S(1)}, f32[8,128]{1,0:T(8,128)S(1)}, u32[]{:S(2)}, u32[]{:S(2)}) collective-permute-start(f32[8,128]{1,0:T(8,128)S(1)} %get-tuple-element.61.refs_0_), channel_id=1, source_target_pairs={{0,24},{8,16},{16,8},{24,0},{1,25},{9,17},{17,9},{25,1},{2,26},{10... | collective-permute-start | bytes 12296 | tf_op jit(solution)/shard_map/ppermute | solution.py:406
  114.3 0.6 collective-permute-start.25
  114.9 0.7 collective-permute-start.24
  115.6 1.0 collective-permute-done.26.refs_3_
  116.6 1.3 %collective-permute-done.25.refs_2_ = f32[8,128]{1,0:T(8,128)S(1)} collective-permute-done((f32[8,128]{1,0:T(8,128)S(1)}, f32[8,128]{1,0:T(8,128)S(1)}, u32[]{:S(2)}, u32[]{:S(2)}) %collective-permute-start.25) | collective-permute-done | bytes 4128 | tf_op jit(solution)/shard_map/ppermute | solution.py:406
  117.9 0.6 collective-permute-done.24.refs_1_
  118.5 1.6 %end.1 = (f32[2,4,64]{2,1,0:T(4,128)}, f32[2,4,64]{2,1,0:T(4,128)}, f32[2,3]{1,0:T(2,128)}, f32[2,3]{1,0:T(2,128)}) custom-call(f32[8,128]{1,0:T(8,128)S(1)} %get-tuple-element.61.refs_0_, f32[8,128]{1,0:T(8,128)S(1)} %collective-permute-done.24.refs_1_, f32[8,128]{1,0:T(8,128)S(1)} %collective-permute-done.25.refs_2_, ...), custom_call_target="tpu_custom_call" | custom-call | tf_op jit(solution)/shard_map/end/pallas_call | solution.py:371
  (27 shorter events, 0.1 us)
Async XLA Ops:
  0.6 13.6 %copy-start.1 = (bf16[4,512,512]{2,1,0:T(8,128)(2,1)S(1)}, bf16[4,512,512]{2,1,0:T(8,128)(2,1)}, u32[]{:S(2)}) copy-start(bf16[4,512,512]{2,1,0:T(8,128)(2,1)} %refs_8_.3) | copy-start | bytes 6291460
  0.6 26.7 %slice-start = ((s8[16777216]{0:T(1024)(128)(4,1)}), s8[4194304]{0:T(1024)(128)(4,1)S(1)}, s32[]{:S(2)}) async-start(s8[16777216]{0:T(1024)(128)(4,1)} %bitcast.1), calls=%async_computation.4 | async-start | bytes 8388608
  0.7 26.7 %slice-start.1 = ((s8[16777216]{0:T(1024)(128)(4,1)}), s8[4194304]{0:T(1024)(128)(4,1)S(1)}, s32[]{:S(2)}) async-start(s8[16777216]{0:T(1024)(128)(4,1)} %bitcast.1), calls=%async_computation.5 | async-start | bytes 8388608
  14.3 13.0 %slice-start.2 = ((s8[16777216]{0:T(1024)(128)(4,1)}), s8[4194304]{0:T(1024)(128)(4,1)S(1)}, s32[]{:S(2)}) async-start(s8[16777216]{0:T(1024)(128)(4,1)} %bitcast.1), calls=%async_computation.6 | async-start | bytes 8388608
  14.3 13.0 %slice-start.3 = ((s8[16777216]{0:T(1024)(128)(4,1)}), s8[4194304]{0:T(1024)(128)(4,1)S(1)}, s32[]{:S(2)}) async-start(s8[16777216]{0:T(1024)(128)(4,1)} %bitcast.1), calls=%async_computation.7 | async-start | bytes 8388608
  27.3 2.4 %collective-permute-start = (bf16[16,8,640]{2,1,0:T(8,128)(2,1)S(1)}, bf16[16,8,640]{2,1,0:T(8,128)(2,1)S(1)}, u32[]{:S(2)}, u32[]{:S(2)}) collective-permute-start(bf16[16,8,640]{2,1,0:T(8,128)(2,1)S(1)} %all_to_all.21.packet_ref.refs_1_), channel_id=1, source_target_pairs={{0,1},{1,0},{2,3},{3,2},{4,5},{5,4},{6,7},{7,6},{8,9},{9,8},{10,11... | collective-permute-start | bytes 491528 | tf_op jit(solution)/shard_map/ppermute | solution.py:406
  29.7 8.4 %copy-start = (bf16[4,512,512]{2,1,0:T(8,128)(2,1)S(1)}, bf16[4,512,512]{2,1,0:T(8,128)(2,1)}, u32[]{:S(2)}) copy-start(bf16[4,512,512]{2,1,0:T(8,128)(2,1)} %refs_4_.9) | copy-start | bytes 6291460
  32.3 13.8 %copy-start.2 = (f32[2]{0:T(128)S(1)}, f32[2]{0:T(128)}, u32[]{:S(2)}) copy-start(f32[2]{0:T(128)} %param.11) | copy-start | bytes 28
  32.3 3.8 %collective-permute-start.1 = (f32[8,512]{1,0:T(8,128)S(1)}, f32[8,512]{1,0:T(8,128)S(1)}, u32[]{:S(2)}, u32[]{:S(2)}) collective-permute-start(f32[8,512]{1,0:T(8,128)S(1)} %get-tuple-element.38), channel_id=1, source_target_pairs={{0,8},{8,0},{16,24},{24,16},{1,9},{9,1},{17,25},{25,17},{2,10},{10... | collective-permute-start | bytes 49160 | tf_op jit(solution)/shard_map/ppermute | solution.py:406
  32.7 3.7 %collective-permute-start.2 = (f32[8,512]{1,0:T(8,128)S(1)}, f32[8,512]{1,0:T(8,128)S(1)}, u32[]{:S(2)}, u32[]{:S(2)}) collective-permute-start(f32[8,512]{1,0:T(8,128)S(1)} %get-tuple-element.39), channel_id=1, source_target_pairs={{0,16},{8,24},{16,0},{24,8},{1,17},{9,25},{17,1},{25,9},{2,18},{10... | collective-permute-start | bytes 49160 | tf_op jit(solution)/shard_map/ppermute | solution.py:406
  33.5 4.6 %collective-permute-start.3 = (f32[8,512]{1,0:T(8,128)S(1)}, f32[8,512]{1,0:T(8,128)S(1)}, u32[]{:S(2)}, u32[]{:S(2)}) collective-permute-start(f32[8,512]{1,0:T(8,128)S(1)} %get-tuple-element.40), channel_id=1, source_target_pairs={{0,24},{8,16},{16,8},{24,0},{1,25},{9,17},{17,9},{25,1},{2,26},{10... | collective-permute-start | bytes 49160 | tf_op jit(solution)/shard_map/ppermute | solution.py:406
  38.8 1.2 collective-permute-start.4
  40.0 5.4 %collective-permute-start.7 = (bf16[8,512]{1,0:T(8,128)(2,1)S(1)}, bf16[8,512]{1,0:T(8,128)(2,1)S(1)}, u32[]{:S(2)}, u32[]{:S(2)}) collective-permute-start(bf16[8,512]{1,0:T(8,128)(2,1)S(1)} %pair.3.refs_0_), channel_id=1, source_target_pairs={{0,6},{2,4},{4,2},{6,0},{1,7},{3,5},{5,3},{7,1},{8,14},{10,12},{12... | collective-permute-start | bytes 24584 | tf_op jit(solution)/shard_map/ppermute | solution.py:406
  41.4 4.6 %collective-permute-start.6 = (bf16[8,512]{1,0:T(8,128)(2,1)S(1)}, bf16[8,512]{1,0:T(8,128)(2,1)S(1)}, u32[]{:S(2)}, u32[]{:S(2)}) collective-permute-start(bf16[8,512]{1,0:T(8,128)(2,1)S(1)} %pair.3.refs_0_), channel_id=1, source_target_pairs={{0,4},{2,6},{4,0},{6,2},{1,5},{3,7},{5,1},{7,3},{8,12},{10,14},{12... | collective-permute-start | bytes 24584 | tf_op jit(solution)/shard_map/ppermute | solution.py:406
  42.2 3.9 %collective-permute-start.5 = (bf16[8,512]{1,0:T(8,128)(2,1)S(1)}, bf16[8,512]{1,0:T(8,128)(2,1)S(1)}, u32[]{:S(2)}, u32[]{:S(2)}) collective-permute-start(bf16[8,512]{1,0:T(8,128)(2,1)S(1)} %pair.3.refs_0_), channel_id=1, source_target_pairs={{0,2},{2,0},{4,6},{6,4},{1,3},{3,1},{5,7},{7,5},{8,10},{10,8},{12,... | collective-permute-start | bytes 24584 | tf_op jit(solution)/shard_map/ppermute | solution.py:406
  59.8 2.4 %collective-permute-start.8 = (bf16[16,8,640]{2,1,0:T(8,128)(2,1)S(1)}, bf16[16,8,640]{2,1,0:T(8,128)(2,1)S(1)}, u32[]{:S(2)}, u32[]{:S(2)}) collective-permute-start(bf16[16,8,640]{2,1,0:T(8,128)(2,1)S(1)} %all_to_all.22.packet_ref.refs_1_), channel_id=1, source_target_pairs={{0,1},{1,0},{2,3},{3,2},{4,5},{5,4},{6,7},{7,6},{8,9},{9,8},{10,11... | collective-permute-start | bytes 491528 | tf_op jit(solution)/shard_map/ppermute | solution.py:406
  64.7 3.8 %collective-permute-start.9 = (f32[8,512]{1,0:T(8,128)S(1)}, f32[8,512]{1,0:T(8,128)S(1)}, u32[]{:S(2)}, u32[]{:S(2)}) collective-permute-start(f32[8,512]{1,0:T(8,128)S(1)} %get-tuple-element.47), channel_id=1, source_target_pairs={{0,8},{8,0},{16,24},{24,16},{1,9},{9,1},{17,25},{25,17},{2,10},{10... | collective-permute-start | bytes 49160 | tf_op jit(solution)/shard_map/ppermute | solution.py:406
  65.8 3.7 %collective-permute-start.10 = (f32[8,512]{1,0:T(8,128)S(1)}, f32[8,512]{1,0:T(8,128)S(1)}, u32[]{:S(2)}, u32[]{:S(2)}) collective-permute-start(f32[8,512]{1,0:T(8,128)S(1)} %get-tuple-element.48), channel_id=1, source_target_pairs={{0,16},{8,24},{16,0},{24,8},{1,17},{9,25},{17,1},{25,9},{2,18},{10... | collective-permute-start | bytes 49160 | tf_op jit(solution)/shard_map/ppermute | solution.py:406
  66.6 4.6 %collective-permute-start.11 = (f32[8,512]{1,0:T(8,128)S(1)}, f32[8,512]{1,0:T(8,128)S(1)}, u32[]{:S(2)}, u32[]{:S(2)}) collective-permute-start(f32[8,512]{1,0:T(8,128)S(1)} %get-tuple-element.49), channel_id=1, source_target_pairs={{0,24},{8,16},{16,8},{24,0},{1,25},{9,17},{17,9},{25,1},{2,26},{10... | collective-permute-start | bytes 49160 | tf_op jit(solution)/shard_map/ppermute | solution.py:406
  71.9 1.2 %collective-permute-start.12 = (f32[8,512]{1,0:T(8,128)S(1)}, f32[8,512]{1,0:T(8,128)S(1)}, u32[]{:S(2)}, u32[]{:S(2)}) collective-permute-start(f32[8,512]{1,0:T(8,128)S(1)} %field.4.own_ref), channel_id=1, source_target_pairs={{0,1},{1,0},{2,3},{3,2},{4,5},{5,4},{6,7},{7,6},{8,9},{9,8},{10,11... | collective-permute-start | bytes 49160 | tf_op jit(solution)/shard_map/ppermute | solution.py:406
  73.1 5.4 %collective-permute-start.15 = (bf16[8,512]{1,0:T(8,128)(2,1)S(1)}, bf16[8,512]{1,0:T(8,128)(2,1)S(1)}, u32[]{:S(2)}, u32[]{:S(2)}) collective-permute-start(bf16[8,512]{1,0:T(8,128)(2,1)S(1)} %pair.4.refs_0_), channel_id=1, source_target_pairs={{0,6},{2,4},{4,2},{6,0},{1,7},{3,5},{5,3},{7,1},{8,14},{10,12},{12... | collective-permute-start | bytes 24584 | tf_op jit(solution)/shard_map/ppermute | solution.py:406
  74.3 4.5 %collective-permute-start.14 = (bf16[8,512]{1,0:T(8,128)(2,1)S(1)}, bf16[8,512]{1,0:T(8,128)(2,1)S(1)}, u32[]{:S(2)}, u32[]{:S(2)}) collective-permute-start(bf16[8,512]{1,0:T(8,128)(2,1)S(1)} %pair.4.refs_0_), channel_id=1, source_target_pairs={{0,4},{2,6},{4,0},{6,2},{1,5},{3,7},{5,1},{7,3},{8,12},{10,14},{12... | collective-permute-start | bytes 24584 | tf_op jit(solution)/shard_map/ppermute | solution.py:406
  75.3 3.8 %collective-permute-start.13 = (bf16[8,512]{1,0:T(8,128)(2,1)S(1)}, bf16[8,512]{1,0:T(8,128)(2,1)S(1)}, u32[]{:S(2)}, u32[]{:S(2)}) collective-permute-start(bf16[8,512]{1,0:T(8,128)(2,1)S(1)} %pair.4.refs_0_), channel_id=1, source_target_pairs={{0,2},{2,0},{4,6},{6,4},{1,3},{3,1},{5,7},{7,5},{8,10},{10,8},{12,... | collective-permute-start | bytes 24584 | tf_op jit(solution)/shard_map/ppermute | solution.py:406
  92.2 2.4 %collective-permute-start.16 = (bf16[16,8,640]{2,1,0:T(8,128)(2,1)S(1)}, bf16[16,8,640]{2,1,0:T(8,128)(2,1)S(1)}, u32[]{:S(2)}, u32[]{:S(2)}) collective-permute-start(bf16[16,8,640]{2,1,0:T(8,128)(2,1)S(1)} %all_to_all.23.packet_ref.refs_1_), channel_id=1, source_target_pairs={{0,1},{1,0},{2,3},{3,2},{4,5},{5,4},{6,7},{7,6},{8,9},{9,8},{10,11... | collective-permute-start | bytes 491528 | tf_op jit(solution)/shard_map/ppermute | solution.py:406
  97.2 3.8 %collective-permute-start.17 = (f32[8,512]{1,0:T(8,128)S(1)}, f32[8,512]{1,0:T(8,128)S(1)}, u32[]{:S(2)}, u32[]{:S(2)}) collective-permute-start(f32[8,512]{1,0:T(8,128)S(1)} %get-tuple-element.55), channel_id=1, source_target_pairs={{0,8},{8,0},{16,24},{24,16},{1,9},{9,1},{17,25},{25,17},{2,10},{10... | collective-permute-start | bytes 49160 | tf_op jit(solution)/shard_map/ppermute | solution.py:406
  98.2 3.7 %collective-permute-start.18 = (f32[8,512]{1,0:T(8,128)S(1)}, f32[8,512]{1,0:T(8,128)S(1)}, u32[]{:S(2)}, u32[]{:S(2)}) collective-permute-start(f32[8,512]{1,0:T(8,128)S(1)} %get-tuple-element.56), channel_id=1, source_target_pairs={{0,16},{8,24},{16,0},{24,8},{1,17},{9,25},{17,1},{25,9},{2,18},{10... | collective-permute-start | bytes 49160 | tf_op jit(solution)/shard_map/ppermute | solution.py:406
  99.0 4.6 %collective-permute-start.19 = (f32[8,512]{1,0:T(8,128)S(1)}, f32[8,512]{1,0:T(8,128)S(1)}, u32[]{:S(2)}, u32[]{:S(2)}) collective-permute-start(f32[8,512]{1,0:T(8,128)S(1)} %get-tuple-element.57), channel_id=1, source_target_pairs={{0,24},{8,16},{16,8},{24,0},{1,25},{9,17},{17,9},{25,1},{2,26},{10... | collective-permute-start | bytes 49160 | tf_op jit(solution)/shard_map/ppermute | solution.py:406
  104.3 1.2 %collective-permute-start.20 = (f32[8,512]{1,0:T(8,128)S(1)}, f32[8,512]{1,0:T(8,128)S(1)}, u32[]{:S(2)}, u32[]{:S(2)}) collective-permute-start(f32[8,512]{1,0:T(8,128)S(1)} %field.5.own_ref), channel_id=1, source_target_pairs={{0,1},{1,0},{2,3},{3,2},{4,5},{5,4},{6,7},{7,6},{8,9},{9,8},{10,11... | collective-permute-start | bytes 49160 | tf_op jit(solution)/shard_map/ppermute | solution.py:406
  105.5 5.4 %collective-permute-start.23 = (bf16[8,512]{1,0:T(8,128)(2,1)S(1)}, bf16[8,512]{1,0:T(8,128)(2,1)S(1)}, u32[]{:S(2)}, u32[]{:S(2)}) collective-permute-start(bf16[8,512]{1,0:T(8,128)(2,1)S(1)} %pair.5.refs_0_), channel_id=1, source_target_pairs={{0,6},{2,4},{4,2},{6,0},{1,7},{3,5},{5,3},{7,1},{8,14},{10,12},{12... | collective-permute-start | bytes 24584 | tf_op jit(solution)/shard_map/ppermute | solution.py:406
  106.7 4.5 %collective-permute-start.22 = (bf16[8,512]{1,0:T(8,128)(2,1)S(1)}, bf16[8,512]{1,0:T(8,128)(2,1)S(1)}, u32[]{:S(2)}, u32[]{:S(2)}) collective-permute-start(bf16[8,512]{1,0:T(8,128)(2,1)S(1)} %pair.5.refs_0_), channel_id=1, source_target_pairs={{0,4},{2,6},{4,0},{6,2},{1,5},{3,7},{5,1},{7,3},{8,12},{10,14},{12... | collective-permute-start | bytes 24584 | tf_op jit(solution)/shard_map/ppermute | solution.py:406
  107.8 3.8 %collective-permute-start.21 = (bf16[8,512]{1,0:T(8,128)(2,1)S(1)}, bf16[8,512]{1,0:T(8,128)(2,1)S(1)}, u32[]{:S(2)}, u32[]{:S(2)}) collective-permute-start(bf16[8,512]{1,0:T(8,128)(2,1)S(1)} %pair.5.refs_0_), channel_id=1, source_target_pairs={{0,2},{2,0},{4,6},{6,4},{1,3},{3,1},{5,7},{7,5},{8,10},{10,8},{12,... | collective-permute-start | bytes 24584 | tf_op jit(solution)/shard_map/ppermute | solution.py:406
  112.0 4.6 %collective-permute-start.26 = (f32[8,128]{1,0:T(8,128)S(1)}, f32[8,128]{1,0:T(8,128)S(1)}, u32[]{:S(2)}, u32[]{:S(2)}) collective-permute-start(f32[8,128]{1,0:T(8,128)S(1)} %get-tuple-element.61.refs_0_), channel_id=1, source_target_pairs={{0,24},{8,16},{16,8},{24,0},{1,25},{9,17},{17,9},{25,1},{2,26},{10... | collective-permute-start | bytes 12296 | tf_op jit(solution)/shard_map/ppermute | solution.py:406
  114.3 3.6 %collective-permute-start.25 = (f32[8,128]{1,0:T(8,128)S(1)}, f32[8,128]{1,0:T(8,128)S(1)}, u32[]{:S(2)}, u32[]{:S(2)}) collective-permute-start(f32[8,128]{1,0:T(8,128)S(1)} %get-tuple-element.61.refs_0_), channel_id=1, source_target_pairs={{0,16},{8,24},{16,0},{24,8},{1,17},{9,25},{17,1},{25,9},{2,18},{10... | collective-permute-start | bytes 12296 | tf_op jit(solution)/shard_map/ppermute | solution.py:406
  114.9 3.6 %collective-permute-start.24 = (f32[8,128]{1,0:T(8,128)S(1)}, f32[8,128]{1,0:T(8,128)S(1)}, u32[]{:S(2)}, u32[]{:S(2)}) collective-permute-start(f32[8,128]{1,0:T(8,128)S(1)} %get-tuple-element.61.refs_0_), channel_id=1, source_target_pairs={{0,8},{8,0},{16,24},{24,16},{1,9},{9,1},{17,25},{25,17},{2,10},{10... | collective-permute-start | bytes 12296 | tf_op jit(solution)/shard_map/ppermute | solution.py:406

commit v5 on v4

--- a/solution.py
+++ b/solution.py
@@ -9,7 +9,7 @@
 
 STEPS = 3
 EPSILON = 1e-06
-COVER = 5_000_000_000
+COVER = 10_000_000_000
 LANES = 128
 CORES = 2
 BF, F32 = jnp.bfloat16, jnp.float32
@@ -52,20 +52,28 @@
 
 
 def begin_kernel(s, *refs):
-    sources, held, sems = refs[:4], refs[6:10], refs[10]
-    pick_ref, out_ref = refs[4:6]
+    sources, out_ref, held, sems = refs[:3], refs[3], refs[4:7], refs[7]
     copy_all(sources, held, sems)
-    mi_ref, current_ref, previous_ref, energies_ref = held
-    rows = s.rows
+    current_ref, previous_ref, energies_ref = held
     both = []
     for ref in (current_ref, previous_ref):
         both.append(jnp.concatenate([ref[n] for n in range(s.chains)], axis=0))
     levels = jnp.concatenate([energies_ref[...]] * s.chains, axis=0)
-    piece = jnp.concatenate(
+    out_ref[...] = jnp.concatenate(
         [jnp.concatenate(both, axis=1), jnp.concatenate([levels] * 2, axis=1)], axis=0
     )
-    for b in range(s.parts):
-        out_ref[b] = piece
+
+
+def stack_kernel(s, own_ref, other_ref, out_ref):
+    core = lax.axis_index("core")
+    height = own_ref.shape[0]
+    for c in range(CORES):
+        value = jnp.where(core == c, own_ref[...], other_ref[...])
+        out_ref[c * height : (c + 1) * height, :] = value
+
+
+def pick_kernel(s, mi_ref, pick_ref):
+    rows = s.rows
     mi = mi_ref[...].astype(F32).astype(BF)
     total, nk = s.groups * rows, mi.shape[0]
 
@@ -88,17 +96,18 @@
             pick_ref[:, at : at + total] = one
 
 
-def unpack_kernel(s, gathered_ref, right_ref, packet_ref, vector_ref, earlier_ref, levels_ref):
+def unpack_kernel(s, *refs):
+    right_ref, _, packet_ref, vector_ref, earlier_ref, levels_ref = refs[s.chips :]
     rows = s.rows
-    width = gathered_ref.shape[2] // 2
+    width = refs[0].shape[1] // 2
+    pieces = in_order(lax.axis_index("z"), [ref[...] for ref in refs[: s.chips]])
     for ref, row, lane in ((vector_ref, 0, 0), (earlier_ref, 0, width), (levels_ref, rows, 0)):
-        ref[...] = jnp.concatenate(
-            [
-                gathered_ref[b, row : row + rows, lane : lane + width]
-                for b in range(s.parts)
-            ],
-            axis=1,
-        )
+        blocks = []
+        for piece in pieces:
+            for c in range(CORES):
+                at = 2 * rows * c + row
+                blocks.append(piece[at : at + rows, lane : lane + width])
+        ref[...] = jnp.concatenate(blocks, axis=1)
     density = project(s, (vector_ref[...].astype(BF),), right_ref)
     send(s, density, jnp.zeros((rows, LANES), F32), packet_ref)
 
@@ -228,30 +237,45 @@
     return ordered
 
 
+def own_kernel(s, work_ref, vector_ref, *refs):
+    scalar_refs = refs[:-6]
+    own_work_ref, own_vector_ref, terms_ref, prior_ref, prior, sem = refs[-6:]
+    width = own_work_ref.shape[1]
+    me = lax.axis_index("z") * CORES + lax.axis_index("core")
+    for source, target in ((work_ref, own_work_ref), (vector_ref, own_vector_ref)):
+        own = source[:, :width]
+        for b in range(1, s.parts):
+            own = jnp.where(me == b, source[:, b * width : (b + 1) * width], own)
+        target[...] = own
+    for n in range(s.chains):
+        prior[n] = own_vector_ref[n * s.kpoints : (n + 1) * s.kpoints, :]
+    copy = pltpu.make_async_copy(prior, prior_ref, sem.at[0])
+    copy.start()
+    lane = iota((s.rows, LANES), 1)
+    terms = jnp.zeros((s.rows, LANES), F32)
+    for at, ref in enumerate(scalar_refs):
+        terms = jnp.where(lane == at, ref[:, 0:1], terms)
+        terms = jnp.where(lane == STEPS + at, ref[:, 1:2], terms)
+    terms_ref[...] = terms
+    copy.wait()
+
+
 def end_kernel(s, *refs):
     sums, refs = [ref[...] for ref in refs[: s.groups]], refs[s.groups :]
-    work_ref, vector_ref = refs[:2]
-    scalar_refs, targets, held, sems = refs[2:-9], refs[-9:-5], refs[-5:-1], refs[-1]
-    last_ref, prior_ref, alphas_ref, betas_ref = held
+    work_ref, vector_ref, terms_ref = refs[:3]
+    targets, held, sems = refs[3:6], refs[6:9], refs[9]
+    last_ref, alphas_ref, betas_ref = held
     alpha, beta, offsets = read_sums(s, in_order(lax.axis_index("kpt"), sums))
     offset = own_offset(s, offsets)
-    vector = vector_ref[...]
-    last = (work_ref[...] + offset * vector) / beta
-    width = last_ref.shape[2]
-    me = lax.axis_index("z") * CORES + lax.axis_index("core")
+    last = (work_ref[...] + offset * vector_ref[...]) / beta
+    lane = iota((s.rows, LANES), 1)
+    terms = jnp.where(lane == STEPS - 1, alpha, terms_ref[...])
+    terms = jnp.where(lane == 2 * STEPS - 1, beta, terms)
     k = s.kpoints
-    for value, ref in ((last, last_ref), (vector, prior_ref)):
-        own = jnp.zeros((s.rows, width), F32)
-        for b in range(s.parts):
-            own = jnp.where(me == b, value[:, b * width : (b + 1) * width], own)
-        for n in range(s.chains):
-            ref[n] = own[n * k : (n + 1) * k]
-    alphas = [ref[:, 0:1] for ref in scalar_refs] + [alpha]
-    betas = [ref[:, 1:2] for ref in scalar_refs] + [beta]
     for n in range(s.chains):
-        at = slice(n * k, n * k + 1)
-        alphas_ref[n : n + 1, :] = jnp.concatenate([x[at] for x in alphas], axis=1)
-        betas_ref[n : n + 1, :] = jnp.concatenate([x[at] for x in betas], axis=1)
+        last_ref[n] = last[n * k : (n + 1) * k]
+        alphas_ref[n : n + 1, :] = terms[n * k : n * k + 1, :STEPS]
+        betas_ref[n : n + 1, :] = terms[n * k : n * k + 1, STEPS : 2 * STEPS]
     copy_all(held, targets, sems)
 
 
@@ -397,7 +421,6 @@
     total = groups * s.rows
     state = ((s.rows, bands), F32)
     packet = ((groups * parts // CORES, s.rows, width + LANES), BF)
-    chip = ("z", "core")
 
     def exchange(x, axes):
         return lax.all_to_all(x, axes, 0, 0, tiled=True)
@@ -413,25 +436,35 @@
     screened = pltpu.with_memory_space_constraint(screened, pltpu.VMEM)
     inputs = tuple(
         pltpu.with_memory_space_constraint(x, pltpu.HBM)
-        for x in (momentum_index, current, previous, energies)
-    )
-    pick, start = call(
+        for x in (current, previous, energies)
+    )
+    piece = ((2 * s.rows, 2 * band_block), F32)
+    (start,) = call(
         functools.partial(begin_kernel, s),
         inputs,
-        [
-            ((total, s.transfers * 3 * total), BF),
-            ((parts, 2 * s.rows, 2 * band_block), F32),
-        ],
+        [piece],
         "begin",
         specs=[HBM] * len(inputs),
         scratch=[pltpu.VMEM(x.shape, x.dtype) for x in inputs]
         + [pltpu.SemaphoreType.DMA((len(inputs),))],
         cost=COVER,
     )
-    start = exchange(start, chip)
+    (start,) = call(
+        functools.partial(stack_kernel, s),
+        (start, across(start, "core", CORES, 1)),
+        [((CORES * 2 * s.rows, 2 * band_block), F32)],
+        "stack",
+    )
+    (pick,) = call(
+        functools.partial(pick_kernel, s),
+        (momentum_index,),
+        [((total, s.transfers * 3 * total), BF)],
+        "pick",
+    )
+    start = swap([start] * s.chips, "z")
     sent, vector, earlier, levels = call(
         functools.partial(unpack_kernel, s),
-        (start, pair_right),
+        (*start, pair_right, pick),
         [packet, state, state, state],
         "unpack",
         cost=COVER,
@@ -463,7 +496,7 @@
             before = results[-1]
         (direct,) = call(
             functools.partial(field_kernel, s, first),
-            (*swap(results[:groups]), pair_left),
+            (*swap(results[:groups])[::-1], pair_left),
             [state],
             "field",
         )
@@ -498,17 +531,25 @@
     sums = swap([sent] * groups)
     own = (current.shape, F32)
     terms = ((s.chains, STEPS), F32)
-    return tuple(
-        call(
-            functools.partial(end_kernel, s),
-            (*sums, work, vector, *scalars),
-            [own, own, terms, terms],
-            "end",
-            out_specs=[HBM] * 4,
-            scratch=[pltpu.VMEM(*x) for x in (own, own, terms, terms)]
-            + [pltpu.SemaphoreType.DMA((4,))],
-        )
-    )
+    block = ((s.rows, band_block), F32)
+    own_work, own_vector, known, prior = call(
+        functools.partial(own_kernel, s),
+        (work, vector, *scalars),
+        [block, block, ((s.rows, LANES), F32), own],
+        "own",
+        out_specs=[VMEM] * 3 + [HBM],
+        scratch=[pltpu.VMEM(*own), pltpu.SemaphoreType.DMA((1,))],
+    )
+    last, alphas, betas = call(
+        functools.partial(end_kernel, s),
+        (*sums, own_work, own_vector, known),
+        [own, terms, terms],
+        "end",
+        out_specs=[HBM] * 3,
+        scratch=[pltpu.VMEM(*x) for x in (own, terms, terms)]
+        + [pltpu.SemaphoreType.DMA((3,))],
+    )
+    return last, prior, alphas, betas
 
 
 def solution(mesh):

time: 121 us -> 118 us (0.975)
  blocking collectives: 50.3 us -> 37.2 us
  starting transfers between devices: 27.4 us -> 33.5 us
  waiting for transfers between devices: 19.6 us -> 23.1 us
    all_to_all x4 -> x3, blocking collectives: 50.3 us -> 37.2 us  [exchange(): return lax.all_to_all(x, axes, 0, 0, tiled=True)]
    ppermute x27 -> x31, starting transfers between devices: 27.4 us -> 33.5 us  [across(): return lax.ppermute(x, axis, [(i, i ^ distance) for i in range(size)])]
    ppermute x27 -> x31, waiting for transfers between devices: 19.6 us -> 23.1 us  [across(): return lax.ppermute(x, axis, [(i, i ^ distance) for i in range(size)])]
    pallas_call x18 -> x21, Pallas kernels: 22 us -> 22.6 us  [call(): pl.pallas_call(body, out_shape=[jax.ShapeDtypeStruct(shape, dtype) for sh...]
  transfers between devices with their start and end apart: 27 -> 31, of which waited for: 24 -> 25; matrix products, arithmetic and copies ran while one was open for 0% -> 0% of each run, Pallas kernels for 6% -> 7%
where the time goes in v5:
time: 118 us; the launch traced here: 117 us
  blocking collectives  37.2 us (32%)
  starting transfers between devices  33.5 us (28%)
  waiting for transfers between devices  23.1 us (20%)
  Pallas kernels  22.6 us (19%)
    all_to_all x3, blocking collectives, exchange(): return lax.all_to_all(x, axes, 0, 0, tiled=True)  37.2 us
    ppermute x31, starting transfers between devices, across(): return lax.ppermute(x, axis, [(i, i ^ distance) for i in range(size)])  33.5 us
    ppermute x31, waiting for transfers between devices, across(): return lax.ppermute(x, axis, [(i, i ^ distance) for i in range(size)])  23.1 us
    pallas_call x21, Pallas kernels, call(): pl.pallas_call(body, out_shape=[jax.ShapeDtypeStruct(shape, dtype) for sh...  22.6 us
  transfers between devices with their start and end apart: 31, of which 25 were waited for; matrix products, arithmetic and copies ran while one was open for 0% of the time, Pallas kernels for 7%

profile of v5, /device:TPU:0, one launch (start us, length us, event | category | flops | bytes accessed | tf_op | source)
XLA Modules:
  0.0 117.4 jit_solution(12768373627215107046)
XLA Ops:
  0.7 1.0 begin.1.own_ref
  1.6 0.6 collective-permute-start
  2.2 0.8 collective-permute-done.other_ref
  3.0 4.9 %collective-permute-start.3 = (f32[32,128]{1,0:T(8,128)S(1)}, f32[32,128]{1,0:T(8,128)S(1)}, u32[]{:S(2)}, u32[]{:S(2)}) collective-permute-start(f32[32,128]{1,0:T(8,128)S(1)} %stack.1.refs_0_), channel_id=1, source_target_pairs={{0,6},{2,4},{4,2},{6,0},{1,7},{3,5},{5,3},{7,1},{8,14},{10,12},{12... | collective-permute-start | bytes 49160 | tf_op jit(solution)/shard_map/ppermute | solution.py:429
  7.9 0.6 collective-permute-start.1
  8.6 0.3 pick.1.refs_5_.refs_4_
  9.0 0.7 collective-permute-done.3.refs_3_
  9.7 2.9 %collective-permute-done.2.refs_2_ = f32[32,128]{1,0:T(8,128)S(1)} collective-permute-done((f32[32,128]{1,0:T(8,128)S(1)}, f32[32,128]{1,0:T(8,128)S(1)}, u32[]{:S(2)}, u32[]{:S(2)}) %collective-permute-start.2) | collective-permute-done | bytes 16416 | tf_op jit(solution)/shard_map/ppermute | solution.py:429
  12.6 0.4 unpack.1
  13.0 12.9 %all_to_all.15.packet_ref.refs_1_ = bf16[16,8,640]{2,1,0:T(8,128)(2,1)S(1)} all-to-all(bf16[16,8,640]{2,1,0:T(8,128)(2,1)S(1)} %get-tuple-element.39), channel_id=1, replica_groups=mesh['kpt'=4,'z'=4,'core'=2] {'kpt','z'}, dimensions={0} | all-to-all | bytes 327680 | tf_op jit(solution)/shard_map/all_to_all | solution.py:426
  26.0 2.4 %half.3.refs_0_ = f32[4,32,512]{2,1,0:T(8,128)S(1)} custom-call(bf16[16,8,640]{2,1,0:T(8,128)(2,1)S(1)} %all_to_all.15.packet_ref.refs_1_, bf16[4,512,4096]{2,1,0:T(8,128)(2,1)S(1)} %bitcast.2), custom_call_target="tpu_custom_call" | custom-call | flops 10000000000 | bytes 39062500 | tf_op jit(solution)/shard_map/half/pallas_call | solution.py:395
  28.4 2.6 %screen.3 = (f32[8,512]{1,0:T(8,128)S(1)}, f32[8,512]{1,0:T(8,128)S(1)}, f32[8,512]{1,0:T(8,128)S(1)}, f32[8,512]{1,0:T(8,128)S(1)}, f32[4,32,512]{2,1,0:T(8,128)S(1)}) custom-call(f32[4,32,512]{2,1,0:T(8,128)S(1)} %half.3.refs_0_, bf16[16,8,640]{2,1,0:T(8,128)(2,1)S(1)} %all_to_all.15.packet_ref.refs_1_, ...), custom_call_target="tpu_custom_call" | custom-call | tf_op jit(solution)/shard_map/screen/pallas_call | solution.py:395
  31.0 1.3 %collective-permute-start.5 = (f32[8,512]{1,0:T(8,128)S(1)}, f32[8,512]{1,0:T(8,128)S(1)}, u32[]{:S(2)}, u32[]{:S(2)}) collective-permute-start(f32[8,512]{1,0:T(8,128)S(1)} %get-tuple-element.40), channel_id=1, source_target_pairs={{0,24},{8,16},{16,8},{24,0},{1,25},{9,17},{17,9},{25,1},{2,26},{10... | collective-permute-start | bytes 49160 | tf_op jit(solution)/shard_map/ppermute | solution.py:429
  32.3 1.2 %collective-permute-start.6 = (f32[8,512]{1,0:T(8,128)S(1)}, f32[8,512]{1,0:T(8,128)S(1)}, u32[]{:S(2)}, u32[]{:S(2)}) collective-permute-start(f32[8,512]{1,0:T(8,128)S(1)} %get-tuple-element.41), channel_id=1, source_target_pairs={{0,16},{8,24},{16,0},{24,8},{1,17},{9,25},{17,1},{25,9},{2,18},{10... | collective-permute-start | bytes 49160 | tf_op jit(solution)/shard_map/ppermute | solution.py:429
  33.5 1.0 collective-permute-start.7
  34.5 1.1 collective-permute-done.5.refs_0_
  36.0 1.2 %collective-permute-done.7.refs_2_ = f32[8,512]{1,0:T(8,128)S(1)} collective-permute-done((f32[8,512]{1,0:T(8,128)S(1)}, f32[8,512]{1,0:T(8,128)S(1)}, u32[]{:S(2)}, u32[]{:S(2)}) %collective-permute-start.7) | collective-permute-done | bytes 16416 | tf_op jit(solution)/shard_map/ppermute | solution.py:429
  37.2 0.6 field.3.own_ref
  37.9 1.2 %collective-permute-done.8.other_ref = f32[8,512]{1,0:T(8,128)S(1)} collective-permute-done((f32[8,512]{1,0:T(8,128)S(1)}, f32[8,512]{1,0:T(8,128)S(1)}, u32[]{:S(2)}, u32[]{:S(2)}) %collective-permute-start.8) | collective-permute-done | bytes 16416 | tf_op jit(solution)/shard_map/ppermute | solution.py:429
  39.1 0.9 collective-permute-start.11
  40.0 1.0 collective-permute-start.10
  41.0 2.5 %collective-permute-start.9 = (bf16[8,512]{1,0:T(8,128)(2,1)S(1)}, bf16[8,512]{1,0:T(8,128)(2,1)S(1)}, u32[]{:S(2)}, u32[]{:S(2)}) collective-permute-start(bf16[8,512]{1,0:T(8,128)(2,1)S(1)} %pair.3.refs_0_), channel_id=1, source_target_pairs={{0,2},{2,0},{4,6},{6,4},{1,3},{3,1},{5,7},{7,5},{8,10},{10,8},{12,... | collective-permute-start | bytes 24584 | tf_op jit(solution)/shard_map/ppermute | solution.py:429
  43.5 1.1 collective-permute-done.11.refs_3_
  44.7 0.4 collective-permute-done.9.refs_1_
  45.1 0.7 apply.3
  45.8 12.2 %all_to_all.16.packet_ref.refs_1_ = bf16[16,8,640]{2,1,0:T(8,128)(2,1)S(1)} all-to-all(bf16[16,8,640]{2,1,0:T(8,128)(2,1)S(1)} %get-tuple-element.47), channel_id=1, replica_groups=mesh['kpt'=4,'z'=4,'core'=2] {'kpt','z'}, dimensions={0} | all-to-all | bytes 327680 | tf_op jit(solution)/shard_map/all_to_all | solution.py:426
  58.0 2.4 %half.4.refs_0_ = f32[4,32,512]{2,1,0:T(8,128)S(1)} custom-call(bf16[16,8,640]{2,1,0:T(8,128)(2,1)S(1)} %all_to_all.16.packet_ref.refs_1_, bf16[4,512,4096]{2,1,0:T(8,128)(2,1)S(1)} %bitcast.2), custom_call_target="tpu_custom_call" | custom-call | flops 10000000000 | bytes 39062500 | tf_op jit(solution)/shard_map/half/pallas_call | solution.py:395
  60.4 2.6 %screen.4 = (f32[8,512]{1,0:T(8,128)S(1)}, f32[8,512]{1,0:T(8,128)S(1)}, f32[8,512]{1,0:T(8,128)S(1)}, f32[8,512]{1,0:T(8,128)S(1)}, f32[8,128]{1,0:T(8,128)S(1)}, /*index=5*/f32[4,32,512]{2,1,0:T(8,128)S(1)}) custom-call(f32[4,32,512]{2,1,0:T(8,128)S(1)} %half.4.refs_0_, bf16[16,8,640]{2,1,0:T(8,128)(2,1)S(1)} %all_to_all.16.packet_ref.refs_1_, ...), custom_call_target="tpu_custom_call" | custom-call | tf_op jit(solution)/shard_map/screen/pallas_call | solution.py:395
  62.9 1.3 %collective-permute-start.13 = (f32[8,512]{1,0:T(8,128)S(1)}, f32[8,512]{1,0:T(8,128)S(1)}, u32[]{:S(2)}, u32[]{:S(2)}) collective-permute-start(f32[8,512]{1,0:T(8,128)S(1)} %get-tuple-element.49), channel_id=1, source_target_pairs={{0,24},{8,16},{16,8},{24,0},{1,25},{9,17},{17,9},{25,1},{2,26},{10... | collective-permute-start | bytes 49160 | tf_op jit(solution)/shard_map/ppermute | solution.py:429
  64.2 1.2 %collective-permute-start.14 = (f32[8,512]{1,0:T(8,128)S(1)}, f32[8,512]{1,0:T(8,128)S(1)}, u32[]{:S(2)}, u32[]{:S(2)}) collective-permute-start(f32[8,512]{1,0:T(8,128)S(1)} %get-tuple-element.50), channel_id=1, source_target_pairs={{0,16},{8,24},{16,0},{24,8},{1,17},{9,25},{17,1},{25,9},{2,18},{10... | collective-permute-start | bytes 49160 | tf_op jit(solution)/shard_map/ppermute | solution.py:429
  65.5 1.0 collective-permute-start.15
  66.5 1.1 collective-permute-done.13.refs_0_
  68.0 1.2 %collective-permute-done.15.refs_2_ = f32[8,512]{1,0:T(8,128)S(1)} collective-permute-done((f32[8,512]{1,0:T(8,128)S(1)}, f32[8,512]{1,0:T(8,128)S(1)}, u32[]{:S(2)}, u32[]{:S(2)}) %collective-permute-start.15) | collective-permute-done | bytes 16416 | tf_op jit(solution)/shard_map/ppermute | solution.py:429
  69.2 0.6 field.4.own_ref
  69.9 1.2 %collective-permute-done.16.other_ref = f32[8,512]{1,0:T(8,128)S(1)} collective-permute-done((f32[8,512]{1,0:T(8,128)S(1)}, f32[8,512]{1,0:T(8,128)S(1)}, u32[]{:S(2)}, u32[]{:S(2)}) %collective-permute-start.16) | collective-permute-done | bytes 16416 | tf_op jit(solution)/shard_map/ppermute | solution.py:429
  71.1 0.9 collective-permute-start.19
  72.0 1.0 collective-permute-start.18
  73.0 2.5 %collective-permute-start.17 = (bf16[8,512]{1,0:T(8,128)(2,1)S(1)}, bf16[8,512]{1,0:T(8,128)(2,1)S(1)}, u32[]{:S(2)}, u32[]{:S(2)}) collective-permute-start(bf16[8,512]{1,0:T(8,128)(2,1)S(1)} %pair.4.refs_0_), channel_id=1, source_target_pairs={{0,2},{2,0},{4,6},{6,4},{1,3},{3,1},{5,7},{7,5},{8,10},{10,8},{12,... | collective-permute-start | bytes 24584 | tf_op jit(solution)/shard_map/ppermute | solution.py:429
  75.5 1.1 collective-permute-done.19.refs_3_
  76.6 0.5 collective-permute-done.17.refs_1_
  77.1 0.7 apply.4
  77.8 12.1 %all_to_all.17.packet_ref.refs_1_ = bf16[16,8,640]{2,1,0:T(8,128)(2,1)S(1)} all-to-all(bf16[16,8,640]{2,1,0:T(8,128)(2,1)S(1)} %get-tuple-element.55), channel_id=1, replica_groups=mesh['kpt'=4,'z'=4,'core'=2] {'kpt','z'}, dimensions={0} | all-to-all | bytes 327680 | tf_op jit(solution)/shard_map/all_to_all | solution.py:426
  89.9 2.4 %half.5.refs_0_ = f32[4,32,512]{2,1,0:T(8,128)S(1)} custom-call(bf16[16,8,640]{2,1,0:T(8,128)(2,1)S(1)} %all_to_all.17.packet_ref.refs_1_, bf16[4,512,4096]{2,1,0:T(8,128)(2,1)S(1)} %bitcast.2), custom_call_target="tpu_custom_call" | custom-call | flops 10000000000 | bytes 39062500 | tf_op jit(solution)/shard_map/half/pallas_call | solution.py:395
  92.3 2.6 %screen.5 = (f32[8,512]{1,0:T(8,128)S(1)}, f32[8,512]{1,0:T(8,128)S(1)}, f32[8,512]{1,0:T(8,128)S(1)}, f32[8,512]{1,0:T(8,128)S(1)}, f32[8,128]{1,0:T(8,128)S(1)}) custom-call(f32[4,32,512]{2,1,0:T(8,128)S(1)} %half.5.refs_0_, bf16[16,8,640]{2,1,0:T(8,128)(2,1)S(1)} %all_to_all.17.packet_ref.refs_1_, ...), custom_call_target="tpu_custom_call" | custom-call | tf_op jit(solution)/shard_map/screen/pallas_call | solution.py:395
  94.8 1.3 %collective-permute-start.21 = (f32[8,512]{1,0:T(8,128)S(1)}, f32[8,512]{1,0:T(8,128)S(1)}, u32[]{:S(2)}, u32[]{:S(2)}) collective-permute-start(f32[8,512]{1,0:T(8,128)S(1)} %get-tuple-element.57), channel_id=1, source_target_pairs={{0,24},{8,16},{16,8},{24,0},{1,25},{9,17},{17,9},{25,1},{2,26},{10... | collective-permute-start | bytes 49160 | tf_op jit(solution)/shard_map/ppermute | solution.py:429
  96.1 1.2 %collective-permute-start.22 = (f32[8,512]{1,0:T(8,128)S(1)}, f32[8,512]{1,0:T(8,128)S(1)}, u32[]{:S(2)}, u32[]{:S(2)}) collective-permute-start(f32[8,512]{1,0:T(8,128)S(1)} %get-tuple-element.58), channel_id=1, source_target_pairs={{0,16},{8,24},{16,0},{24,8},{1,17},{9,25},{17,1},{25,9},{2,18},{10... | collective-permute-start | bytes 49160 | tf_op jit(solution)/shard_map/ppermute | solution.py:429
  97.4 1.0 collective-permute-start.23
  98.4 1.1 collective-permute-done.21.refs_0_
  99.9 1.2 %collective-permute-done.23.refs_2_ = f32[8,512]{1,0:T(8,128)S(1)} collective-permute-done((f32[8,512]{1,0:T(8,128)S(1)}, f32[8,512]{1,0:T(8,128)S(1)}, u32[]{:S(2)}, u32[]{:S(2)}) %collective-permute-start.23) | collective-permute-done | bytes 16416 | tf_op jit(solution)/shard_map/ppermute | solution.py:429
  101.1 0.6 field.5.own_ref
  101.8 1.2 %collective-permute-done.24.other_ref = f32[8,512]{1,0:T(8,128)S(1)} collective-permute-done((f32[8,512]{1,0:T(8,128)S(1)}, f32[8,512]{1,0:T(8,128)S(1)}, u32[]{:S(2)}, u32[]{:S(2)}) %collective-permute-start.24) | collective-permute-done | bytes 16416 | tf_op jit(solution)/shard_map/ppermute | solution.py:429
  103.0 0.9 collective-permute-start.27
  103.9 1.0 collective-permute-start.26
  104.9 2.5 %collective-permute-start.25 = (bf16[8,512]{1,0:T(8,128)(2,1)S(1)}, bf16[8,512]{1,0:T(8,128)(2,1)S(1)}, u32[]{:S(2)}, u32[]{:S(2)}) collective-permute-start(bf16[8,512]{1,0:T(8,128)(2,1)S(1)} %pair.5.refs_0_), channel_id=1, source_target_pairs={{0,2},{2,0},{4,6},{6,4},{1,3},{3,1},{5,7},{7,5},{8,10},{10,8},{12,... | collective-permute-start | bytes 24584 | tf_op jit(solution)/shard_map/ppermute | solution.py:429
  107.4 1.1 collective-permute-done.27.refs_3_
  108.6 0.4 collective-permute-done.25.refs_1_
  109.0 0.5 apply.5
  109.5 1.6 %collective-permute-start.30 = (f32[8,128]{1,0:T(8,128)S(1)}, f32[8,128]{1,0:T(8,128)S(1)}, u32[]{:S(2)}, u32[]{:S(2)}) collective-permute-start(f32[8,128]{1,0:T(8,128)S(1)} %get-tuple-element.64.refs_0_), channel_id=1, source_target_pairs={{0,24},{8,16},{16,8},{24,0},{1,25},{9,17},{17,9},{25,1},{2,26},{10... | collective-permute-start | bytes 12296 | tf_op jit(solution)/shard_map/ppermute | solution.py:429
  111.1 1.5 %collective-permute-start.29 = (f32[8,128]{1,0:T(8,128)S(1)}, f32[8,128]{1,0:T(8,128)S(1)}, u32[]{:S(2)}, u32[]{:S(2)}) collective-permute-start(f32[8,128]{1,0:T(8,128)S(1)} %get-tuple-element.64.refs_0_), channel_id=1, source_target_pairs={{0,16},{8,24},{16,0},{24,8},{1,17},{9,25},{17,1},{25,9},{2,18},{10... | collective-permute-start | bytes 12296 | tf_op jit(solution)/shard_map/ppermute | solution.py:429
  112.6 0.4 collective-permute-start.28
  113.0 1.1 own.1
  114.2 0.5 collective-permute-done.29.refs_2_
  114.7 1.5 %collective-permute-done.28.refs_1_ = f32[8,128]{1,0:T(8,128)S(1)} collective-permute-done((f32[8,128]{1,0:T(8,128)S(1)}, f32[8,128]{1,0:T(8,128)S(1)}, u32[]{:S(2)}, u32[]{:S(2)}) %collective-permute-start.28) | collective-permute-done | bytes 4128 | tf_op jit(solution)/shard_map/ppermute | solution.py:429
  116.2 1.1 end.1
  (39 shorter events, 1.4 us)
Async XLA Ops:
  0.6 7.9 %copy-start.2 = (s32[16,16]{1,0:T(8,128)S(1)}, s32[16,16]{1,0:T(8,128)}, u32[]{:S(2)}) copy-start(s32[16,16]{1,0:T(8,128)} %mi_ref.1) | copy-start | bytes 3076
  0.6 11.9 %copy-start.1 = (bf16[4,512,512]{2,1,0:T(8,128)(2,1)S(1)}, bf16[4,512,512]{2,1,0:T(8,128)(2,1)}, u32[]{:S(2)}) copy-start(bf16[4,512,512]{2,1,0:T(8,128)(2,1)} %refs_8_.3) | copy-start | bytes 6291460
  1.6 1.4 %collective-permute-start = (f32[16,128]{1,0:T(8,128)S(1)}, f32[16,128]{1,0:T(8,128)S(1)}, u32[]{:S(2)}, u32[]{:S(2)}) collective-permute-start(f32[16,128]{1,0:T(8,128)S(1)} %begin.1.own_ref), channel_id=1, source_target_pairs={{0,1},{1,0},{2,3},{3,2},{4,5},{5,4},{6,7},{7,6},{8,9},{9,8},{10,11... | collective-permute-start | bytes 24584 | tf_op jit(solution)/shard_map/ppermute | solution.py:429
  3.0 6.6 %collective-permute-start.3 = (f32[32,128]{1,0:T(8,128)S(1)}, f32[32,128]{1,0:T(8,128)S(1)}, u32[]{:S(2)}, u32[]{:S(2)}) collective-permute-start(f32[32,128]{1,0:T(8,128)S(1)} %stack.1.refs_0_), channel_id=1, source_target_pairs={{0,6},{2,4},{4,2},{6,0},{1,7},{3,5},{5,3},{7,1},{8,14},{10,12},{12... | collective-permute-start | bytes 49160 | tf_op jit(solution)/shard_map/ppermute | solution.py:429
  7.9 4.6 %collective-permute-start.2 = (f32[32,128]{1,0:T(8,128)S(1)}, f32[32,128]{1,0:T(8,128)S(1)}, u32[]{:S(2)}, u32[]{:S(2)}) collective-permute-start(f32[32,128]{1,0:T(8,128)S(1)} %stack.1.refs_0_), channel_id=1, source_target_pairs={{0,4},{2,6},{4,0},{6,2},{1,5},{3,7},{5,1},{7,3},{8,12},{10,14},{12... | collective-permute-start | bytes 49160 | tf_op jit(solution)/shard_map/ppermute | solution.py:429
  7.9 4.6 %collective-permute-start.1 = (f32[32,128]{1,0:T(8,128)S(1)}, f32[32,128]{1,0:T(8,128)S(1)}, u32[]{:S(2)}, u32[]{:S(2)}) collective-permute-start(f32[32,128]{1,0:T(8,128)S(1)} %stack.1.refs_0_), channel_id=1, source_target_pairs={{0,2},{2,0},{4,6},{6,4},{1,3},{3,1},{5,7},{7,5},{8,10},{10,8},{12,... | collective-permute-start | bytes 49160 | tf_op jit(solution)/shard_map/ppermute | solution.py:429
  8.6 17.4 %slice-start = ((s8[16777216]{0:T(1024)(128)(4,1)}), s8[4194304]{0:T(1024)(128)(4,1)S(1)}, s32[]{:S(2)}) async-start(s8[16777216]{0:T(1024)(128)(4,1)} %bitcast.1), calls=%async_computation.3 | async-start | bytes 8388608
  8.9 17.0 %slice-start.1 = ((s8[16777216]{0:T(1024)(128)(4,1)}), s8[4194304]{0:T(1024)(128)(4,1)S(1)}, s32[]{:S(2)}) async-start(s8[16777216]{0:T(1024)(128)(4,1)} %bitcast.1), calls=%async_computation.4 | async-start | bytes 8388608
  8.9 17.0 %slice-start.2 = ((s8[16777216]{0:T(1024)(128)(4,1)}), s8[4194304]{0:T(1024)(128)(4,1)S(1)}, s32[]{:S(2)}) async-start(s8[16777216]{0:T(1024)(128)(4,1)} %bitcast.1), calls=%async_computation.5 | async-start | bytes 8388608
  9.0 17.0 %slice-start.3 = ((s8[16777216]{0:T(1024)(128)(4,1)}), s8[4194304]{0:T(1024)(128)(4,1)S(1)}, s32[]{:S(2)}) async-start(s8[16777216]{0:T(1024)(128)(4,1)} %bitcast.1), calls=%async_computation.6 | async-start | bytes 8388608
  26.0 2.4 %collective-permute-start.4 = (bf16[16,8,640]{2,1,0:T(8,128)(2,1)S(1)}, bf16[16,8,640]{2,1,0:T(8,128)(2,1)S(1)}, u32[]{:S(2)}, u32[]{:S(2)}) collective-permute-start(bf16[16,8,640]{2,1,0:T(8,128)(2,1)S(1)} %all_to_all.15.packet_ref.refs_1_), channel_id=1, source_target_pairs={{0,1},{1,0},{2,3},{3,2},{4,5},{5,4},{6,7},{7,6},{8,9},{9,8},{10,11... | collective-permute-start | bytes 491528 | tf_op jit(solution)/shard_map/ppermute | solution.py:429
  28.4 8.9 %copy-start = (bf16[4,512,512]{2,1,0:T(8,128)(2,1)S(1)}, bf16[4,512,512]{2,1,0:T(8,128)(2,1)}, u32[]{:S(2)}) copy-start(bf16[4,512,512]{2,1,0:T(8,128)(2,1)} %refs_4_.11) | copy-start | bytes 6291460
  31.0 14.2 %copy-start.3 = (f32[2]{0:T(128)S(1)}, f32[2]{0:T(128)}, u32[]{:S(2)}) copy-start(f32[2]{0:T(128)} %param.11) | copy-start | bytes 28
  31.0 4.7 %collective-permute-start.5 = (f32[8,512]{1,0:T(8,128)S(1)}, f32[8,512]{1,0:T(8,128)S(1)}, u32[]{:S(2)}, u32[]{:S(2)}) collective-permute-start(f32[8,512]{1,0:T(8,128)S(1)} %get-tuple-element.40), channel_id=1, source_target_pairs={{0,24},{8,16},{16,8},{24,0},{1,25},{9,17},{17,9},{25,1},{2,26},{10... | collective-permute-start | bytes 49160 | tf_op jit(solution)/shard_map/ppermute | solution.py:429
  32.3 3.7 %collective-permute-start.6 = (f32[8,512]{1,0:T(8,128)S(1)}, f32[8,512]{1,0:T(8,128)S(1)}, u32[]{:S(2)}, u32[]{:S(2)}) collective-permute-start(f32[8,512]{1,0:T(8,128)S(1)} %get-tuple-element.41), channel_id=1, source_target_pairs={{0,16},{8,24},{16,0},{24,8},{1,17},{9,25},{17,1},{25,9},{2,18},{10... | collective-permute-start | bytes 49160 | tf_op jit(solution)/shard_map/ppermute | solution.py:429
  33.5 3.7 %collective-permute-start.7 = (f32[8,512]{1,0:T(8,128)S(1)}, f32[8,512]{1,0:T(8,128)S(1)}, u32[]{:S(2)}, u32[]{:S(2)}) collective-permute-start(f32[8,512]{1,0:T(8,128)S(1)} %get-tuple-element.42), channel_id=1, source_target_pairs={{0,8},{8,0},{16,24},{24,16},{1,9},{9,1},{17,25},{25,17},{2,10},{10... | collective-permute-start | bytes 49160 | tf_op jit(solution)/shard_map/ppermute | solution.py:429
  37.9 1.2 %collective-permute-start.8 = (f32[8,512]{1,0:T(8,128)S(1)}, f32[8,512]{1,0:T(8,128)S(1)}, u32[]{:S(2)}, u32[]{:S(2)}) collective-permute-start(f32[8,512]{1,0:T(8,128)S(1)} %field.3.own_ref), channel_id=1, source_target_pairs={{0,1},{1,0},{2,3},{3,2},{4,5},{5,4},{6,7},{7,6},{8,9},{9,8},{10,11... | collective-permute-start | bytes 49160 | tf_op jit(solution)/shard_map/ppermute | solution.py:429
  39.1 5.5 %collective-permute-start.11 = (bf16[8,512]{1,0:T(8,128)(2,1)S(1)}, bf16[8,512]{1,0:T(8,128)(2,1)S(1)}, u32[]{:S(2)}, u32[]{:S(2)}) collective-permute-start(bf16[8,512]{1,0:T(8,128)(2,1)S(1)} %pair.3.refs_0_), channel_id=1, source_target_pairs={{0,6},{2,4},{4,2},{6,0},{1,7},{3,5},{5,3},{7,1},{8,14},{10,12},{12... | collective-permute-start | bytes 24584 | tf_op jit(solution)/shard_map/ppermute | solution.py:429
  40.0 4.7 %collective-permute-start.10 = (bf16[8,512]{1,0:T(8,128)(2,1)S(1)}, bf16[8,512]{1,0:T(8,128)(2,1)S(1)}, u32[]{:S(2)}, u32[]{:S(2)}) collective-permute-start(bf16[8,512]{1,0:T(8,128)(2,1)S(1)} %pair.3.refs_0_), channel_id=1, source_target_pairs={{0,4},{2,6},{4,0},{6,2},{1,5},{3,7},{5,1},{7,3},{8,12},{10,14},{12... | collective-permute-start | bytes 24584 | tf_op jit(solution)/shard_map/ppermute | solution.py:429
  41.0 4.1 %collective-permute-start.9 = (bf16[8,512]{1,0:T(8,128)(2,1)S(1)}, bf16[8,512]{1,0:T(8,128)(2,1)S(1)}, u32[]{:S(2)}, u32[]{:S(2)}) collective-permute-start(bf16[8,512]{1,0:T(8,128)(2,1)S(1)} %pair.3.refs_0_), channel_id=1, source_target_pairs={{0,2},{2,0},{4,6},{6,4},{1,3},{3,1},{5,7},{7,5},{8,10},{10,8},{12,... | collective-permute-start | bytes 24584 | tf_op jit(solution)/shard_map/ppermute | solution.py:429
  58.0 2.4 %collective-permute-start.12 = (bf16[16,8,640]{2,1,0:T(8,128)(2,1)S(1)}, bf16[16,8,640]{2,1,0:T(8,128)(2,1)S(1)}, u32[]{:S(2)}, u32[]{:S(2)}) collective-permute-start(bf16[16,8,640]{2,1,0:T(8,128)(2,1)S(1)} %all_to_all.16.packet_ref.refs_1_), channel_id=1, source_target_pairs={{0,1},{1,0},{2,3},{3,2},{4,5},{5,4},{6,7},{7,6},{8,9},{9,8},{10,11... | collective-permute-start | bytes 491528 | tf_op jit(solution)/shard_map/ppermute | solution.py:429
  62.9 4.7 %collective-permute-start.13 = (f32[8,512]{1,0:T(8,128)S(1)}, f32[8,512]{1,0:T(8,128)S(1)}, u32[]{:S(2)}, u32[]{:S(2)}) collective-permute-start(f32[8,512]{1,0:T(8,128)S(1)} %get-tuple-element.49), channel_id=1, source_target_pairs={{0,24},{8,16},{16,8},{24,0},{1,25},{9,17},{17,9},{25,1},{2,26},{10... | collective-permute-start | bytes 49160 | tf_op jit(solution)/shard_map/ppermute | solution.py:429
  64.2 3.7 %collective-permute-start.14 = (f32[8,512]{1,0:T(8,128)S(1)}, f32[8,512]{1,0:T(8,128)S(1)}, u32[]{:S(2)}, u32[]{:S(2)}) collective-permute-start(f32[8,512]{1,0:T(8,128)S(1)} %get-tuple-element.50), channel_id=1, source_target_pairs={{0,16},{8,24},{16,0},{24,8},{1,17},{9,25},{17,1},{25,9},{2,18},{10... | collective-permute-start | bytes 49160 | tf_op jit(solution)/shard_map/ppermute | solution.py:429
  65.5 3.7 %collective-permute-start.15 = (f32[8,512]{1,0:T(8,128)S(1)}, f32[8,512]{1,0:T(8,128)S(1)}, u32[]{:S(2)}, u32[]{:S(2)}) collective-permute-start(f32[8,512]{1,0:T(8,128)S(1)} %get-tuple-element.51), channel_id=1, source_target_pairs={{0,8},{8,0},{16,24},{24,16},{1,9},{9,1},{17,25},{25,17},{2,10},{10... | collective-permute-start | bytes 49160 | tf_op jit(solution)/shard_map/ppermute | solution.py:429
  69.9 1.2 %collective-permute-start.16 = (f32[8,512]{1,0:T(8,128)S(1)}, f32[8,512]{1,0:T(8,128)S(1)}, u32[]{:S(2)}, u32[]{:S(2)}) collective-permute-start(f32[8,512]{1,0:T(8,128)S(1)} %field.4.own_ref), channel_id=1, source_target_pairs={{0,1},{1,0},{2,3},{3,2},{4,5},{5,4},{6,7},{7,6},{8,9},{9,8},{10,11... | collective-permute-start | bytes 49160 | tf_op jit(solution)/shard_map/ppermute | solution.py:429
  71.1 5.5 %collective-permute-start.19 = (bf16[8,512]{1,0:T(8,128)(2,1)S(1)}, bf16[8,512]{1,0:T(8,128)(2,1)S(1)}, u32[]{:S(2)}, u32[]{:S(2)}) collective-permute-start(bf16[8,512]{1,0:T(8,128)(2,1)S(1)} %pair.4.refs_0_), channel_id=1, source_target_pairs={{0,6},{2,4},{4,2},{6,0},{1,7},{3,5},{5,3},{7,1},{8,14},{10,12},{12... | collective-permute-start | bytes 24584 | tf_op jit(solution)/shard_map/ppermute | solution.py:429
  72.0 4.6 %collective-permute-start.18 = (bf16[8,512]{1,0:T(8,128)(2,1)S(1)}, bf16[8,512]{1,0:T(8,128)(2,1)S(1)}, u32[]{:S(2)}, u32[]{:S(2)}) collective-permute-start(bf16[8,512]{1,0:T(8,128)(2,1)S(1)} %pair.4.refs_0_), channel_id=1, source_target_pairs={{0,4},{2,6},{4,0},{6,2},{1,5},{3,7},{5,1},{7,3},{8,12},{10,14},{12... | collective-permute-start | bytes 24584 | tf_op jit(solution)/shard_map/ppermute | solution.py:429
  73.0 4.1 %collective-permute-start.17 = (bf16[8,512]{1,0:T(8,128)(2,1)S(1)}, bf16[8,512]{1,0:T(8,128)(2,1)S(1)}, u32[]{:S(2)}, u32[]{:S(2)}) collective-permute-start(bf16[8,512]{1,0:T(8,128)(2,1)S(1)} %pair.4.refs_0_), channel_id=1, source_target_pairs={{0,2},{2,0},{4,6},{6,4},{1,3},{3,1},{5,7},{7,5},{8,10},{10,8},{12,... | collective-permute-start | bytes 24584 | tf_op jit(solution)/shard_map/ppermute | solution.py:429
  89.9 2.4 %collective-permute-start.20 = (bf16[16,8,640]{2,1,0:T(8,128)(2,1)S(1)}, bf16[16,8,640]{2,1,0:T(8,128)(2,1)S(1)}, u32[]{:S(2)}, u32[]{:S(2)}) collective-permute-start(bf16[16,8,640]{2,1,0:T(8,128)(2,1)S(1)} %all_to_all.17.packet_ref.refs_1_), channel_id=1, source_target_pairs={{0,1},{1,0},{2,3},{3,2},{4,5},{5,4},{6,7},{7,6},{8,9},{9,8},{10,11... | collective-permute-start | bytes 491528 | tf_op jit(solution)/shard_map/ppermute | solution.py:429
  94.8 4.7 %collective-permute-start.21 = (f32[8,512]{1,0:T(8,128)S(1)}, f32[8,512]{1,0:T(8,128)S(1)}, u32[]{:S(2)}, u32[]{:S(2)}) collective-permute-start(f32[8,512]{1,0:T(8,128)S(1)} %get-tuple-element.57), channel_id=1, source_target_pairs={{0,24},{8,16},{16,8},{24,0},{1,25},{9,17},{17,9},{25,1},{2,26},{10... | collective-permute-start | bytes 49160 | tf_op jit(solution)/shard_map/ppermute | solution.py:429
  96.1 3.7 %collective-permute-start.22 = (f32[8,512]{1,0:T(8,128)S(1)}, f32[8,512]{1,0:T(8,128)S(1)}, u32[]{:S(2)}, u32[]{:S(2)}) collective-permute-start(f32[8,512]{1,0:T(8,128)S(1)} %get-tuple-element.58), channel_id=1, source_target_pairs={{0,16},{8,24},{16,0},{24,8},{1,17},{9,25},{17,1},{25,9},{2,18},{10... | collective-permute-start | bytes 49160 | tf_op jit(solution)/shard_map/ppermute | solution.py:429
  97.4 3.7 %collective-permute-start.23 = (f32[8,512]{1,0:T(8,128)S(1)}, f32[8,512]{1,0:T(8,128)S(1)}, u32[]{:S(2)}, u32[]{:S(2)}) collective-permute-start(f32[8,512]{1,0:T(8,128)S(1)} %get-tuple-element.59), channel_id=1, source_target_pairs={{0,8},{8,0},{16,24},{24,16},{1,9},{9,1},{17,25},{25,17},{2,10},{10... | collective-permute-start | bytes 49160 | tf_op jit(solution)/shard_map/ppermute | solution.py:429
  101.8 1.2 %collective-permute-start.24 = (f32[8,512]{1,0:T(8,128)S(1)}, f32[8,512]{1,0:T(8,128)S(1)}, u32[]{:S(2)}, u32[]{:S(2)}) collective-permute-start(f32[8,512]{1,0:T(8,128)S(1)} %field.5.own_ref), channel_id=1, source_target_pairs={{0,1},{1,0},{2,3},{3,2},{4,5},{5,4},{6,7},{7,6},{8,9},{9,8},{10,11... | collective-permute-start | bytes 49160 | tf_op jit(solution)/shard_map/ppermute | solution.py:429
  103.0 5.5 %collective-permute-start.27 = (bf16[8,512]{1,0:T(8,128)(2,1)S(1)}, bf16[8,512]{1,0:T(8,128)(2,1)S(1)}, u32[]{:S(2)}, u32[]{:S(2)}) collective-permute-start(bf16[8,512]{1,0:T(8,128)(2,1)S(1)} %pair.5.refs_0_), channel_id=1, source_target_pairs={{0,6},{2,4},{4,2},{6,0},{1,7},{3,5},{5,3},{7,1},{8,14},{10,12},{12... | collective-permute-start | bytes 24584 | tf_op jit(solution)/shard_map/ppermute | solution.py:429
  103.9 4.7 %collective-permute-start.26 = (bf16[8,512]{1,0:T(8,128)(2,1)S(1)}, bf16[8,512]{1,0:T(8,128)(2,1)S(1)}, u32[]{:S(2)}, u32[]{:S(2)}) collective-permute-start(bf16[8,512]{1,0:T(8,128)(2,1)S(1)} %pair.5.refs_0_), channel_id=1, source_target_pairs={{0,4},{2,6},{4,0},{6,2},{1,5},{3,7},{5,1},{7,3},{8,12},{10,14},{12... | collective-permute-start | bytes 24584 | tf_op jit(solution)/shard_map/ppermute | solution.py:429
  104.9 4.1 %collective-permute-start.25 = (bf16[8,512]{1,0:T(8,128)(2,1)S(1)}, bf16[8,512]{1,0:T(8,128)(2,1)S(1)}, u32[]{:S(2)}, u32[]{:S(2)}) collective-permute-start(bf16[8,512]{1,0:T(8,128)(2,1)S(1)} %pair.5.refs_0_), channel_id=1, source_target_pairs={{0,2},{2,0},{4,6},{6,4},{1,3},{3,1},{5,7},{7,5},{8,10},{10,8},{12,... | collective-permute-start | bytes 24584 | tf_op jit(solution)/shard_map/ppermute | solution.py:429
  109.5 4.7 %collective-permute-start.30 = (f32[8,128]{1,0:T(8,128)S(1)}, f32[8,128]{1,0:T(8,128)S(1)}, u32[]{:S(2)}, u32[]{:S(2)}) collective-permute-start(f32[8,128]{1,0:T(8,128)S(1)} %get-tuple-element.64.refs_0_), channel_id=1, source_target_pairs={{0,24},{8,16},{16,8},{24,0},{1,25},{9,17},{17,9},{25,1},{2,26},{10... | collective-permute-start | bytes 12296 | tf_op jit(solution)/shard_map/ppermute | solution.py:429
  111.1 3.6 %collective-permute-start.29 = (f32[8,128]{1,0:T(8,128)S(1)}, f32[8,128]{1,0:T(8,128)S(1)}, u32[]{:S(2)}, u32[]{:S(2)}) collective-permute-start(f32[8,128]{1,0:T(8,128)S(1)} %get-tuple-element.64.refs_0_), channel_id=1, source_target_pairs={{0,16},{8,24},{16,0},{24,8},{1,17},{9,25},{17,1},{25,9},{2,18},{10... | collective-permute-start | bytes 12296 | tf_op jit(solution)/shard_map/ppermute | solution.py:429
  112.6 3.6 %collective-permute-start.28 = (f32[8,128]{1,0:T(8,128)S(1)}, f32[8,128]{1,0:T(8,128)S(1)}, u32[]{:S(2)}, u32[]{:S(2)}) collective-permute-start(f32[8,128]{1,0:T(8,128)S(1)} %get-tuple-element.64.refs_0_), channel_id=1, source_target_pairs={{0,8},{8,0},{16,24},{24,16},{1,9},{9,1},{17,25},{25,17},{2,10},{10... | collective-permute-start | bytes 12296 | tf_op jit(solution)/shard_map/ppermute | solution.py:429

commit v6 on v5

--- a/solution.py
+++ b/solution.py
@@ -124,12 +124,26 @@
 
 
 def send(s, density, sums, packet_ref):
-    width = density.shape[1]
-    density = density.astype(BF)
-    sums = sums.astype(BF)
-    for d in range(packet_ref.shape[0]):
-        packet_ref[d, :, :width] = density
-        packet_ref[d, :, width:] = sums
+    half = density.shape[1] // CORES
+    k = s.kpoints
+    ends = [sums[n * k : n * k + 1] for n in range(s.chains)]
+    for c in range(CORES):
+        blocks = [density[:, at : at + LANES] for at in range(c * half, (c + 1) * half, LANES)]
+        value = jnp.concatenate(blocks + ends, axis=0).astype(BF)
+        value = value.reshape(packet_ref.shape[1:])
+        for d in range(c, packet_ref.shape[0], CORES):
+            packet_ref[d] = value
+
+
+def received(s, packet_ref, d):
+    value = packet_ref[d].reshape(-1, LANES).astype(F32)
+    height = value.shape[0] - s.chains
+    blocks = [value[at : at + s.rows] for at in range(0, height, s.rows)]
+    sums = [
+        jnp.broadcast_to(value[height + n : height + n + 1], (s.kpoints, LANES))
+        for n in range(s.chains)
+    ]
+    return jnp.concatenate(blocks, axis=1), jnp.concatenate(sums, axis=0)
 
 
 def pair_kernel(s, own_ref, other_ref, out_ref):
@@ -288,23 +302,20 @@
 
 
 def images(s, packet_ref, screened_ref, other):
-    width = packet_ref.shape[2] - LANES
-    rows, core = s.rows, lax.axis_index("core") ^ other
     columns = []
-    for z in range(s.chips):
-        blocks = [
-            packet_ref[a * s.chips + z, :, :width].astype(F32) for a in range(s.groups)
-        ]
+    for b in range(s.parts):
+        blocks = [received(s, packet_ref, a * s.parts + b)[0] for a in range(s.groups)]
         columns.append(jnp.concatenate(blocks, axis=0).astype(BF))
+    half = columns[0].shape[1]
+    core = lax.axis_index("core") ^ other
     result = []
     for q in range(s.transfers):
         image = None
-        for z in range(s.chips):
-            part = z * CORES + core
-            lanes = pl.ds(pl.multiple_of(part * width, width), width)
+        for b in range(s.parts):
+            at = (b * CORES + core) * half
             piece = lax.dot_general(
-                screened_ref[q, :, lanes],
-                columns[z],
+                screened_ref[q, :, pl.ds(pl.multiple_of(at, half), half)],
+                columns[b],
                 (((1,), (1,)), ((), ())),
                 preferred_element_type=F32,
             )
@@ -331,15 +342,8 @@
     image_ref = refs.pop(0) if keep else None
     (field_ref,) = refs
     rows = s.rows
-    width = packet_refs[0].shape[2] - LANES
-    core = lax.axis_index("core")
     if not first:
-        tiles = [
-            jnp.where(
-                core == 0, *(ref[a * s.chips, :, width:].astype(F32) for ref in packet_refs)
-            )
-            for a in range(s.groups)
-        ]
+        tiles = [received(s, packet_refs[0], a * s.parts)[1] for a in range(s.groups)]
         alpha, beta, offsets = read_sums(s, tiles)
         scale = 1.0 / beta
         lane = iota((rows, LANES), 1)
@@ -420,7 +424,8 @@
     s.entries = float(nk * bands)
     total = groups * s.rows
     state = ((s.rows, bands), F32)
-    packet = ((groups * parts // CORES, s.rows, width + LANES), BF)
+    pairs = (s.rows * width // CORES // LANES + s.chains) // 2
+    packet = ((groups * parts, pairs, 2, LANES), BF)
 
     def exchange(x, axes):
         return lax.all_to_all(x, axes, 0, 0, tiled=True)
@@ -473,7 +478,7 @@
     before = work = None
     for step in range(STEPS):
         first, keep = step == 0, step < STEPS - 1
-        got = exchange(sent, ("kpt", "z"))
+        got = exchange(sent, ("kpt", "z", "core"))
         other = across(got, "core", CORES, 1)
         image = ((s.transfers, total, width), F32)
         (half,) = call(

time: 118 us -> 116 us (0.983)
  waiting for transfers between devices: 23.1 us -> 21.5 us
    ppermute x31, waiting for transfers between devices: 23.1 us -> 21.5 us  [across(): return lax.ppermute(x, axis, [(i, i ^ distance) for i in range(size)])]
  transfers between devices with their start and end apart: 31 -> 31, of which waited for: 25 -> 23; matrix products, arithmetic and copies ran while one was open for 0% -> 0% of each run, Pallas kernels for 7% -> 7%
where the time goes in v6:
time: 116 us
  blocking collectives  36.2 us (31%)
  starting transfers between devices  34.6 us (30%)
  Pallas kernels  22.8 us (20%)
  waiting for transfers between devices  21.5 us (19%)
    all_to_all x3, blocking collectives, exchange(): return lax.all_to_all(x, axes, 0, 0, tiled=True)  36.2 us
    ppermute x31, starting transfers between devices, across(): return lax.ppermute(x, axis, [(i, i ^ distance) for i in range(size)])  34.6 us
    pallas_call x21, Pallas kernels, call(): pl.pallas_call(body, out_shape=[jax.ShapeDtypeStruct(shape, dtype) for sh...  22.8 us
    ppermute x31, waiting for transfers between devices, across(): return lax.ppermute(x, axis, [(i, i ^ distance) for i in range(size)])  21.5 us
  transfers between devices with their start and end apart: 31, of which 23 were waited for; matrix products, arithmetic and copies ran while one was open for 0% of the time, Pallas kernels for 7%

profile of v6, /device:TPU:0, one launch (start us, length us, event | category | flops | bytes accessed | tf_op | source)
XLA Modules:
  0.0 116.1 jit_solution(2247212665724385439)
XLA Ops:
  0.7 1.0 begin.1.own_ref
  1.6 0.6 collective-permute-start
  2.2 0.8 collective-permute-done.other_ref
  3.0 4.9 %collective-permute-start.3 = (f32[32,128]{1,0:T(8,128)S(1)}, f32[32,128]{1,0:T(8,128)S(1)}, u32[]{:S(2)}, u32[]{:S(2)}) collective-permute-start(f32[32,128]{1,0:T(8,128)S(1)} %stack.1.refs_0_), channel_id=1, source_target_pairs={{0,6},{2,4},{4,2},{6,0},{1,7},{3,5},{5,3},{7,1},{8,14},{10,12},{12... | collective-permute-start | bytes 49160 | tf_op jit(solution)/shard_map/ppermute | solution.py:434
  7.9 0.6 collective-permute-start.1
  9.0 0.7 collective-permute-done.3.refs_3_
  9.7 2.9 %collective-permute-done.2.refs_2_ = f32[32,128]{1,0:T(8,128)S(1)} collective-permute-done((f32[32,128]{1,0:T(8,128)S(1)}, f32[32,128]{1,0:T(8,128)S(1)}, u32[]{:S(2)}, u32[]{:S(2)}) %collective-permute-start.2) | collective-permute-done | bytes 16416 | tf_op jit(solution)/shard_map/ppermute | solution.py:434
  12.6 0.5 unpack.1
  13.1 12.4 %all_to_all.15.packet_ref.refs_1_ = bf16[32,9,2,128]{3,2,1,0:T(2,128)(2,1)S(1)} all-to-all(bf16[32,9,2,128]{3,2,1,0:T(2,128)(2,1)S(1)} %get-tuple-element.39), channel_id=1, replica_groups=mesh['kpt'=4,'z'=4,'core'=2] {'kpt','z','core'}, dimensions={0} | all-to-all | bytes 294912 | tf_op jit(solution)/shard_map/all_to_all | solution.py:431
  25.5 0.4 collective-permute-start.4
  25.9 2.4 %half.3.refs_0_ = f32[4,32,512]{2,1,0:T(8,128)S(1)} custom-call(bf16[32,9,2,128]{3,2,1,0:T(2,128)(2,1)S(1)} %all_to_all.15.packet_ref.refs_1_, bf16[4,512,4096]{2,1,0:T(8,128)(2,1)S(1)} %bitcast.2), custom_call_target="tpu_custom_call" | custom-call | flops 10000000000 | bytes 39062500 | tf_op jit(solution)/shard_map/half/pallas_call | solution.py:399
  28.3 2.6 %screen.3 = (f32[8,512]{1,0:T(8,128)S(1)}, f32[8,512]{1,0:T(8,128)S(1)}, f32[8,512]{1,0:T(8,128)S(1)}, f32[8,512]{1,0:T(8,128)S(1)}, f32[4,32,512]{2,1,0:T(8,128)S(1)}) custom-call(f32[4,32,512]{2,1,0:T(8,128)S(1)} %half.3.refs_0_, bf16[32,9,2,128]{3,2,1,0:T(2,128)(2,1)S(1)} %all_to_all.15.packet_ref.refs_1_, ...), custom_call_target="tpu_custom_call" | custom-call | tf_op jit(solution)/shard_map/screen/pallas_call | solution.py:399
  30.9 0.7 collective-permute-start.5
  31.6 1.3 %collective-permute-start.6 = (f32[8,512]{1,0:T(8,128)S(1)}, f32[8,512]{1,0:T(8,128)S(1)}, u32[]{:S(2)}, u32[]{:S(2)}) collective-permute-start(f32[8,512]{1,0:T(8,128)S(1)} %get-tuple-element.41), channel_id=1, source_target_pairs={{0,16},{8,24},{16,0},{24,8},{1,17},{9,25},{17,1},{25,9},{2,18},{10... | collective-permute-start | bytes 49160 | tf_op jit(solution)/shard_map/ppermute | solution.py:434
  32.9 1.5 %collective-permute-start.7 = (f32[8,512]{1,0:T(8,128)S(1)}, f32[8,512]{1,0:T(8,128)S(1)}, u32[]{:S(2)}, u32[]{:S(2)}) collective-permute-start(f32[8,512]{1,0:T(8,128)S(1)} %get-tuple-element.42), channel_id=1, source_target_pairs={{0,8},{8,0},{16,24},{24,16},{1,9},{9,1},{17,25},{25,17},{2,10},{10... | collective-permute-start | bytes 49160 | tf_op jit(solution)/shard_map/ppermute | solution.py:434
  34.4 1.1 collective-permute-done.5.refs_0_
  35.6 1.1 collective-permute-done.7.refs_2_
  36.6 0.6 field.3.own_ref
  37.3 1.2 %collective-permute-done.8.other_ref = f32[8,512]{1,0:T(8,128)S(1)} collective-permute-done((f32[8,512]{1,0:T(8,128)S(1)}, f32[8,512]{1,0:T(8,128)S(1)}, u32[]{:S(2)}, u32[]{:S(2)}) %collective-permute-start.8) | collective-permute-done | bytes 16416 | tf_op jit(solution)/shard_map/ppermute | solution.py:434
  38.5 1.3 %collective-permute-start.11 = (bf16[8,512]{1,0:T(8,128)(2,1)S(1)}, bf16[8,512]{1,0:T(8,128)(2,1)S(1)}, u32[]{:S(2)}, u32[]{:S(2)}) collective-permute-start(bf16[8,512]{1,0:T(8,128)(2,1)S(1)} %pair.3.refs_0_), channel_id=1, source_target_pairs={{0,6},{2,4},{4,2},{6,0},{1,7},{3,5},{5,3},{7,1},{8,14},{10,12},{12... | collective-permute-start | bytes 24584 | tf_op jit(solution)/shard_map/ppermute | solution.py:434
  39.8 0.8 collective-permute-start.10
  40.5 2.4 %collective-permute-start.9 = (bf16[8,512]{1,0:T(8,128)(2,1)S(1)}, bf16[8,512]{1,0:T(8,128)(2,1)S(1)}, u32[]{:S(2)}, u32[]{:S(2)}) collective-permute-start(bf16[8,512]{1,0:T(8,128)(2,1)S(1)} %pair.3.refs_0_), channel_id=1, source_target_pairs={{0,2},{2,0},{4,6},{6,4},{1,3},{3,1},{5,7},{7,5},{8,10},{10,8},{12,... | collective-permute-start | bytes 24584 | tf_op jit(solution)/shard_map/ppermute | solution.py:434
  42.9 1.1 collective-permute-done.11.refs_3_
  44.0 0.4 collective-permute-done.10.refs_2_
  44.5 0.8 apply.3
  45.3 11.9 %all_to_all.16.packet_ref.refs_1_ = bf16[32,9,2,128]{3,2,1,0:T(2,128)(2,1)S(1)} all-to-all(bf16[32,9,2,128]{3,2,1,0:T(2,128)(2,1)S(1)} %get-tuple-element.47), channel_id=1, replica_groups=mesh['kpt'=4,'z'=4,'core'=2] {'kpt','z','core'}, dimensions={0} | all-to-all | bytes 294912 | tf_op jit(solution)/shard_map/all_to_all | solution.py:431
  57.5 2.4 %half.4.refs_0_ = f32[4,32,512]{2,1,0:T(8,128)S(1)} custom-call(bf16[32,9,2,128]{3,2,1,0:T(2,128)(2,1)S(1)} %all_to_all.16.packet_ref.refs_1_, bf16[4,512,4096]{2,1,0:T(8,128)(2,1)S(1)} %bitcast.2), custom_call_target="tpu_custom_call" | custom-call | flops 10000000000 | bytes 39062500 | tf_op jit(solution)/shard_map/half/pallas_call | solution.py:399
  59.9 2.6 %screen.4 = (f32[8,512]{1,0:T(8,128)S(1)}, f32[8,512]{1,0:T(8,128)S(1)}, f32[8,512]{1,0:T(8,128)S(1)}, f32[8,512]{1,0:T(8,128)S(1)}, f32[8,128]{1,0:T(8,128)S(1)}, /*index=5*/f32[4,32,512]{2,1,0:T(8,128)S(1)}) custom-call(f32[4,32,512]{2,1,0:T(8,128)S(1)} %half.4.refs_0_, bf16[32,9,2,128]{3,2,1,0:T(2,128)(2,1)S(1)} %all_to_all.16.packet_ref.refs_1_, ...), custom_call_target="tpu_custom_call" | custom-call | tf_op jit(solution)/shard_map/screen/pallas_call | solution.py:399
  62.5 0.7 collective-permute-start.13
  63.2 1.3 %collective-permute-start.14 = (f32[8,512]{1,0:T(8,128)S(1)}, f32[8,512]{1,0:T(8,128)S(1)}, u32[]{:S(2)}, u32[]{:S(2)}) collective-permute-start(f32[8,512]{1,0:T(8,128)S(1)} %get-tuple-element.50), channel_id=1, source_target_pairs={{0,16},{8,24},{16,0},{24,8},{1,17},{9,25},{17,1},{25,9},{2,18},{10... | collective-permute-start | bytes 49160 | tf_op jit(solution)/shard_map/ppermute | solution.py:434
  64.5 1.5 %collective-permute-start.15 = (f32[8,512]{1,0:T(8,128)S(1)}, f32[8,512]{1,0:T(8,128)S(1)}, u32[]{:S(2)}, u32[]{:S(2)}) collective-permute-start(f32[8,512]{1,0:T(8,128)S(1)} %get-tuple-element.51), channel_id=1, source_target_pairs={{0,8},{8,0},{16,24},{24,16},{1,9},{9,1},{17,25},{25,17},{2,10},{10... | collective-permute-start | bytes 49160 | tf_op jit(solution)/shard_map/ppermute | solution.py:434
  66.0 1.1 collective-permute-done.13.refs_0_
  67.2 1.0 collective-permute-done.15.refs_2_
  68.2 0.6 field.4.own_ref
  68.9 1.2 %collective-permute-done.16.other_ref = f32[8,512]{1,0:T(8,128)S(1)} collective-permute-done((f32[8,512]{1,0:T(8,128)S(1)}, f32[8,512]{1,0:T(8,128)S(1)}, u32[]{:S(2)}, u32[]{:S(2)}) %collective-permute-start.16) | collective-permute-done | bytes 16416 | tf_op jit(solution)/shard_map/ppermute | solution.py:434
  70.1 1.3 %collective-permute-start.19 = (bf16[8,512]{1,0:T(8,128)(2,1)S(1)}, bf16[8,512]{1,0:T(8,128)(2,1)S(1)}, u32[]{:S(2)}, u32[]{:S(2)}) collective-permute-start(bf16[8,512]{1,0:T(8,128)(2,1)S(1)} %pair.4.refs_0_), channel_id=1, source_target_pairs={{0,6},{2,4},{4,2},{6,0},{1,7},{3,5},{5,3},{7,1},{8,14},{10,12},{12... | collective-permute-start | bytes 24584 | tf_op jit(solution)/shard_map/ppermute | solution.py:434
  71.4 0.8 collective-permute-start.18
  72.1 2.4 %collective-permute-start.17 = (bf16[8,512]{1,0:T(8,128)(2,1)S(1)}, bf16[8,512]{1,0:T(8,128)(2,1)S(1)}, u32[]{:S(2)}, u32[]{:S(2)}) collective-permute-start(bf16[8,512]{1,0:T(8,128)(2,1)S(1)} %pair.4.refs_0_), channel_id=1, source_target_pairs={{0,2},{2,0},{4,6},{6,4},{1,3},{3,1},{5,7},{7,5},{8,10},{10,8},{12,... | collective-permute-start | bytes 24584 | tf_op jit(solution)/shard_map/ppermute | solution.py:434
  74.5 1.1 collective-permute-done.19.refs_3_
  75.5 0.4 collective-permute-done.18.refs_2_
  76.1 0.7 apply.4
  76.8 11.9 %all_to_all.17.packet_ref.refs_1_ = bf16[32,9,2,128]{3,2,1,0:T(2,128)(2,1)S(1)} all-to-all(bf16[32,9,2,128]{3,2,1,0:T(2,128)(2,1)S(1)} %get-tuple-element.55), channel_id=1, replica_groups=mesh['kpt'=4,'z'=4,'core'=2] {'kpt','z','core'}, dimensions={0} | all-to-all | bytes 294912 | tf_op jit(solution)/shard_map/all_to_all | solution.py:431
  89.1 2.4 %half.5.refs_0_ = f32[4,32,512]{2,1,0:T(8,128)S(1)} custom-call(bf16[32,9,2,128]{3,2,1,0:T(2,128)(2,1)S(1)} %all_to_all.17.packet_ref.refs_1_, bf16[4,512,4096]{2,1,0:T(8,128)(2,1)S(1)} %bitcast.2), custom_call_target="tpu_custom_call" | custom-call | flops 10000000000 | bytes 39062500 | tf_op jit(solution)/shard_map/half/pallas_call | solution.py:399
  91.5 2.6 %screen.5 = (f32[8,512]{1,0:T(8,128)S(1)}, f32[8,512]{1,0:T(8,128)S(1)}, f32[8,512]{1,0:T(8,128)S(1)}, f32[8,512]{1,0:T(8,128)S(1)}, f32[8,128]{1,0:T(8,128)S(1)}) custom-call(f32[4,32,512]{2,1,0:T(8,128)S(1)} %half.5.refs_0_, bf16[32,9,2,128]{3,2,1,0:T(2,128)(2,1)S(1)} %all_to_all.17.packet_ref.refs_1_, ...), custom_call_target="tpu_custom_call" | custom-call | tf_op jit(solution)/shard_map/screen/pallas_call | solution.py:399
  94.0 0.7 collective-permute-start.21
  94.7 1.3 %collective-permute-start.22 = (f32[8,512]{1,0:T(8,128)S(1)}, f32[8,512]{1,0:T(8,128)S(1)}, u32[]{:S(2)}, u32[]{:S(2)}) collective-permute-start(f32[8,512]{1,0:T(8,128)S(1)} %get-tuple-element.58), channel_id=1, source_target_pairs={{0,16},{8,24},{16,0},{24,8},{1,17},{9,25},{17,1},{25,9},{2,18},{10... | collective-permute-start | bytes 49160 | tf_op jit(solution)/shard_map/ppermute | solution.py:434
  96.0 1.5 %collective-permute-start.23 = (f32[8,512]{1,0:T(8,128)S(1)}, f32[8,512]{1,0:T(8,128)S(1)}, u32[]{:S(2)}, u32[]{:S(2)}) collective-permute-start(f32[8,512]{1,0:T(8,128)S(1)} %get-tuple-element.59), channel_id=1, source_target_pairs={{0,8},{8,0},{16,24},{24,16},{1,9},{9,1},{17,25},{25,17},{2,10},{10... | collective-permute-start | bytes 49160 | tf_op jit(solution)/shard_map/ppermute | solution.py:434
  97.6 1.1 collective-permute-done.21.refs_0_
  98.7 1.0 collective-permute-done.23.refs_2_
  99.8 0.6 field.5.own_ref
  100.4 1.2 %collective-permute-done.24.other_ref = f32[8,512]{1,0:T(8,128)S(1)} collective-permute-done((f32[8,512]{1,0:T(8,128)S(1)}, f32[8,512]{1,0:T(8,128)S(1)}, u32[]{:S(2)}, u32[]{:S(2)}) %collective-permute-start.24) | collective-permute-done | bytes 16416 | tf_op jit(solution)/shard_map/ppermute | solution.py:434
  101.6 1.3 %collective-permute-start.27 = (bf16[8,512]{1,0:T(8,128)(2,1)S(1)}, bf16[8,512]{1,0:T(8,128)(2,1)S(1)}, u32[]{:S(2)}, u32[]{:S(2)}) collective-permute-start(bf16[8,512]{1,0:T(8,128)(2,1)S(1)} %pair.5.refs_0_), channel_id=1, source_target_pairs={{0,6},{2,4},{4,2},{6,0},{1,7},{3,5},{5,3},{7,1},{8,14},{10,12},{12... | collective-permute-start | bytes 24584 | tf_op jit(solution)/shard_map/ppermute | solution.py:434
  102.9 0.8 collective-permute-start.26
  103.7 2.4 %collective-permute-start.25 = (bf16[8,512]{1,0:T(8,128)(2,1)S(1)}, bf16[8,512]{1,0:T(8,128)(2,1)S(1)}, u32[]{:S(2)}, u32[]{:S(2)}) collective-permute-start(bf16[8,512]{1,0:T(8,128)(2,1)S(1)} %pair.5.refs_0_), channel_id=1, source_target_pairs={{0,2},{2,0},{4,6},{6,4},{1,3},{3,1},{5,7},{7,5},{8,10},{10,8},{12,... | collective-permute-start | bytes 24584 | tf_op jit(solution)/shard_map/ppermute | solution.py:434
  106.0 1.1 collective-permute-done.27.refs_3_
  107.1 0.4 collective-permute-done.26.refs_2_
  107.7 0.5 apply.5
  108.2 1.5 %collective-permute-start.30 = (f32[8,128]{1,0:T(8,128)S(1)}, f32[8,128]{1,0:T(8,128)S(1)}, u32[]{:S(2)}, u32[]{:S(2)}) collective-permute-start(f32[8,128]{1,0:T(8,128)S(1)} %get-tuple-element.64.refs_0_), channel_id=1, source_target_pairs={{0,24},{8,16},{16,8},{24,0},{1,25},{9,17},{17,9},{25,1},{2,26},{10... | collective-permute-start | bytes 12296 | tf_op jit(solution)/shard_map/ppermute | solution.py:434
  109.7 1.5 %collective-permute-start.29 = (f32[8,128]{1,0:T(8,128)S(1)}, f32[8,128]{1,0:T(8,128)S(1)}, u32[]{:S(2)}, u32[]{:S(2)}) collective-permute-start(f32[8,128]{1,0:T(8,128)S(1)} %get-tuple-element.64.refs_0_), channel_id=1, source_target_pairs={{0,16},{8,24},{16,0},{24,8},{1,17},{9,25},{17,1},{25,9},{2,18},{10... | collective-permute-start | bytes 12296 | tf_op jit(solution)/shard_map/ppermute | solution.py:434
  111.2 0.5 collective-permute-start.28
  111.7 1.1 own.1
  112.8 0.5 collective-permute-done.29.refs_2_
  113.3 1.5 %collective-permute-done.28.refs_1_ = f32[8,128]{1,0:T(8,128)S(1)} collective-permute-done((f32[8,128]{1,0:T(8,128)S(1)}, f32[8,128]{1,0:T(8,128)S(1)}, u32[]{:S(2)}, u32[]{:S(2)}) %collective-permute-start.28) | collective-permute-done | bytes 4128 | tf_op jit(solution)/shard_map/ppermute | solution.py:434
  114.8 1.1 end.1
  (39 shorter events, 1.7 us)
Async XLA Ops:
  0.6 7.9 %copy-start.2 = (s32[16,16]{1,0:T(8,128)S(1)}, s32[16,16]{1,0:T(8,128)}, u32[]{:S(2)}) copy-start(s32[16,16]{1,0:T(8,128)} %mi_ref.1) | copy-start | bytes 3076
  0.6 11.9 %copy-start.1 = (bf16[4,512,512]{2,1,0:T(8,128)(2,1)S(1)}, bf16[4,512,512]{2,1,0:T(8,128)(2,1)}, u32[]{:S(2)}) copy-start(bf16[4,512,512]{2,1,0:T(8,128)(2,1)} %refs_8_.3) | copy-start | bytes 6291460
  1.6 1.4 %collective-permute-start = (f32[16,128]{1,0:T(8,128)S(1)}, f32[16,128]{1,0:T(8,128)S(1)}, u32[]{:S(2)}, u32[]{:S(2)}) collective-permute-start(f32[16,128]{1,0:T(8,128)S(1)} %begin.1.own_ref), channel_id=1, source_target_pairs={{0,1},{1,0},{2,3},{3,2},{4,5},{5,4},{6,7},{7,6},{8,9},{9,8},{10,11... | collective-permute-start | bytes 24584 | tf_op jit(solution)/shard_map/ppermute | solution.py:434
  3.0 6.6 %collective-permute-start.3 = (f32[32,128]{1,0:T(8,128)S(1)}, f32[32,128]{1,0:T(8,128)S(1)}, u32[]{:S(2)}, u32[]{:S(2)}) collective-permute-start(f32[32,128]{1,0:T(8,128)S(1)} %stack.1.refs_0_), channel_id=1, source_target_pairs={{0,6},{2,4},{4,2},{6,0},{1,7},{3,5},{5,3},{7,1},{8,14},{10,12},{12... | collective-permute-start | bytes 49160 | tf_op jit(solution)/shard_map/ppermute | solution.py:434
  7.9 4.6 %collective-permute-start.2 = (f32[32,128]{1,0:T(8,128)S(1)}, f32[32,128]{1,0:T(8,128)S(1)}, u32[]{:S(2)}, u32[]{:S(2)}) collective-permute-start(f32[32,128]{1,0:T(8,128)S(1)} %stack.1.refs_0_), channel_id=1, source_target_pairs={{0,4},{2,6},{4,0},{6,2},{1,5},{3,7},{5,1},{7,3},{8,12},{10,14},{12... | collective-permute-start | bytes 49160 | tf_op jit(solution)/shard_map/ppermute | solution.py:434
  7.9 4.6 %collective-permute-start.1 = (f32[32,128]{1,0:T(8,128)S(1)}, f32[32,128]{1,0:T(8,128)S(1)}, u32[]{:S(2)}, u32[]{:S(2)}) collective-permute-start(f32[32,128]{1,0:T(8,128)S(1)} %stack.1.refs_0_), channel_id=1, source_target_pairs={{0,2},{2,0},{4,6},{6,4},{1,3},{3,1},{5,7},{7,5},{8,10},{10,8},{12,... | collective-permute-start | bytes 49160 | tf_op jit(solution)/shard_map/ppermute | solution.py:434
  8.6 17.3 %slice-start = ((s8[16777216]{0:T(1024)(128)(4,1)}), s8[4194304]{0:T(1024)(128)(4,1)S(1)}, s32[]{:S(2)}) async-start(s8[16777216]{0:T(1024)(128)(4,1)} %bitcast.1), calls=%async_computation.3 | async-start | bytes 8388608
  8.9 17.0 %slice-start.1 = ((s8[16777216]{0:T(1024)(128)(4,1)}), s8[4194304]{0:T(1024)(128)(4,1)S(1)}, s32[]{:S(2)}) async-start(s8[16777216]{0:T(1024)(128)(4,1)} %bitcast.1), calls=%async_computation.4 | async-start | bytes 8388608
  8.9 17.0 %slice-start.2 = ((s8[16777216]{0:T(1024)(128)(4,1)}), s8[4194304]{0:T(1024)(128)(4,1)S(1)}, s32[]{:S(2)}) async-start(s8[16777216]{0:T(1024)(128)(4,1)} %bitcast.1), calls=%async_computation.5 | async-start | bytes 8388608
  9.0 17.0 %slice-start.3 = ((s8[16777216]{0:T(1024)(128)(4,1)}), s8[4194304]{0:T(1024)(128)(4,1)S(1)}, s32[]{:S(2)}) async-start(s8[16777216]{0:T(1024)(128)(4,1)} %bitcast.1), calls=%async_computation.6 | async-start | bytes 8388608
  25.5 2.8 %collective-permute-start.4 = (bf16[32,9,2,128]{3,2,1,0:T(2,128)(2,1)S(1)}, bf16[32,9,2,128]{3,2,1,0:T(2,128)(2,1)S(1)}, u32[]{:S(2)}, u32[]{:S(2)}) collective-permute-start(bf16[32,9,2,128]{3,2,1,0:T(2,128)(2,1)S(1)} %all_to_all.15.packet_ref.refs_1_), channel_id=1, source_target_pairs={{0,1},{1,0},{2,3},{3,2},{4,5},{5,4},{6,7},{7,6},{8,9},{9,8},{10,11... | collective-permute-start | bytes 442376 | tf_op jit(solution)/shard_map/ppermute | solution.py:434
  28.3 8.3 %copy-start = (bf16[4,512,512]{2,1,0:T(8,128)(2,1)S(1)}, bf16[4,512,512]{2,1,0:T(8,128)(2,1)}, u32[]{:S(2)}) copy-start(bf16[4,512,512]{2,1,0:T(8,128)(2,1)} %refs_4_.11) | copy-start | bytes 6291460
  30.9 13.7 %copy-start.3 = (f32[2]{0:T(128)S(1)}, f32[2]{0:T(128)}, u32[]{:S(2)}) copy-start(f32[2]{0:T(128)} %param.11) | copy-start | bytes 28
  30.9 4.7 %collective-permute-start.5 = (f32[8,512]{1,0:T(8,128)S(1)}, f32[8,512]{1,0:T(8,128)S(1)}, u32[]{:S(2)}, u32[]{:S(2)}) collective-permute-start(f32[8,512]{1,0:T(8,128)S(1)} %get-tuple-element.40), channel_id=1, source_target_pairs={{0,24},{8,16},{16,8},{24,0},{1,25},{9,17},{17,9},{25,1},{2,26},{10... | collective-permute-start | bytes 49160 | tf_op jit(solution)/shard_map/ppermute | solution.py:434
  31.6 4.0 %collective-permute-start.6 = (f32[8,512]{1,0:T(8,128)S(1)}, f32[8,512]{1,0:T(8,128)S(1)}, u32[]{:S(2)}, u32[]{:S(2)}) collective-permute-start(f32[8,512]{1,0:T(8,128)S(1)} %get-tuple-element.41), channel_id=1, source_target_pairs={{0,16},{8,24},{16,0},{24,8},{1,17},{9,25},{17,1},{25,9},{2,18},{10... | collective-permute-start | bytes 49160 | tf_op jit(solution)/shard_map/ppermute | solution.py:434
  32.9 3.7 %collective-permute-start.7 = (f32[8,512]{1,0:T(8,128)S(1)}, f32[8,512]{1,0:T(8,128)S(1)}, u32[]{:S(2)}, u32[]{:S(2)}) collective-permute-start(f32[8,512]{1,0:T(8,128)S(1)} %get-tuple-element.42), channel_id=1, source_target_pairs={{0,8},{8,0},{16,24},{24,16},{1,9},{9,1},{17,25},{25,17},{2,10},{10... | collective-permute-start | bytes 49160 | tf_op jit(solution)/shard_map/ppermute | solution.py:434
  37.3 1.2 %collective-permute-start.8 = (f32[8,512]{1,0:T(8,128)S(1)}, f32[8,512]{1,0:T(8,128)S(1)}, u32[]{:S(2)}, u32[]{:S(2)}) collective-permute-start(f32[8,512]{1,0:T(8,128)S(1)} %field.3.own_ref), channel_id=1, source_target_pairs={{0,1},{1,0},{2,3},{3,2},{4,5},{5,4},{6,7},{7,6},{8,9},{9,8},{10,11... | collective-permute-start | bytes 49160 | tf_op jit(solution)/shard_map/ppermute | solution.py:434
  38.5 5.4 %collective-permute-start.11 = (bf16[8,512]{1,0:T(8,128)(2,1)S(1)}, bf16[8,512]{1,0:T(8,128)(2,1)S(1)}, u32[]{:S(2)}, u32[]{:S(2)}) collective-permute-start(bf16[8,512]{1,0:T(8,128)(2,1)S(1)} %pair.3.refs_0_), channel_id=1, source_target_pairs={{0,6},{2,4},{4,2},{6,0},{1,7},{3,5},{5,3},{7,1},{8,14},{10,12},{12... | collective-permute-start | bytes 24584 | tf_op jit(solution)/shard_map/ppermute | solution.py:434
  39.8 4.5 %collective-permute-start.10 = (bf16[8,512]{1,0:T(8,128)(2,1)S(1)}, bf16[8,512]{1,0:T(8,128)(2,1)S(1)}, u32[]{:S(2)}, u32[]{:S(2)}) collective-permute-start(bf16[8,512]{1,0:T(8,128)(2,1)S(1)} %pair.3.refs_0_), channel_id=1, source_target_pairs={{0,4},{2,6},{4,0},{6,2},{1,5},{3,7},{5,1},{7,3},{8,12},{10,14},{12... | collective-permute-start | bytes 24584 | tf_op jit(solution)/shard_map/ppermute | solution.py:434
  40.5 4.0 %collective-permute-start.9 = (bf16[8,512]{1,0:T(8,128)(2,1)S(1)}, bf16[8,512]{1,0:T(8,128)(2,1)S(1)}, u32[]{:S(2)}, u32[]{:S(2)}) collective-permute-start(bf16[8,512]{1,0:T(8,128)(2,1)S(1)} %pair.3.refs_0_), channel_id=1, source_target_pairs={{0,2},{2,0},{4,6},{6,4},{1,3},{3,1},{5,7},{7,5},{8,10},{10,8},{12,... | collective-permute-start | bytes 24584 | tf_op jit(solution)/shard_map/ppermute | solution.py:434
  57.2 2.7 %collective-permute-start.12 = (bf16[32,9,2,128]{3,2,1,0:T(2,128)(2,1)S(1)}, bf16[32,9,2,128]{3,2,1,0:T(2,128)(2,1)S(1)}, u32[]{:S(2)}, u32[]{:S(2)}) collective-permute-start(bf16[32,9,2,128]{3,2,1,0:T(2,128)(2,1)S(1)} %all_to_all.16.packet_ref.refs_1_), channel_id=1, source_target_pairs={{0,1},{1,0},{2,3},{3,2},{4,5},{5,4},{6,7},{7,6},{8,9},{9,8},{10,11... | collective-permute-start | bytes 442376 | tf_op jit(solution)/shard_map/ppermute | solution.py:434
  62.5 4.7 %collective-permute-start.13 = (f32[8,512]{1,0:T(8,128)S(1)}, f32[8,512]{1,0:T(8,128)S(1)}, u32[]{:S(2)}, u32[]{:S(2)}) collective-permute-start(f32[8,512]{1,0:T(8,128)S(1)} %get-tuple-element.49), channel_id=1, source_target_pairs={{0,24},{8,16},{16,8},{24,0},{1,25},{9,17},{17,9},{25,1},{2,26},{10... | collective-permute-start | bytes 49160 | tf_op jit(solution)/shard_map/ppermute | solution.py:434
  63.2 4.0 %collective-permute-start.14 = (f32[8,512]{1,0:T(8,128)S(1)}, f32[8,512]{1,0:T(8,128)S(1)}, u32[]{:S(2)}, u32[]{:S(2)}) collective-permute-start(f32[8,512]{1,0:T(8,128)S(1)} %get-tuple-element.50), channel_id=1, source_target_pairs={{0,16},{8,24},{16,0},{24,8},{1,17},{9,25},{17,1},{25,9},{2,18},{10... | collective-permute-start | bytes 49160 | tf_op jit(solution)/shard_map/ppermute | solution.py:434
  64.5 3.7 %collective-permute-start.15 = (f32[8,512]{1,0:T(8,128)S(1)}, f32[8,512]{1,0:T(8,128)S(1)}, u32[]{:S(2)}, u32[]{:S(2)}) collective-permute-start(f32[8,512]{1,0:T(8,128)S(1)} %get-tuple-element.51), channel_id=1, source_target_pairs={{0,8},{8,0},{16,24},{24,16},{1,9},{9,1},{17,25},{25,17},{2,10},{10... | collective-permute-start | bytes 49160 | tf_op jit(solution)/shard_map/ppermute | solution.py:434
  68.9 1.2 %collective-permute-start.16 = (f32[8,512]{1,0:T(8,128)S(1)}, f32[8,512]{1,0:T(8,128)S(1)}, u32[]{:S(2)}, u32[]{:S(2)}) collective-permute-start(f32[8,512]{1,0:T(8,128)S(1)} %field.4.own_ref), channel_id=1, source_target_pairs={{0,1},{1,0},{2,3},{3,2},{4,5},{5,4},{6,7},{7,6},{8,9},{9,8},{10,11... | collective-permute-start | bytes 49160 | tf_op jit(solution)/shard_map/ppermute | solution.py:434
  70.1 5.4 %collective-permute-start.19 = (bf16[8,512]{1,0:T(8,128)(2,1)S(1)}, bf16[8,512]{1,0:T(8,128)(2,1)S(1)}, u32[]{:S(2)}, u32[]{:S(2)}) collective-permute-start(bf16[8,512]{1,0:T(8,128)(2,1)S(1)} %pair.4.refs_0_), channel_id=1, source_target_pairs={{0,6},{2,4},{4,2},{6,0},{1,7},{3,5},{5,3},{7,1},{8,14},{10,12},{12... | collective-permute-start | bytes 24584 | tf_op jit(solution)/shard_map/ppermute | solution.py:434
  71.4 4.5 %collective-permute-start.18 = (bf16[8,512]{1,0:T(8,128)(2,1)S(1)}, bf16[8,512]{1,0:T(8,128)(2,1)S(1)}, u32[]{:S(2)}, u32[]{:S(2)}) collective-permute-start(bf16[8,512]{1,0:T(8,128)(2,1)S(1)} %pair.4.refs_0_), channel_id=1, source_target_pairs={{0,4},{2,6},{4,0},{6,2},{1,5},{3,7},{5,1},{7,3},{8,12},{10,14},{12... | collective-permute-start | bytes 24584 | tf_op jit(solution)/shard_map/ppermute | solution.py:434
  72.1 4.0 %collective-permute-start.17 = (bf16[8,512]{1,0:T(8,128)(2,1)S(1)}, bf16[8,512]{1,0:T(8,128)(2,1)S(1)}, u32[]{:S(2)}, u32[]{:S(2)}) collective-permute-start(bf16[8,512]{1,0:T(8,128)(2,1)S(1)} %pair.4.refs_0_), channel_id=1, source_target_pairs={{0,2},{2,0},{4,6},{6,4},{1,3},{3,1},{5,7},{7,5},{8,10},{10,8},{12,... | collective-permute-start | bytes 24584 | tf_op jit(solution)/shard_map/ppermute | solution.py:434
  88.7 2.7 %collective-permute-start.20 = (bf16[32,9,2,128]{3,2,1,0:T(2,128)(2,1)S(1)}, bf16[32,9,2,128]{3,2,1,0:T(2,128)(2,1)S(1)}, u32[]{:S(2)}, u32[]{:S(2)}) collective-permute-start(bf16[32,9,2,128]{3,2,1,0:T(2,128)(2,1)S(1)} %all_to_all.17.packet_ref.refs_1_), channel_id=1, source_target_pairs={{0,1},{1,0},{2,3},{3,2},{4,5},{5,4},{6,7},{7,6},{8,9},{9,8},{10,11... | collective-permute-start | bytes 442376 | tf_op jit(solution)/shard_map/ppermute | solution.py:434
  94.0 4.7 %collective-permute-start.21 = (f32[8,512]{1,0:T(8,128)S(1)}, f32[8,512]{1,0:T(8,128)S(1)}, u32[]{:S(2)}, u32[]{:S(2)}) collective-permute-start(f32[8,512]{1,0:T(8,128)S(1)} %get-tuple-element.57), channel_id=1, source_target_pairs={{0,24},{8,16},{16,8},{24,0},{1,25},{9,17},{17,9},{25,1},{2,26},{10... | collective-permute-start | bytes 49160 | tf_op jit(solution)/shard_map/ppermute | solution.py:434
  94.7 4.0 %collective-permute-start.22 = (f32[8,512]{1,0:T(8,128)S(1)}, f32[8,512]{1,0:T(8,128)S(1)}, u32[]{:S(2)}, u32[]{:S(2)}) collective-permute-start(f32[8,512]{1,0:T(8,128)S(1)} %get-tuple-element.58), channel_id=1, source_target_pairs={{0,16},{8,24},{16,0},{24,8},{1,17},{9,25},{17,1},{25,9},{2,18},{10... | collective-permute-start | bytes 49160 | tf_op jit(solution)/shard_map/ppermute | solution.py:434
  96.0 3.7 %collective-permute-start.23 = (f32[8,512]{1,0:T(8,128)S(1)}, f32[8,512]{1,0:T(8,128)S(1)}, u32[]{:S(2)}, u32[]{:S(2)}) collective-permute-start(f32[8,512]{1,0:T(8,128)S(1)} %get-tuple-element.59), channel_id=1, source_target_pairs={{0,8},{8,0},{16,24},{24,16},{1,9},{9,1},{17,25},{25,17},{2,10},{10... | collective-permute-start | bytes 49160 | tf_op jit(solution)/shard_map/ppermute | solution.py:434
  100.4 1.2 %collective-permute-start.24 = (f32[8,512]{1,0:T(8,128)S(1)}, f32[8,512]{1,0:T(8,128)S(1)}, u32[]{:S(2)}, u32[]{:S(2)}) collective-permute-start(f32[8,512]{1,0:T(8,128)S(1)} %field.5.own_ref), channel_id=1, source_target_pairs={{0,1},{1,0},{2,3},{3,2},{4,5},{5,4},{6,7},{7,6},{8,9},{9,8},{10,11... | collective-permute-start | bytes 49160 | tf_op jit(solution)/shard_map/ppermute | solution.py:434
  101.6 5.4 %collective-permute-start.27 = (bf16[8,512]{1,0:T(8,128)(2,1)S(1)}, bf16[8,512]{1,0:T(8,128)(2,1)S(1)}, u32[]{:S(2)}, u32[]{:S(2)}) collective-permute-start(bf16[8,512]{1,0:T(8,128)(2,1)S(1)} %pair.5.refs_0_), channel_id=1, source_target_pairs={{0,6},{2,4},{4,2},{6,0},{1,7},{3,5},{5,3},{7,1},{8,14},{10,12},{12... | collective-permute-start | bytes 24584 | tf_op jit(solution)/shard_map/ppermute | solution.py:434
  102.9 4.5 %collective-permute-start.26 = (bf16[8,512]{1,0:T(8,128)(2,1)S(1)}, bf16[8,512]{1,0:T(8,128)(2,1)S(1)}, u32[]{:S(2)}, u32[]{:S(2)}) collective-permute-start(bf16[8,512]{1,0:T(8,128)(2,1)S(1)} %pair.5.refs_0_), channel_id=1, source_target_pairs={{0,4},{2,6},{4,0},{6,2},{1,5},{3,7},{5,1},{7,3},{8,12},{10,14},{12... | collective-permute-start | bytes 24584 | tf_op jit(solution)/shard_map/ppermute | solution.py:434
  103.7 4.0 %collective-permute-start.25 = (bf16[8,512]{1,0:T(8,128)(2,1)S(1)}, bf16[8,512]{1,0:T(8,128)(2,1)S(1)}, u32[]{:S(2)}, u32[]{:S(2)}) collective-permute-start(bf16[8,512]{1,0:T(8,128)(2,1)S(1)} %pair.5.refs_0_), channel_id=1, source_target_pairs={{0,2},{2,0},{4,6},{6,4},{1,3},{3,1},{5,7},{7,5},{8,10},{10,8},{12,... | collective-permute-start | bytes 24584 | tf_op jit(solution)/shard_map/ppermute | solution.py:434
  108.2 4.7 %collective-permute-start.30 = (f32[8,128]{1,0:T(8,128)S(1)}, f32[8,128]{1,0:T(8,128)S(1)}, u32[]{:S(2)}, u32[]{:S(2)}) collective-permute-start(f32[8,128]{1,0:T(8,128)S(1)} %get-tuple-element.64.refs_0_), channel_id=1, source_target_pairs={{0,24},{8,16},{16,8},{24,0},{1,25},{9,17},{17,9},{25,1},{2,26},{10... | collective-permute-start | bytes 12296 | tf_op jit(solution)/shard_map/ppermute | solution.py:434
  109.7 3.6 %collective-permute-start.29 = (f32[8,128]{1,0:T(8,128)S(1)}, f32[8,128]{1,0:T(8,128)S(1)}, u32[]{:S(2)}, u32[]{:S(2)}) collective-permute-start(f32[8,128]{1,0:T(8,128)S(1)} %get-tuple-element.64.refs_0_), channel_id=1, source_target_pairs={{0,16},{8,24},{16,0},{24,8},{1,17},{9,25},{17,1},{25,9},{2,18},{10... | collective-permute-start | bytes 12296 | tf_op jit(solution)/shard_map/ppermute | solution.py:434
  111.2 3.6 %collective-permute-start.28 = (f32[8,128]{1,0:T(8,128)S(1)}, f32[8,128]{1,0:T(8,128)S(1)}, u32[]{:S(2)}, u32[]{:S(2)}) collective-permute-start(f32[8,128]{1,0:T(8,128)S(1)} %get-tuple-element.64.refs_0_), channel_id=1, source_target_pairs={{0,8},{8,0},{16,24},{24,16},{1,9},{9,1},{17,25},{25,17},{2,10},{10... | collective-permute-start | bytes 12296 | tf_op jit(solution)/shard_map/ppermute | solution.py:434

commit v7 on v6

--- a/solution.py
+++ b/solution.py
@@ -433,6 +433,10 @@
     def across(x, axis, size, distance):
         return lax.ppermute(x, axis, [(i, i ^ distance) for i in range(size)])
 
+    def farthest_first(pieces):
+        order = sorted(range(len(pieces)), key=lambda at: -at.bit_count())
+        return [pieces[at] for at in order]
+
     def swap(pieces, axis="kpt"):
         return [pieces[0]] + [
             across(piece, axis, len(pieces), at) for at, piece in enumerate(pieces) if at
@@ -501,7 +505,7 @@
             before = results[-1]
         (direct,) = call(
             functools.partial(field_kernel, s, first),
-            (*swap(results[:groups])[::-1], pair_left),
+            (*farthest_first(swap(results[:groups])), pair_left),
             [state],
             "field",
         )

time: 116 us -> 115 us (level)
  no operation moved by 1% of the time
where the time goes in v7:
time: 115 us
  blocking collectives  36.1 us (31%)
  starting transfers between devices  34.6 us (30%)
  Pallas kernels  22.8 us (20%)
  waiting for transfers between devices  20.8 us (18%)
    all_to_all x3, blocking collectives, exchange(): return lax.all_to_all(x, axes, 0, 0, tiled=True)  36.1 us
    ppermute x31, starting transfers between devices, across(): return lax.ppermute(x, axis, [(i, i ^ distance) for i in range(size)])  34.6 us
    pallas_call x21, Pallas kernels, call(): pl.pallas_call(body, out_shape=[jax.ShapeDtypeStruct(shape, dtype) for sh...  22.8 us
    ppermute x31, waiting for transfers between devices, across(): return lax.ppermute(x, axis, [(i, i ^ distance) for i in range(size)])  20.8 us
  transfers between devices with their start and end apart: 31, of which 23 were waited for; matrix products, arithmetic and copies ran while one was open for 0% of the time, Pallas kernels for 7%

profile of v7, /device:TPU:0, one launch (start us, length us, event | category | flops | bytes accessed | tf_op | source)
XLA Modules:
  0.0 115.3 jit_solution(5629991036553053267)
XLA Ops:
  0.7 1.0 begin.1.own_ref
  1.6 0.6 collective-permute-start
  2.2 0.8 collective-permute-done.other_ref
  3.0 4.9 %collective-permute-start.3 = (f32[32,128]{1,0:T(8,128)S(1)}, f32[32,128]{1,0:T(8,128)S(1)}, u32[]{:S(2)}, u32[]{:S(2)}) collective-permute-start(f32[32,128]{1,0:T(8,128)S(1)} %stack.1.refs_0_), channel_id=1, source_target_pairs={{0,6},{2,4},{4,2},{6,0},{1,7},{3,5},{5,3},{7,1},{8,14},{10,12},{12... | collective-permute-start | bytes 49160 | tf_op jit(solution)/shard_map/ppermute | solution.py:434
  7.9 0.6 collective-permute-start.1
  9.0 0.7 collective-permute-done.3.refs_3_
  9.7 2.9 %collective-permute-done.2.refs_2_ = f32[32,128]{1,0:T(8,128)S(1)} collective-permute-done((f32[32,128]{1,0:T(8,128)S(1)}, f32[32,128]{1,0:T(8,128)S(1)}, u32[]{:S(2)}, u32[]{:S(2)}) %collective-permute-start.2) | collective-permute-done | bytes 16416 | tf_op jit(solution)/shard_map/ppermute | solution.py:434
  12.6 0.5 unpack.1
  13.1 12.4 %all_to_all.15.packet_ref.refs_1_ = bf16[32,9,2,128]{3,2,1,0:T(2,128)(2,1)S(1)} all-to-all(bf16[32,9,2,128]{3,2,1,0:T(2,128)(2,1)S(1)} %get-tuple-element.39), channel_id=1, replica_groups=mesh['kpt'=4,'z'=4,'core'=2] {'kpt','z','core'}, dimensions={0} | all-to-all | bytes 294912 | tf_op jit(solution)/shard_map/all_to_all | solution.py:431
  25.5 0.4 collective-permute-start.4
  25.9 2.4 %half.3.refs_0_ = f32[4,32,512]{2,1,0:T(8,128)S(1)} custom-call(bf16[32,9,2,128]{3,2,1,0:T(2,128)(2,1)S(1)} %all_to_all.15.packet_ref.refs_1_, bf16[4,512,4096]{2,1,0:T(8,128)(2,1)S(1)} %bitcast.2), custom_call_target="tpu_custom_call" | custom-call | flops 10000000000 | bytes 39062500 | tf_op jit(solution)/shard_map/half/pallas_call | solution.py:399
  28.3 2.6 %screen.3 = (f32[8,512]{1,0:T(8,128)S(1)}, f32[8,512]{1,0:T(8,128)S(1)}, f32[8,512]{1,0:T(8,128)S(1)}, f32[8,512]{1,0:T(8,128)S(1)}, f32[4,32,512]{2,1,0:T(8,128)S(1)}) custom-call(f32[4,32,512]{2,1,0:T(8,128)S(1)} %half.3.refs_0_, bf16[32,9,2,128]{3,2,1,0:T(2,128)(2,1)S(1)} %all_to_all.15.packet_ref.refs_1_, ...), custom_call_target="tpu_custom_call" | custom-call | tf_op jit(solution)/shard_map/screen/pallas_call | solution.py:399
  30.9 0.7 collective-permute-start.5
  31.6 1.3 %collective-permute-start.6 = (f32[8,512]{1,0:T(8,128)S(1)}, f32[8,512]{1,0:T(8,128)S(1)}, u32[]{:S(2)}, u32[]{:S(2)}) collective-permute-start(f32[8,512]{1,0:T(8,128)S(1)} %get-tuple-element.41), channel_id=1, source_target_pairs={{0,8},{8,0},{16,24},{24,16},{1,9},{9,1},{17,25},{25,17},{2,10},{10... | collective-permute-start | bytes 49160 | tf_op jit(solution)/shard_map/ppermute | solution.py:434
  33.0 1.5 %collective-permute-start.7 = (f32[8,512]{1,0:T(8,128)S(1)}, f32[8,512]{1,0:T(8,128)S(1)}, u32[]{:S(2)}, u32[]{:S(2)}) collective-permute-start(f32[8,512]{1,0:T(8,128)S(1)} %get-tuple-element.42), channel_id=1, source_target_pairs={{0,16},{8,24},{16,0},{24,8},{1,17},{9,25},{17,1},{25,9},{2,18},{10... | collective-permute-start | bytes 49160 | tf_op jit(solution)/shard_map/ppermute | solution.py:434
  34.4 1.2 %collective-permute-done.5.refs_0_ = f32[8,512]{1,0:T(8,128)S(1)} collective-permute-done((f32[8,512]{1,0:T(8,128)S(1)}, f32[8,512]{1,0:T(8,128)S(1)}, u32[]{:S(2)}, u32[]{:S(2)}) %collective-permute-start.5) | collective-permute-done | bytes 16416 | tf_op jit(solution)/shard_map/ppermute | solution.py:434
  35.6 1.1 collective-permute-done.7.refs_2_
  36.7 0.6 field.3.own_ref
  37.3 1.2 %collective-permute-done.8.other_ref = f32[8,512]{1,0:T(8,128)S(1)} collective-permute-done((f32[8,512]{1,0:T(8,128)S(1)}, f32[8,512]{1,0:T(8,128)S(1)}, u32[]{:S(2)}, u32[]{:S(2)}) %collective-permute-start.8) | collective-permute-done | bytes 16416 | tf_op jit(solution)/shard_map/ppermute | solution.py:434
  38.5 1.1 collective-permute-start.11
  39.7 0.9 collective-permute-start.10
  40.5 2.4 %collective-permute-start.9 = (bf16[8,512]{1,0:T(8,128)(2,1)S(1)}, bf16[8,512]{1,0:T(8,128)(2,1)S(1)}, u32[]{:S(2)}, u32[]{:S(2)}) collective-permute-start(bf16[8,512]{1,0:T(8,128)(2,1)S(1)} %pair.3.refs_0_), channel_id=1, source_target_pairs={{0,2},{2,0},{4,6},{6,4},{1,3},{3,1},{5,7},{7,5},{8,10},{10,8},{12,... | collective-permute-start | bytes 24584 | tf_op jit(solution)/shard_map/ppermute | solution.py:434
  42.9 1.1 collective-permute-done.11.refs_3_
  44.2 0.4 collective-permute-done.9.refs_1_
  44.6 0.8 apply.3
  45.3 11.8 %all_to_all.16.packet_ref.refs_1_ = bf16[32,9,2,128]{3,2,1,0:T(2,128)(2,1)S(1)} all-to-all(bf16[32,9,2,128]{3,2,1,0:T(2,128)(2,1)S(1)} %get-tuple-element.47), channel_id=1, replica_groups=mesh['kpt'=4,'z'=4,'core'=2] {'kpt','z','core'}, dimensions={0} | all-to-all | bytes 294912 | tf_op jit(solution)/shard_map/all_to_all | solution.py:431
  57.2 0.4 collective-permute-start.12
  57.5 2.4 %half.4.refs_0_ = f32[4,32,512]{2,1,0:T(8,128)S(1)} custom-call(bf16[32,9,2,128]{3,2,1,0:T(2,128)(2,1)S(1)} %all_to_all.16.packet_ref.refs_1_, bf16[4,512,4096]{2,1,0:T(8,128)(2,1)S(1)} %bitcast.2), custom_call_target="tpu_custom_call" | custom-call | flops 10000000000 | bytes 39062500 | tf_op jit(solution)/shard_map/half/pallas_call | solution.py:399
  59.9 2.6 %screen.4 = (f32[8,512]{1,0:T(8,128)S(1)}, f32[8,512]{1,0:T(8,128)S(1)}, f32[8,512]{1,0:T(8,128)S(1)}, f32[8,512]{1,0:T(8,128)S(1)}, f32[8,128]{1,0:T(8,128)S(1)}, /*index=5*/f32[4,32,512]{2,1,0:T(8,128)S(1)}) custom-call(f32[4,32,512]{2,1,0:T(8,128)S(1)} %half.4.refs_0_, bf16[32,9,2,128]{3,2,1,0:T(2,128)(2,1)S(1)} %all_to_all.16.packet_ref.refs_1_, ...), custom_call_target="tpu_custom_call" | custom-call | tf_op jit(solution)/shard_map/screen/pallas_call | solution.py:399
  62.5 0.7 collective-permute-start.13
  63.2 1.3 %collective-permute-start.14 = (f32[8,512]{1,0:T(8,128)S(1)}, f32[8,512]{1,0:T(8,128)S(1)}, u32[]{:S(2)}, u32[]{:S(2)}) collective-permute-start(f32[8,512]{1,0:T(8,128)S(1)} %get-tuple-element.50), channel_id=1, source_target_pairs={{0,8},{8,0},{16,24},{24,16},{1,9},{9,1},{17,25},{25,17},{2,10},{10... | collective-permute-start | bytes 49160 | tf_op jit(solution)/shard_map/ppermute | solution.py:434
  64.5 1.5 %collective-permute-start.15 = (f32[8,512]{1,0:T(8,128)S(1)}, f32[8,512]{1,0:T(8,128)S(1)}, u32[]{:S(2)}, u32[]{:S(2)}) collective-permute-start(f32[8,512]{1,0:T(8,128)S(1)} %get-tuple-element.51), channel_id=1, source_target_pairs={{0,16},{8,24},{16,0},{24,8},{1,17},{9,25},{17,1},{25,9},{2,18},{10... | collective-permute-start | bytes 49160 | tf_op jit(solution)/shard_map/ppermute | solution.py:434
  66.0 1.2 %collective-permute-done.13.refs_0_ = f32[8,512]{1,0:T(8,128)S(1)} collective-permute-done((f32[8,512]{1,0:T(8,128)S(1)}, f32[8,512]{1,0:T(8,128)S(1)}, u32[]{:S(2)}, u32[]{:S(2)}) %collective-permute-start.13) | collective-permute-done | bytes 16416 | tf_op jit(solution)/shard_map/ppermute | solution.py:434
  67.2 1.1 collective-permute-done.15.refs_2_
  68.3 0.6 field.4.own_ref
  68.9 1.2 %collective-permute-done.16.other_ref = f32[8,512]{1,0:T(8,128)S(1)} collective-permute-done((f32[8,512]{1,0:T(8,128)S(1)}, f32[8,512]{1,0:T(8,128)S(1)}, u32[]{:S(2)}, u32[]{:S(2)}) %collective-permute-start.16) | collective-permute-done | bytes 16416 | tf_op jit(solution)/shard_map/ppermute | solution.py:434
  70.1 1.1 collective-permute-start.19
  71.3 0.9 collective-permute-start.18
  72.1 2.4 %collective-permute-start.17 = (bf16[8,512]{1,0:T(8,128)(2,1)S(1)}, bf16[8,512]{1,0:T(8,128)(2,1)S(1)}, u32[]{:S(2)}, u32[]{:S(2)}) collective-permute-start(bf16[8,512]{1,0:T(8,128)(2,1)S(1)} %pair.4.refs_0_), channel_id=1, source_target_pairs={{0,2},{2,0},{4,6},{6,4},{1,3},{3,1},{5,7},{7,5},{8,10},{10,8},{12,... | collective-permute-start | bytes 24584 | tf_op jit(solution)/shard_map/ppermute | solution.py:434
  74.5 1.1 collective-permute-done.19.refs_3_
  76.1 0.7 apply.4
  76.9 11.8 %all_to_all.17.packet_ref.refs_1_ = bf16[32,9,2,128]{3,2,1,0:T(2,128)(2,1)S(1)} all-to-all(bf16[32,9,2,128]{3,2,1,0:T(2,128)(2,1)S(1)} %get-tuple-element.55), channel_id=1, replica_groups=mesh['kpt'=4,'z'=4,'core'=2] {'kpt','z','core'}, dimensions={0} | all-to-all | bytes 294912 | tf_op jit(solution)/shard_map/all_to_all | solution.py:431
  88.7 0.4 collective-permute-start.20
  89.1 2.4 %half.5.refs_0_ = f32[4,32,512]{2,1,0:T(8,128)S(1)} custom-call(bf16[32,9,2,128]{3,2,1,0:T(2,128)(2,1)S(1)} %all_to_all.17.packet_ref.refs_1_, bf16[4,512,4096]{2,1,0:T(8,128)(2,1)S(1)} %bitcast.2), custom_call_target="tpu_custom_call" | custom-call | flops 10000000000 | bytes 39062500 | tf_op jit(solution)/shard_map/half/pallas_call | solution.py:399
  91.5 2.6 %screen.5 = (f32[8,512]{1,0:T(8,128)S(1)}, f32[8,512]{1,0:T(8,128)S(1)}, f32[8,512]{1,0:T(8,128)S(1)}, f32[8,512]{1,0:T(8,128)S(1)}, f32[8,128]{1,0:T(8,128)S(1)}) custom-call(f32[4,32,512]{2,1,0:T(8,128)S(1)} %half.5.refs_0_, bf16[32,9,2,128]{3,2,1,0:T(2,128)(2,1)S(1)} %all_to_all.17.packet_ref.refs_1_, ...), custom_call_target="tpu_custom_call" | custom-call | tf_op jit(solution)/shard_map/screen/pallas_call | solution.py:399
  94.0 0.7 collective-permute-start.21
  94.7 1.3 %collective-permute-start.22 = (f32[8,512]{1,0:T(8,128)S(1)}, f32[8,512]{1,0:T(8,128)S(1)}, u32[]{:S(2)}, u32[]{:S(2)}) collective-permute-start(f32[8,512]{1,0:T(8,128)S(1)} %get-tuple-element.58), channel_id=1, source_target_pairs={{0,8},{8,0},{16,24},{24,16},{1,9},{9,1},{17,25},{25,17},{2,10},{10... | collective-permute-start | bytes 49160 | tf_op jit(solution)/shard_map/ppermute | solution.py:434
  96.1 1.5 %collective-permute-start.23 = (f32[8,512]{1,0:T(8,128)S(1)}, f32[8,512]{1,0:T(8,128)S(1)}, u32[]{:S(2)}, u32[]{:S(2)}) collective-permute-start(f32[8,512]{1,0:T(8,128)S(1)} %get-tuple-element.59), channel_id=1, source_target_pairs={{0,16},{8,24},{16,0},{24,8},{1,17},{9,25},{17,1},{25,9},{2,18},{10... | collective-permute-start | bytes 49160 | tf_op jit(solution)/shard_map/ppermute | solution.py:434
  97.6 1.2 %collective-permute-done.21.refs_0_ = f32[8,512]{1,0:T(8,128)S(1)} collective-permute-done((f32[8,512]{1,0:T(8,128)S(1)}, f32[8,512]{1,0:T(8,128)S(1)}, u32[]{:S(2)}, u32[]{:S(2)}) %collective-permute-start.21) | collective-permute-done | bytes 16416 | tf_op jit(solution)/shard_map/ppermute | solution.py:434
  98.7 1.1 collective-permute-done.23.refs_2_
  99.8 0.6 field.5.own_ref
  100.5 1.2 %collective-permute-done.24.other_ref = f32[8,512]{1,0:T(8,128)S(1)} collective-permute-done((f32[8,512]{1,0:T(8,128)S(1)}, f32[8,512]{1,0:T(8,128)S(1)}, u32[]{:S(2)}, u32[]{:S(2)}) %collective-permute-start.24) | collective-permute-done | bytes 16416 | tf_op jit(solution)/shard_map/ppermute | solution.py:434
  101.7 1.1 collective-permute-start.27
  102.8 0.9 collective-permute-start.26
  103.7 2.4 %collective-permute-start.25 = (bf16[8,512]{1,0:T(8,128)(2,1)S(1)}, bf16[8,512]{1,0:T(8,128)(2,1)S(1)}, u32[]{:S(2)}, u32[]{:S(2)}) collective-permute-start(bf16[8,512]{1,0:T(8,128)(2,1)S(1)} %pair.5.refs_0_), channel_id=1, source_target_pairs={{0,2},{2,0},{4,6},{6,4},{1,3},{3,1},{5,7},{7,5},{8,10},{10,8},{12,... | collective-permute-start | bytes 24584 | tf_op jit(solution)/shard_map/ppermute | solution.py:434
  106.1 1.1 collective-permute-done.27.refs_3_
  107.7 0.5 apply.5
  108.2 1.4 %collective-permute-start.30 = (f32[8,128]{1,0:T(8,128)S(1)}, f32[8,128]{1,0:T(8,128)S(1)}, u32[]{:S(2)}, u32[]{:S(2)}) collective-permute-start(f32[8,128]{1,0:T(8,128)S(1)} %get-tuple-element.64.refs_0_), channel_id=1, source_target_pairs={{0,24},{8,16},{16,8},{24,0},{1,25},{9,17},{17,9},{25,1},{2,26},{10... | collective-permute-start | bytes 12296 | tf_op jit(solution)/shard_map/ppermute | solution.py:434
  109.7 0.7 collective-permute-start.29
  110.4 1.3 %collective-permute-start.28 = (f32[8,128]{1,0:T(8,128)S(1)}, f32[8,128]{1,0:T(8,128)S(1)}, u32[]{:S(2)}, u32[]{:S(2)}) collective-permute-start(f32[8,128]{1,0:T(8,128)S(1)} %get-tuple-element.64.refs_0_), channel_id=1, source_target_pairs={{0,8},{8,0},{16,24},{24,16},{1,9},{9,1},{17,25},{25,17},{2,10},{10... | collective-permute-start | bytes 12296 | tf_op jit(solution)/shard_map/ppermute | solution.py:434
  111.7 1.1 own.1
  112.9 0.4 collective-permute-done.29.refs_2_
  113.3 0.7 collective-permute-done.28.refs_1_
  114.0 1.1 end.1
  (39 shorter events, 1.8 us)
Async XLA Ops:
  0.6 7.9 %copy-start.2 = (s32[16,16]{1,0:T(8,128)S(1)}, s32[16,16]{1,0:T(8,128)}, u32[]{:S(2)}) copy-start(s32[16,16]{1,0:T(8,128)} %mi_ref.1) | copy-start | bytes 3076
  0.6 11.9 %copy-start.1 = (bf16[4,512,512]{2,1,0:T(8,128)(2,1)S(1)}, bf16[4,512,512]{2,1,0:T(8,128)(2,1)}, u32[]{:S(2)}) copy-start(bf16[4,512,512]{2,1,0:T(8,128)(2,1)} %refs_8_.3) | copy-start | bytes 6291460
  1.6 1.4 %collective-permute-start = (f32[16,128]{1,0:T(8,128)S(1)}, f32[16,128]{1,0:T(8,128)S(1)}, u32[]{:S(2)}, u32[]{:S(2)}) collective-permute-start(f32[16,128]{1,0:T(8,128)S(1)} %begin.1.own_ref), channel_id=1, source_target_pairs={{0,1},{1,0},{2,3},{3,2},{4,5},{5,4},{6,7},{7,6},{8,9},{9,8},{10,11... | collective-permute-start | bytes 24584 | tf_op jit(solution)/shard_map/ppermute | solution.py:434
  3.0 6.6 %collective-permute-start.3 = (f32[32,128]{1,0:T(8,128)S(1)}, f32[32,128]{1,0:T(8,128)S(1)}, u32[]{:S(2)}, u32[]{:S(2)}) collective-permute-start(f32[32,128]{1,0:T(8,128)S(1)} %stack.1.refs_0_), channel_id=1, source_target_pairs={{0,6},{2,4},{4,2},{6,0},{1,7},{3,5},{5,3},{7,1},{8,14},{10,12},{12... | collective-permute-start | bytes 49160 | tf_op jit(solution)/shard_map/ppermute | solution.py:434
  7.9 4.6 %collective-permute-start.2 = (f32[32,128]{1,0:T(8,128)S(1)}, f32[32,128]{1,0:T(8,128)S(1)}, u32[]{:S(2)}, u32[]{:S(2)}) collective-permute-start(f32[32,128]{1,0:T(8,128)S(1)} %stack.1.refs_0_), channel_id=1, source_target_pairs={{0,4},{2,6},{4,0},{6,2},{1,5},{3,7},{5,1},{7,3},{8,12},{10,14},{12... | collective-permute-start | bytes 49160 | tf_op jit(solution)/shard_map/ppermute | solution.py:434
  7.9 4.6 %collective-permute-start.1 = (f32[32,128]{1,0:T(8,128)S(1)}, f32[32,128]{1,0:T(8,128)S(1)}, u32[]{:S(2)}, u32[]{:S(2)}) collective-permute-start(f32[32,128]{1,0:T(8,128)S(1)} %stack.1.refs_0_), channel_id=1, source_target_pairs={{0,2},{2,0},{4,6},{6,4},{1,3},{3,1},{5,7},{7,5},{8,10},{10,8},{12,... | collective-permute-start | bytes 49160 | tf_op jit(solution)/shard_map/ppermute | solution.py:434
  8.6 17.3 %slice-start = ((s8[16777216]{0:T(1024)(128)(4,1)}), s8[4194304]{0:T(1024)(128)(4,1)S(1)}, s32[]{:S(2)}) async-start(s8[16777216]{0:T(1024)(128)(4,1)} %bitcast.1), calls=%async_computation.3 | async-start | bytes 8388608
  8.9 17.0 %slice-start.1 = ((s8[16777216]{0:T(1024)(128)(4,1)}), s8[4194304]{0:T(1024)(128)(4,1)S(1)}, s32[]{:S(2)}) async-start(s8[16777216]{0:T(1024)(128)(4,1)} %bitcast.1), calls=%async_computation.4 | async-start | bytes 8388608
  8.9 17.0 %slice-start.2 = ((s8[16777216]{0:T(1024)(128)(4,1)}), s8[4194304]{0:T(1024)(128)(4,1)S(1)}, s32[]{:S(2)}) async-start(s8[16777216]{0:T(1024)(128)(4,1)} %bitcast.1), calls=%async_computation.5 | async-start | bytes 8388608
  9.0 17.0 %slice-start.3 = ((s8[16777216]{0:T(1024)(128)(4,1)}), s8[4194304]{0:T(1024)(128)(4,1)S(1)}, s32[]{:S(2)}) async-start(s8[16777216]{0:T(1024)(128)(4,1)} %bitcast.1), calls=%async_computation.6 | async-start | bytes 8388608
  25.5 2.8 %collective-permute-start.4 = (bf16[32,9,2,128]{3,2,1,0:T(2,128)(2,1)S(1)}, bf16[32,9,2,128]{3,2,1,0:T(2,128)(2,1)S(1)}, u32[]{:S(2)}, u32[]{:S(2)}) collective-permute-start(bf16[32,9,2,128]{3,2,1,0:T(2,128)(2,1)S(1)} %all_to_all.15.packet_ref.refs_1_), channel_id=1, source_target_pairs={{0,1},{1,0},{2,3},{3,2},{4,5},{5,4},{6,7},{7,6},{8,9},{9,8},{10,11... | collective-permute-start | bytes 442376 | tf_op jit(solution)/shard_map/ppermute | solution.py:434
  28.3 8.4 %copy-start = (bf16[4,512,512]{2,1,0:T(8,128)(2,1)S(1)}, bf16[4,512,512]{2,1,0:T(8,128)(2,1)}, u32[]{:S(2)}) copy-start(bf16[4,512,512]{2,1,0:T(8,128)(2,1)} %refs_4_.11) | copy-start | bytes 6291460
  30.9 13.7 %copy-start.3 = (f32[2]{0:T(128)S(1)}, f32[2]{0:T(128)}, u32[]{:S(2)}) copy-start(f32[2]{0:T(128)} %param.11) | copy-start | bytes 28
  30.9 4.7 %collective-permute-start.5 = (f32[8,512]{1,0:T(8,128)S(1)}, f32[8,512]{1,0:T(8,128)S(1)}, u32[]{:S(2)}, u32[]{:S(2)}) collective-permute-start(f32[8,512]{1,0:T(8,128)S(1)} %get-tuple-element.40), channel_id=1, source_target_pairs={{0,24},{8,16},{16,8},{24,0},{1,25},{9,17},{17,9},{25,1},{2,26},{10... | collective-permute-start | bytes 49160 | tf_op jit(solution)/shard_map/ppermute | solution.py:434
  31.6 4.0 %collective-permute-start.6 = (f32[8,512]{1,0:T(8,128)S(1)}, f32[8,512]{1,0:T(8,128)S(1)}, u32[]{:S(2)}, u32[]{:S(2)}) collective-permute-start(f32[8,512]{1,0:T(8,128)S(1)} %get-tuple-element.41), channel_id=1, source_target_pairs={{0,8},{8,0},{16,24},{24,16},{1,9},{9,1},{17,25},{25,17},{2,10},{10... | collective-permute-start | bytes 49160 | tf_op jit(solution)/shard_map/ppermute | solution.py:434
  33.0 3.7 %collective-permute-start.7 = (f32[8,512]{1,0:T(8,128)S(1)}, f32[8,512]{1,0:T(8,128)S(1)}, u32[]{:S(2)}, u32[]{:S(2)}) collective-permute-start(f32[8,512]{1,0:T(8,128)S(1)} %get-tuple-element.42), channel_id=1, source_target_pairs={{0,16},{8,24},{16,0},{24,8},{1,17},{9,25},{17,1},{25,9},{2,18},{10... | collective-permute-start | bytes 49160 | tf_op jit(solution)/shard_map/ppermute | solution.py:434
  37.3 1.2 %collective-permute-start.8 = (f32[8,512]{1,0:T(8,128)S(1)}, f32[8,512]{1,0:T(8,128)S(1)}, u32[]{:S(2)}, u32[]{:S(2)}) collective-permute-start(f32[8,512]{1,0:T(8,128)S(1)} %field.3.own_ref), channel_id=1, source_target_pairs={{0,1},{1,0},{2,3},{3,2},{4,5},{5,4},{6,7},{7,6},{8,9},{9,8},{10,11... | collective-permute-start | bytes 49160 | tf_op jit(solution)/shard_map/ppermute | solution.py:434
  38.5 5.4 %collective-permute-start.11 = (bf16[8,512]{1,0:T(8,128)(2,1)S(1)}, bf16[8,512]{1,0:T(8,128)(2,1)S(1)}, u32[]{:S(2)}, u32[]{:S(2)}) collective-permute-start(bf16[8,512]{1,0:T(8,128)(2,1)S(1)} %pair.3.refs_0_), channel_id=1, source_target_pairs={{0,6},{2,4},{4,2},{6,0},{1,7},{3,5},{5,3},{7,1},{8,14},{10,12},{12... | collective-permute-start | bytes 24584 | tf_op jit(solution)/shard_map/ppermute | solution.py:434
  39.7 4.5 %collective-permute-start.10 = (bf16[8,512]{1,0:T(8,128)(2,1)S(1)}, bf16[8,512]{1,0:T(8,128)(2,1)S(1)}, u32[]{:S(2)}, u32[]{:S(2)}) collective-permute-start(bf16[8,512]{1,0:T(8,128)(2,1)S(1)} %pair.3.refs_0_), channel_id=1, source_target_pairs={{0,4},{2,6},{4,0},{6,2},{1,5},{3,7},{5,1},{7,3},{8,12},{10,14},{12... | collective-permute-start | bytes 24584 | tf_op jit(solution)/shard_map/ppermute | solution.py:434
  40.5 4.0 %collective-permute-start.9 = (bf16[8,512]{1,0:T(8,128)(2,1)S(1)}, bf16[8,512]{1,0:T(8,128)(2,1)S(1)}, u32[]{:S(2)}, u32[]{:S(2)}) collective-permute-start(bf16[8,512]{1,0:T(8,128)(2,1)S(1)} %pair.3.refs_0_), channel_id=1, source_target_pairs={{0,2},{2,0},{4,6},{6,4},{1,3},{3,1},{5,7},{7,5},{8,10},{10,8},{12,... | collective-permute-start | bytes 24584 | tf_op jit(solution)/shard_map/ppermute | solution.py:434
  57.2 2.7 %collective-permute-start.12 = (bf16[32,9,2,128]{3,2,1,0:T(2,128)(2,1)S(1)}, bf16[32,9,2,128]{3,2,1,0:T(2,128)(2,1)S(1)}, u32[]{:S(2)}, u32[]{:S(2)}) collective-permute-start(bf16[32,9,2,128]{3,2,1,0:T(2,128)(2,1)S(1)} %all_to_all.16.packet_ref.refs_1_), channel_id=1, source_target_pairs={{0,1},{1,0},{2,3},{3,2},{4,5},{5,4},{6,7},{7,6},{8,9},{9,8},{10,11... | collective-permute-start | bytes 442376 | tf_op jit(solution)/shard_map/ppermute | solution.py:434
  62.5 4.7 %collective-permute-start.13 = (f32[8,512]{1,0:T(8,128)S(1)}, f32[8,512]{1,0:T(8,128)S(1)}, u32[]{:S(2)}, u32[]{:S(2)}) collective-permute-start(f32[8,512]{1,0:T(8,128)S(1)} %get-tuple-element.49), channel_id=1, source_target_pairs={{0,24},{8,16},{16,8},{24,0},{1,25},{9,17},{17,9},{25,1},{2,26},{10... | collective-permute-start | bytes 49160 | tf_op jit(solution)/shard_map/ppermute | solution.py:434
  63.2 4.0 %collective-permute-start.14 = (f32[8,512]{1,0:T(8,128)S(1)}, f32[8,512]{1,0:T(8,128)S(1)}, u32[]{:S(2)}, u32[]{:S(2)}) collective-permute-start(f32[8,512]{1,0:T(8,128)S(1)} %get-tuple-element.50), channel_id=1, source_target_pairs={{0,8},{8,0},{16,24},{24,16},{1,9},{9,1},{17,25},{25,17},{2,10},{10... | collective-permute-start | bytes 49160 | tf_op jit(solution)/shard_map/ppermute | solution.py:434
  64.5 3.7 %collective-permute-start.15 = (f32[8,512]{1,0:T(8,128)S(1)}, f32[8,512]{1,0:T(8,128)S(1)}, u32[]{:S(2)}, u32[]{:S(2)}) collective-permute-start(f32[8,512]{1,0:T(8,128)S(1)} %get-tuple-element.51), channel_id=1, source_target_pairs={{0,16},{8,24},{16,0},{24,8},{1,17},{9,25},{17,1},{25,9},{2,18},{10... | collective-permute-start | bytes 49160 | tf_op jit(solution)/shard_map/ppermute | solution.py:434
  68.9 1.2 %collective-permute-start.16 = (f32[8,512]{1,0:T(8,128)S(1)}, f32[8,512]{1,0:T(8,128)S(1)}, u32[]{:S(2)}, u32[]{:S(2)}) collective-permute-start(f32[8,512]{1,0:T(8,128)S(1)} %field.4.own_ref), channel_id=1, source_target_pairs={{0,1},{1,0},{2,3},{3,2},{4,5},{5,4},{6,7},{7,6},{8,9},{9,8},{10,11... | collective-permute-start | bytes 49160 | tf_op jit(solution)/shard_map/ppermute | solution.py:434
  70.1 5.4 %collective-permute-start.19 = (bf16[8,512]{1,0:T(8,128)(2,1)S(1)}, bf16[8,512]{1,0:T(8,128)(2,1)S(1)}, u32[]{:S(2)}, u32[]{:S(2)}) collective-permute-start(bf16[8,512]{1,0:T(8,128)(2,1)S(1)} %pair.4.refs_0_), channel_id=1, source_target_pairs={{0,6},{2,4},{4,2},{6,0},{1,7},{3,5},{5,3},{7,1},{8,14},{10,12},{12... | collective-permute-start | bytes 24584 | tf_op jit(solution)/shard_map/ppermute | solution.py:434
  71.3 4.5 %collective-permute-start.18 = (bf16[8,512]{1,0:T(8,128)(2,1)S(1)}, bf16[8,512]{1,0:T(8,128)(2,1)S(1)}, u32[]{:S(2)}, u32[]{:S(2)}) collective-permute-start(bf16[8,512]{1,0:T(8,128)(2,1)S(1)} %pair.4.refs_0_), channel_id=1, source_target_pairs={{0,4},{2,6},{4,0},{6,2},{1,5},{3,7},{5,1},{7,3},{8,12},{10,14},{12... | collective-permute-start | bytes 24584 | tf_op jit(solution)/shard_map/ppermute | solution.py:434
  72.1 4.0 %collective-permute-start.17 = (bf16[8,512]{1,0:T(8,128)(2,1)S(1)}, bf16[8,512]{1,0:T(8,128)(2,1)S(1)}, u32[]{:S(2)}, u32[]{:S(2)}) collective-permute-start(bf16[8,512]{1,0:T(8,128)(2,1)S(1)} %pair.4.refs_0_), channel_id=1, source_target_pairs={{0,2},{2,0},{4,6},{6,4},{1,3},{3,1},{5,7},{7,5},{8,10},{10,8},{12,... | collective-permute-start | bytes 24584 | tf_op jit(solution)/shard_map/ppermute | solution.py:434
  88.7 2.7 %collective-permute-start.20 = (bf16[32,9,2,128]{3,2,1,0:T(2,128)(2,1)S(1)}, bf16[32,9,2,128]{3,2,1,0:T(2,128)(2,1)S(1)}, u32[]{:S(2)}, u32[]{:S(2)}) collective-permute-start(bf16[32,9,2,128]{3,2,1,0:T(2,128)(2,1)S(1)} %all_to_all.17.packet_ref.refs_1_), channel_id=1, source_target_pairs={{0,1},{1,0},{2,3},{3,2},{4,5},{5,4},{6,7},{7,6},{8,9},{9,8},{10,11... | collective-permute-start | bytes 442376 | tf_op jit(solution)/shard_map/ppermute | solution.py:434
  94.0 4.7 %collective-permute-start.21 = (f32[8,512]{1,0:T(8,128)S(1)}, f32[8,512]{1,0:T(8,128)S(1)}, u32[]{:S(2)}, u32[]{:S(2)}) collective-permute-start(f32[8,512]{1,0:T(8,128)S(1)} %get-tuple-element.57), channel_id=1, source_target_pairs={{0,24},{8,16},{16,8},{24,0},{1,25},{9,17},{17,9},{25,1},{2,26},{10... | collective-permute-start | bytes 49160 | tf_op jit(solution)/shard_map/ppermute | solution.py:434
  94.7 4.0 %collective-permute-start.22 = (f32[8,512]{1,0:T(8,128)S(1)}, f32[8,512]{1,0:T(8,128)S(1)}, u32[]{:S(2)}, u32[]{:S(2)}) collective-permute-start(f32[8,512]{1,0:T(8,128)S(1)} %get-tuple-element.58), channel_id=1, source_target_pairs={{0,8},{8,0},{16,24},{24,16},{1,9},{9,1},{17,25},{25,17},{2,10},{10... | collective-permute-start | bytes 49160 | tf_op jit(solution)/shard_map/ppermute | solution.py:434
  96.1 3.7 %collective-permute-start.23 = (f32[8,512]{1,0:T(8,128)S(1)}, f32[8,512]{1,0:T(8,128)S(1)}, u32[]{:S(2)}, u32[]{:S(2)}) collective-permute-start(f32[8,512]{1,0:T(8,128)S(1)} %get-tuple-element.59), channel_id=1, source_target_pairs={{0,16},{8,24},{16,0},{24,8},{1,17},{9,25},{17,1},{25,9},{2,18},{10... | collective-permute-start | bytes 49160 | tf_op jit(solution)/shard_map/ppermute | solution.py:434
  100.5 1.2 %collective-permute-start.24 = (f32[8,512]{1,0:T(8,128)S(1)}, f32[8,512]{1,0:T(8,128)S(1)}, u32[]{:S(2)}, u32[]{:S(2)}) collective-permute-start(f32[8,512]{1,0:T(8,128)S(1)} %field.5.own_ref), channel_id=1, source_target_pairs={{0,1},{1,0},{2,3},{3,2},{4,5},{5,4},{6,7},{7,6},{8,9},{9,8},{10,11... | collective-permute-start | bytes 49160 | tf_op jit(solution)/shard_map/ppermute | solution.py:434
  101.7 5.4 %collective-permute-start.27 = (bf16[8,512]{1,0:T(8,128)(2,1)S(1)}, bf16[8,512]{1,0:T(8,128)(2,1)S(1)}, u32[]{:S(2)}, u32[]{:S(2)}) collective-permute-start(bf16[8,512]{1,0:T(8,128)(2,1)S(1)} %pair.5.refs_0_), channel_id=1, source_target_pairs={{0,6},{2,4},{4,2},{6,0},{1,7},{3,5},{5,3},{7,1},{8,14},{10,12},{12... | collective-permute-start | bytes 24584 | tf_op jit(solution)/shard_map/ppermute | solution.py:434
  102.8 4.5 %collective-permute-start.26 = (bf16[8,512]{1,0:T(8,128)(2,1)S(1)}, bf16[8,512]{1,0:T(8,128)(2,1)S(1)}, u32[]{:S(2)}, u32[]{:S(2)}) collective-permute-start(bf16[8,512]{1,0:T(8,128)(2,1)S(1)} %pair.5.refs_0_), channel_id=1, source_target_pairs={{0,4},{2,6},{4,0},{6,2},{1,5},{3,7},{5,1},{7,3},{8,12},{10,14},{12... | collective-permute-start | bytes 24584 | tf_op jit(solution)/shard_map/ppermute | solution.py:434
  103.7 4.0 %collective-permute-start.25 = (bf16[8,512]{1,0:T(8,128)(2,1)S(1)}, bf16[8,512]{1,0:T(8,128)(2,1)S(1)}, u32[]{:S(2)}, u32[]{:S(2)}) collective-permute-start(bf16[8,512]{1,0:T(8,128)(2,1)S(1)} %pair.5.refs_0_), channel_id=1, source_target_pairs={{0,2},{2,0},{4,6},{6,4},{1,3},{3,1},{5,7},{7,5},{8,10},{10,8},{12,... | collective-permute-start | bytes 24584 | tf_op jit(solution)/shard_map/ppermute | solution.py:434
  108.2 4.7 %collective-permute-start.30 = (f32[8,128]{1,0:T(8,128)S(1)}, f32[8,128]{1,0:T(8,128)S(1)}, u32[]{:S(2)}, u32[]{:S(2)}) collective-permute-start(f32[8,128]{1,0:T(8,128)S(1)} %get-tuple-element.64.refs_0_), channel_id=1, source_target_pairs={{0,24},{8,16},{16,8},{24,0},{1,25},{9,17},{17,9},{25,1},{2,26},{10... | collective-permute-start | bytes 12296 | tf_op jit(solution)/shard_map/ppermute | solution.py:434
  109.7 3.6 %collective-permute-start.29 = (f32[8,128]{1,0:T(8,128)S(1)}, f32[8,128]{1,0:T(8,128)S(1)}, u32[]{:S(2)}, u32[]{:S(2)}) collective-permute-start(f32[8,128]{1,0:T(8,128)S(1)} %get-tuple-element.64.refs_0_), channel_id=1, source_target_pairs={{0,16},{8,24},{16,0},{24,8},{1,17},{9,25},{17,1},{25,9},{2,18},{10... | collective-permute-start | bytes 12296 | tf_op jit(solution)/shard_map/ppermute | solution.py:434
  110.4 3.6 %collective-permute-start.28 = (f32[8,128]{1,0:T(8,128)S(1)}, f32[8,128]{1,0:T(8,128)S(1)}, u32[]{:S(2)}, u32[]{:S(2)}) collective-permute-start(f32[8,128]{1,0:T(8,128)S(1)} %get-tuple-element.64.refs_0_), channel_id=1, source_target_pairs={{0,8},{8,0},{16,24},{24,16},{1,9},{9,1},{17,25},{25,17},{2,10},{10... | collective-permute-start | bytes 12296 | tf_op jit(solution)/shard_map/ppermute | solution.py:434

commit v8 on v7

--- a/solution.py
+++ b/solution.py
@@ -97,7 +97,7 @@
 
 
 def unpack_kernel(s, *refs):
-    right_ref, _, packet_ref, vector_ref, earlier_ref, levels_ref = refs[s.chips :]
+    right_ref, _, packet_ref, vector_ref, earlier_ref, levels_ref, density_ref = refs[s.chips :]
     rows = s.rows
     width = refs[0].shape[1] // 2
     pieces = in_order(lax.axis_index("z"), [ref[...] for ref in refs[: s.chips]])
@@ -108,19 +108,20 @@
                 at = 2 * rows * c + row
                 blocks.append(piece[at : at + rows, lane : lane + width])
         ref[...] = jnp.concatenate(blocks, axis=1)
-    density = project(s, (vector_ref[...].astype(BF),), right_ref)
-    send(s, density, jnp.zeros((rows, LANES), F32), packet_ref)
-
-
-def project(s, parts, right_ref):
-    x = jnp.concatenate([part.astype(F32) for part in parts], axis=0)
+    high, low = project(s, vector_ref[...], right_ref)
+    density_ref[...] = high + low
+    send(s, high, jnp.zeros((rows, LANES), F32), packet_ref)
+
+
+def project(s, x, right_ref):
+    x = jnp.concatenate([part.astype(F32) for part in high_low(x)], axis=0)
     total = None
     for k in range(s.kpoints):
         own = iota(x.shape, 0) % s.kpoints == k
         masked = jnp.where(own, x, 0.0).astype(BF)
         part = jnp.dot(masked, right_ref[k], preferred_element_type=F32)
         total = part if total is None else total + part
-    return sum(total[at : at + s.rows] for at in range(0, x.shape[0], s.rows))
+    return total[: s.rows], total[s.rows :]
 
 
 def send(s, density, sums, packet_ref):
@@ -157,59 +158,60 @@
     square = chain_rows(vector * vector, s.chains)
     cross = chain_rows(vector * applied, s.chains)
     shift = jnp.where(square > 0.0, cross / jnp.where(square > 0.0, square, 1.0), 0.0)
-    shift = shift.astype(BF).astype(F32)
-    work = applied - shift * vector
-    sums = (
-        square,
-        chain_rows(work * vector, s.chains),
-        chain_rows(work * work, s.chains),
-        shift,
-    )
+    sums = (square, cross, chain_rows(applied * applied, s.chains), shift)
     lane = iota((s.rows, LANES), 1)
     value = jnp.zeros((s.rows, LANES), F32)
     for at, item in enumerate(sums):
         value = jnp.where(lane % 4 == at, item, value)
     high, middle, low = three_pieces(value)
     packed = jnp.where(lane < 4, high, jnp.where(lane < 8, middle, low))
-    return work, packed
+    return applied, shift, packed
 
 
 def read_sums(s, tiles):
-    square, cross, work, shift = [], [], [], []
+    square, cross, whole, shift = [], [], [], []
     for tile in tiles:
         value = tile[:, 0:4] + tile[:, 4:8] + tile[:, 8:12]
-        for at, into in enumerate((square, cross, work, shift)):
+        for at, into in enumerate((square, cross, whole, shift)):
             into.append(value[:, at : at + 1])
-    alpha = sum(c + h * q for c, h, q in zip(cross, shift, square)) / s.entries
+    alpha = sum(cross) / s.entries
     offsets = [h - alpha for h in shift]
-    mean = sum(
-        w + 2.0 * o * c + o * (o * q) for w, o, c, q in zip(work, offsets, cross, square)
-    )
+    mean = sum(w + alpha * (alpha * q - 2.0 * c) for w, c, q in zip(whole, cross, square))
     beta = jnp.sqrt(jnp.maximum(mean / s.entries, 0.0) + EPSILON)
     return alpha, beta, offsets
 
 
 def later_kernel(s, *refs):
     direct_refs, refs = refs[: s.chips], refs[s.chips :]
-    work_ref, vector_ref, levels_ref, scalars_ref, right_ref = refs[:5]
-    packet_ref, new_work_ref, new_vector_ref = refs[5:]
+    work_ref, vector_ref, levels_ref, scalars_ref = refs[:4]
+    part_ref, density_ref, right_ref = refs[4:7]
+    packet_ref, new_work_ref, new_vector_ref = refs[7:10]
     vector, beta = advance(work_ref, vector_ref, scalars_ref)
+    density, _ = advance(part_ref, density_ref, scalars_ref)
     new_vector_ref[...] = vector
-    work, packed = apply_step(s, direct_refs, vector, vector_ref[...], levels_ref[...], beta)
-    new_work_ref[...] = work
-    finish_packet(s, work, packed, right_ref, packet_ref)
+    step = apply_step(s, direct_refs, vector, vector_ref[...], levels_ref[...], beta)
+    part = finish(s, step, vector, density, right_ref, packet_ref, new_work_ref)
+    for ref, value in zip(refs[10:], (part, density)):
+        ref[...] = value
 
 
 def first_kernel(s, *refs):
     direct_refs, refs = refs[: s.chips], refs[s.chips :]
-    vector_ref, earlier_ref, levels_ref, beta_ref, right_ref = refs[:5]
-    packet_ref, new_work_ref = refs[5:]
-    beta = first_beta(s, beta_ref)
-    work, packed = apply_step(
-        s, direct_refs, vector_ref[...], earlier_ref[...], levels_ref[...], beta
-    )
-    new_work_ref[...] = work
-    finish_packet(s, work, packed, right_ref, packet_ref)
+    vector_ref, earlier_ref, levels_ref, beta_ref, density_ref, right_ref = refs[:6]
+    packet_ref, new_work_ref, new_part_ref = refs[6:]
+    vector, beta = vector_ref[...], first_beta(s, beta_ref)
+    step = apply_step(s, direct_refs, vector, earlier_ref[...], levels_ref[...], beta)
+    density = density_ref[...]
+    new_part_ref[...] = finish(s, step, vector, density, right_ref, packet_ref, new_work_ref)
+
+
+def finish(s, step, vector, density, right_ref, packet_ref, new_work_ref):
+    applied, shift, packed = step
+    new_work_ref[...] = applied - shift * vector
+    high, low = project(s, applied, right_ref)
+    part = high + low - shift * density
+    send(s, part, packed, packet_ref)
+    return part
 
 
 def first_beta(s, beta_ref):
@@ -226,18 +228,16 @@
     return (work_ref[...] + offset * vector_ref[...]) / beta, beta
 
 
-def finish_packet(s, work, packed, right_ref, packet_ref):
-    send(s, project(s, high_low(work), right_ref), packed, packet_ref)
-
-
 def last_kernel(s, *refs):
     direct_refs, refs = refs[: s.chips], refs[s.chips :]
     work_ref, vector_ref, levels_ref, scalars_ref = refs[:4]
     packet_ref, new_work_ref, new_vector_ref = refs[4:]
     vector, beta = advance(work_ref, vector_ref, scalars_ref)
     new_vector_ref[...] = vector
-    work, packed = apply_step(s, direct_refs, vector, vector_ref[...], levels_ref[...], beta)
-    new_work_ref[...] = work
+    applied, shift, packed = apply_step(
+        s, direct_refs, vector, vector_ref[...], levels_ref[...], beta
+    )
+    new_work_ref[...] = applied - shift * vector
     packet_ref[...] = packed
 
 
@@ -424,6 +424,7 @@
     s.entries = float(nk * bands)
     total = groups * s.rows
     state = ((s.rows, bands), F32)
+    block = ((s.rows, width), F32)
     pairs = (s.rows * width // CORES // LANES + s.chains) // 2
     packet = ((groups * parts, pairs, 2, LANES), BF)
 
@@ -471,10 +472,10 @@
         "pick",
     )
     start = swap([start] * s.chips, "z")
-    sent, vector, earlier, levels = call(
+    sent, vector, earlier, levels, density = call(
         functools.partial(unpack_kernel, s),
         (*start, pair_right, pick),
-        [packet, state, state, state],
+        [packet, state, state, state, block],
         "unpack",
         cost=COVER,
     )
@@ -517,19 +518,20 @@
         )
         direct = swap([direct] * s.chips, "z")
         if first:
-            sent, work = call(
+            sent, work, part = call(
                 functools.partial(first_kernel, s),
-                (*direct, vector, earlier, levels, previous_beta[None], pair_right),
-                [packet, state],
+                (*direct, vector, earlier, levels, previous_beta[None], density, pair_right),
+                [packet, state, block],
                 "apply",
             )
         elif keep:
-            sent, work, vector = call(
+            sent, work, vector, *densities = call(
                 functools.partial(later_kernel, s),
-                (*direct, work, vector, levels, scalars[-1], pair_right),
-                [packet, state, state],
+                (*direct, work, vector, levels, scalars[-1], part, density, pair_right),
+                [packet, state, state] + [block, block] * (step < STEPS - 2),
                 "apply",
             )
+            part, density = densities or (None, None)
         else:
             sent, work, vector = call(
                 functools.partial(last_kernel, s),
@@ -540,11 +542,11 @@
     sums = swap([sent] * groups)
     own = (current.shape, F32)
     terms = ((s.chains, STEPS), F32)
-    block = ((s.rows, band_block), F32)
+    bands_block = ((s.rows, band_block), F32)
     own_work, own_vector, known, prior = call(
         functools.partial(own_kernel, s),
         (work, vector, *scalars),
-        [block, block, ((s.rows, LANES), F32), own],
+        [bands_block, bands_block, ((s.rows, LANES), F32), own],
         "own",
         out_specs=[VMEM] * 3 + [HBM],
         scratch=[pltpu.VMEM(*own), pltpu.SemaphoreType.DMA((1,))],

time: 115 us -> 115 us (level)
  transfers between devices with their start and end apart: 31 -> 31, of which waited for: 23 -> 23; matrix products, arithmetic and copies ran while one was open for 0% -> 0% of each run, Pallas kernels for 7% -> 8%
where the time goes in v8:
time: 115 us
  blocking collectives  36.1 us (31%)
  starting transfers between devices  34.6 us (30%)
  Pallas kernels  22.1 us (19%)
  waiting for transfers between devices  20.8 us (18%)
    all_to_all x3, blocking collectives, exchange(): return lax.all_to_all(x, axes, 0, 0, tiled=True)  36.1 us
    ppermute x31, starting transfers between devices, across(): return lax.ppermute(x, axis, [(i, i ^ distance) for i in range(size)])  34.6 us
    pallas_call x21, Pallas kernels, call(): pl.pallas_call(body, out_shape=[jax.ShapeDtypeStruct(shape, dtype) for sh...  22.1 us
    ppermute x31, waiting for transfers between devices, across(): return lax.ppermute(x, axis, [(i, i ^ distance) for i in range(size)])  20.8 us
  transfers between devices with their start and end apart: 31, of which 23 were waited for; matrix products, arithmetic and copies ran while one was open for 0% of the time, Pallas kernels for 8%

profile of v8, /device:TPU:0, one launch (start us, length us, event | category | flops | bytes accessed | tf_op | source)
XLA Modules:
  0.0 114.5 jit_solution(6310596740475594903)
XLA Ops:
  0.7 1.0 begin.1.own_ref
  1.6 0.6 collective-permute-start
  2.2 0.8 collective-permute-done.other_ref
  3.0 4.9 %collective-permute-start.3 = (f32[32,128]{1,0:T(8,128)S(1)}, f32[32,128]{1,0:T(8,128)S(1)}, u32[]{:S(2)}, u32[]{:S(2)}) collective-permute-start(f32[32,128]{1,0:T(8,128)S(1)} %stack.1.refs_0_), channel_id=1, source_target_pairs={{0,6},{2,4},{4,2},{6,0},{1,7},{3,5},{5,3},{7,1},{8,14},{10,12},{12... | collective-permute-start | bytes 49160 | tf_op jit(solution)/shard_map/ppermute | solution.py:435
  7.9 0.6 collective-permute-start.1
  9.0 0.7 collective-permute-done.3.refs_3_
  9.7 2.9 %collective-permute-done.2.refs_2_ = f32[32,128]{1,0:T(8,128)S(1)} collective-permute-done((f32[32,128]{1,0:T(8,128)S(1)}, f32[32,128]{1,0:T(8,128)S(1)}, u32[]{:S(2)}, u32[]{:S(2)}) %collective-permute-start.2) | collective-permute-done | bytes 16416 | tf_op jit(solution)/shard_map/ppermute | solution.py:435
  12.6 0.5 unpack.1
  13.1 12.4 %all_to_all.15.packet_ref.refs_1_ = bf16[32,9,2,128]{3,2,1,0:T(2,128)(2,1)S(1)} all-to-all(bf16[32,9,2,128]{3,2,1,0:T(2,128)(2,1)S(1)} %get-tuple-element.41), channel_id=1, replica_groups=mesh['kpt'=4,'z'=4,'core'=2] {'kpt','z','core'}, dimensions={0} | all-to-all | bytes 294912 | tf_op jit(solution)/shard_map/all_to_all | solution.py:432
  25.5 0.4 collective-permute-start.4
  25.9 2.4 %half.3.refs_0_ = f32[4,32,512]{2,1,0:T(8,128)S(1)} custom-call(bf16[32,9,2,128]{3,2,1,0:T(2,128)(2,1)S(1)} %all_to_all.15.packet_ref.refs_1_, bf16[4,512,4096]{2,1,0:T(8,128)(2,1)S(1)} %bitcast.2), custom_call_target="tpu_custom_call" | custom-call | flops 10000000000 | bytes 39062500 | tf_op jit(solution)/shard_map/half/pallas_call | solution.py:399
  28.3 2.6 %screen.3 = (f32[8,512]{1,0:T(8,128)S(1)}, f32[8,512]{1,0:T(8,128)S(1)}, f32[8,512]{1,0:T(8,128)S(1)}, f32[8,512]{1,0:T(8,128)S(1)}, f32[4,32,512]{2,1,0:T(8,128)S(1)}) custom-call(f32[4,32,512]{2,1,0:T(8,128)S(1)} %half.3.refs_0_, bf16[32,9,2,128]{3,2,1,0:T(2,128)(2,1)S(1)} %all_to_all.15.packet_ref.refs_1_, ...), custom_call_target="tpu_custom_call" | custom-call | tf_op jit(solution)/shard_map/screen/pallas_call | solution.py:399
  30.9 0.7 collective-permute-start.5
  31.6 1.3 %collective-permute-start.6 = (f32[8,512]{1,0:T(8,128)S(1)}, f32[8,512]{1,0:T(8,128)S(1)}, u32[]{:S(2)}, u32[]{:S(2)}) collective-permute-start(f32[8,512]{1,0:T(8,128)S(1)} %get-tuple-element.43), channel_id=1, source_target_pairs={{0,8},{8,0},{16,24},{24,16},{1,9},{9,1},{17,25},{25,17},{2,10},{10... | collective-permute-start | bytes 49160 | tf_op jit(solution)/shard_map/ppermute | solution.py:435
  32.9 1.5 %collective-permute-start.7 = (f32[8,512]{1,0:T(8,128)S(1)}, f32[8,512]{1,0:T(8,128)S(1)}, u32[]{:S(2)}, u32[]{:S(2)}) collective-permute-start(f32[8,512]{1,0:T(8,128)S(1)} %get-tuple-element.44), channel_id=1, source_target_pairs={{0,16},{8,24},{16,0},{24,8},{1,17},{9,25},{17,1},{25,9},{2,18},{10... | collective-permute-start | bytes 49160 | tf_op jit(solution)/shard_map/ppermute | solution.py:435
  34.4 1.2 %collective-permute-done.5.refs_0_ = f32[8,512]{1,0:T(8,128)S(1)} collective-permute-done((f32[8,512]{1,0:T(8,128)S(1)}, f32[8,512]{1,0:T(8,128)S(1)}, u32[]{:S(2)}, u32[]{:S(2)}) %collective-permute-start.5) | collective-permute-done | bytes 16416 | tf_op jit(solution)/shard_map/ppermute | solution.py:435
  35.6 1.1 collective-permute-done.7.refs_2_
  36.7 0.6 field.3.own_ref
  37.3 1.2 %collective-permute-done.8.other_ref = f32[8,512]{1,0:T(8,128)S(1)} collective-permute-done((f32[8,512]{1,0:T(8,128)S(1)}, f32[8,512]{1,0:T(8,128)S(1)}, u32[]{:S(2)}, u32[]{:S(2)}) %collective-permute-start.8) | collective-permute-done | bytes 16416 | tf_op jit(solution)/shard_map/ppermute | solution.py:435
  38.5 1.1 collective-permute-start.11
  39.7 0.9 collective-permute-start.10
  40.6 2.4 %collective-permute-start.9 = (bf16[8,512]{1,0:T(8,128)(2,1)S(1)}, bf16[8,512]{1,0:T(8,128)(2,1)S(1)}, u32[]{:S(2)}, u32[]{:S(2)}) collective-permute-start(bf16[8,512]{1,0:T(8,128)(2,1)S(1)} %pair.3.refs_0_), channel_id=1, source_target_pairs={{0,2},{2,0},{4,6},{6,4},{1,3},{3,1},{5,7},{7,5},{8,10},{10,8},{12,... | collective-permute-start | bytes 24584 | tf_op jit(solution)/shard_map/ppermute | solution.py:435
  42.9 1.1 collective-permute-done.11.refs_3_
  44.2 0.3 collective-permute-done.9.refs_1_
  44.6 0.6 apply.3
  45.2 11.8 %all_to_all.16.packet_ref.refs_1_ = bf16[32,9,2,128]{3,2,1,0:T(2,128)(2,1)S(1)} all-to-all(bf16[32,9,2,128]{3,2,1,0:T(2,128)(2,1)S(1)} %get-tuple-element.50), channel_id=1, replica_groups=mesh['kpt'=4,'z'=4,'core'=2] {'kpt','z','core'}, dimensions={0} | all-to-all | bytes 294912 | tf_op jit(solution)/shard_map/all_to_all | solution.py:432
  57.0 0.4 collective-permute-start.12
  57.3 2.4 %half.4.refs_0_ = f32[4,32,512]{2,1,0:T(8,128)S(1)} custom-call(bf16[32,9,2,128]{3,2,1,0:T(2,128)(2,1)S(1)} %all_to_all.16.packet_ref.refs_1_, bf16[4,512,4096]{2,1,0:T(8,128)(2,1)S(1)} %bitcast.2), custom_call_target="tpu_custom_call" | custom-call | flops 10000000000 | bytes 39062500 | tf_op jit(solution)/shard_map/half/pallas_call | solution.py:399
  59.7 2.6 %screen.4 = (f32[8,512]{1,0:T(8,128)S(1)}, f32[8,512]{1,0:T(8,128)S(1)}, f32[8,512]{1,0:T(8,128)S(1)}, f32[8,512]{1,0:T(8,128)S(1)}, f32[8,128]{1,0:T(8,128)S(1)}, /*index=5*/f32[4,32,512]{2,1,0:T(8,128)S(1)}) custom-call(f32[4,32,512]{2,1,0:T(8,128)S(1)} %half.4.refs_0_, bf16[32,9,2,128]{3,2,1,0:T(2,128)(2,1)S(1)} %all_to_all.16.packet_ref.refs_1_, ...), custom_call_target="tpu_custom_call" | custom-call | tf_op jit(solution)/shard_map/screen/pallas_call | solution.py:399
  62.3 0.7 collective-permute-start.13
  63.0 1.3 %collective-permute-start.14 = (f32[8,512]{1,0:T(8,128)S(1)}, f32[8,512]{1,0:T(8,128)S(1)}, u32[]{:S(2)}, u32[]{:S(2)}) collective-permute-start(f32[8,512]{1,0:T(8,128)S(1)} %get-tuple-element.53), channel_id=1, source_target_pairs={{0,8},{8,0},{16,24},{24,16},{1,9},{9,1},{17,25},{25,17},{2,10},{10... | collective-permute-start | bytes 49160 | tf_op jit(solution)/shard_map/ppermute | solution.py:435
  64.3 1.5 %collective-permute-start.15 = (f32[8,512]{1,0:T(8,128)S(1)}, f32[8,512]{1,0:T(8,128)S(1)}, u32[]{:S(2)}, u32[]{:S(2)}) collective-permute-start(f32[8,512]{1,0:T(8,128)S(1)} %get-tuple-element.54), channel_id=1, source_target_pairs={{0,16},{8,24},{16,0},{24,8},{1,17},{9,25},{17,1},{25,9},{2,18},{10... | collective-permute-start | bytes 49160 | tf_op jit(solution)/shard_map/ppermute | solution.py:435
  65.8 1.2 %collective-permute-done.13.refs_0_ = f32[8,512]{1,0:T(8,128)S(1)} collective-permute-done((f32[8,512]{1,0:T(8,128)S(1)}, f32[8,512]{1,0:T(8,128)S(1)}, u32[]{:S(2)}, u32[]{:S(2)}) %collective-permute-start.13) | collective-permute-done | bytes 16416 | tf_op jit(solution)/shard_map/ppermute | solution.py:435
  67.0 1.1 collective-permute-done.15.refs_2_
  68.1 0.6 field.4.own_ref
  68.7 1.2 %collective-permute-done.16.other_ref = f32[8,512]{1,0:T(8,128)S(1)} collective-permute-done((f32[8,512]{1,0:T(8,128)S(1)}, f32[8,512]{1,0:T(8,128)S(1)}, u32[]{:S(2)}, u32[]{:S(2)}) %collective-permute-start.16) | collective-permute-done | bytes 16416 | tf_op jit(solution)/shard_map/ppermute | solution.py:435
  69.9 1.1 collective-permute-start.19
  71.1 0.9 collective-permute-start.18
  72.0 2.4 %collective-permute-start.17 = (bf16[8,512]{1,0:T(8,128)(2,1)S(1)}, bf16[8,512]{1,0:T(8,128)(2,1)S(1)}, u32[]{:S(2)}, u32[]{:S(2)}) collective-permute-start(bf16[8,512]{1,0:T(8,128)(2,1)S(1)} %pair.4.refs_0_), channel_id=1, source_target_pairs={{0,2},{2,0},{4,6},{6,4},{1,3},{3,1},{5,7},{7,5},{8,10},{10,8},{12,... | collective-permute-start | bytes 24584 | tf_op jit(solution)/shard_map/ppermute | solution.py:435
  74.3 1.1 collective-permute-done.19.refs_3_
  76.0 0.5 apply.4
  76.5 11.8 %all_to_all.17.packet_ref.refs_1_ = bf16[32,9,2,128]{3,2,1,0:T(2,128)(2,1)S(1)} all-to-all(bf16[32,9,2,128]{3,2,1,0:T(2,128)(2,1)S(1)} %get-tuple-element.59), channel_id=1, replica_groups=mesh['kpt'=4,'z'=4,'core'=2] {'kpt','z','core'}, dimensions={0} | all-to-all | bytes 294912 | tf_op jit(solution)/shard_map/all_to_all | solution.py:432
  88.3 0.4 collective-permute-start.20
  88.7 2.4 %half.5.refs_0_ = f32[4,32,512]{2,1,0:T(8,128)S(1)} custom-call(bf16[32,9,2,128]{3,2,1,0:T(2,128)(2,1)S(1)} %all_to_all.17.packet_ref.refs_1_, bf16[4,512,4096]{2,1,0:T(8,128)(2,1)S(1)} %bitcast.2), custom_call_target="tpu_custom_call" | custom-call | flops 10000000000 | bytes 39062500 | tf_op jit(solution)/shard_map/half/pallas_call | solution.py:399
  91.0 2.6 %screen.5 = (f32[8,512]{1,0:T(8,128)S(1)}, f32[8,512]{1,0:T(8,128)S(1)}, f32[8,512]{1,0:T(8,128)S(1)}, f32[8,512]{1,0:T(8,128)S(1)}, f32[8,128]{1,0:T(8,128)S(1)}) custom-call(f32[4,32,512]{2,1,0:T(8,128)S(1)} %half.5.refs_0_, bf16[32,9,2,128]{3,2,1,0:T(2,128)(2,1)S(1)} %all_to_all.17.packet_ref.refs_1_, ...), custom_call_target="tpu_custom_call" | custom-call | tf_op jit(solution)/shard_map/screen/pallas_call | solution.py:399
  93.6 0.7 collective-permute-start.21
  94.3 1.3 %collective-permute-start.22 = (f32[8,512]{1,0:T(8,128)S(1)}, f32[8,512]{1,0:T(8,128)S(1)}, u32[]{:S(2)}, u32[]{:S(2)}) collective-permute-start(f32[8,512]{1,0:T(8,128)S(1)} %get-tuple-element.62), channel_id=1, source_target_pairs={{0,8},{8,0},{16,24},{24,16},{1,9},{9,1},{17,25},{25,17},{2,10},{10... | collective-permute-start | bytes 49160 | tf_op jit(solution)/shard_map/ppermute | solution.py:435
  95.7 1.5 %collective-permute-start.23 = (f32[8,512]{1,0:T(8,128)S(1)}, f32[8,512]{1,0:T(8,128)S(1)}, u32[]{:S(2)}, u32[]{:S(2)}) collective-permute-start(f32[8,512]{1,0:T(8,128)S(1)} %get-tuple-element.63), channel_id=1, source_target_pairs={{0,16},{8,24},{16,0},{24,8},{1,17},{9,25},{17,1},{25,9},{2,18},{10... | collective-permute-start | bytes 49160 | tf_op jit(solution)/shard_map/ppermute | solution.py:435
  97.2 1.2 %collective-permute-done.21.refs_0_ = f32[8,512]{1,0:T(8,128)S(1)} collective-permute-done((f32[8,512]{1,0:T(8,128)S(1)}, f32[8,512]{1,0:T(8,128)S(1)}, u32[]{:S(2)}, u32[]{:S(2)}) %collective-permute-start.21) | collective-permute-done | bytes 16416 | tf_op jit(solution)/shard_map/ppermute | solution.py:435
  98.3 1.1 collective-permute-done.23.refs_2_
  99.4 0.6 field.5.own_ref
  100.1 1.2 %collective-permute-done.24.other_ref = f32[8,512]{1,0:T(8,128)S(1)} collective-permute-done((f32[8,512]{1,0:T(8,128)S(1)}, f32[8,512]{1,0:T(8,128)S(1)}, u32[]{:S(2)}, u32[]{:S(2)}) %collective-permute-start.24) | collective-permute-done | bytes 16416 | tf_op jit(solution)/shard_map/ppermute | solution.py:435
  101.3 1.1 collective-permute-start.27
  102.4 0.9 collective-permute-start.26
  103.3 2.4 %collective-permute-start.25 = (bf16[8,512]{1,0:T(8,128)(2,1)S(1)}, bf16[8,512]{1,0:T(8,128)(2,1)S(1)}, u32[]{:S(2)}, u32[]{:S(2)}) collective-permute-start(bf16[8,512]{1,0:T(8,128)(2,1)S(1)} %pair.5.refs_0_), channel_id=1, source_target_pairs={{0,2},{2,0},{4,6},{6,4},{1,3},{3,1},{5,7},{7,5},{8,10},{10,8},{12,... | collective-permute-start | bytes 24584 | tf_op jit(solution)/shard_map/ppermute | solution.py:435
  105.7 1.1 collective-permute-done.27.refs_3_
  106.9 0.3 collective-permute-done.25.refs_1_
  107.6 1.5 %collective-permute-start.30 = (f32[8,128]{1,0:T(8,128)S(1)}, f32[8,128]{1,0:T(8,128)S(1)}, u32[]{:S(2)}, u32[]{:S(2)}) collective-permute-start(f32[8,128]{1,0:T(8,128)S(1)} %get-tuple-element.68.refs_0_), channel_id=1, source_target_pairs={{0,24},{8,16},{16,8},{24,0},{1,25},{9,17},{17,9},{25,1},{2,26},{10... | collective-permute-start | bytes 12296 | tf_op jit(solution)/shard_map/ppermute | solution.py:435
  109.1 0.7 collective-permute-start.29
  109.8 1.3 %collective-permute-start.28 = (f32[8,128]{1,0:T(8,128)S(1)}, f32[8,128]{1,0:T(8,128)S(1)}, u32[]{:S(2)}, u32[]{:S(2)}) collective-permute-start(f32[8,128]{1,0:T(8,128)S(1)} %get-tuple-element.68.refs_0_), channel_id=1, source_target_pairs={{0,8},{8,0},{16,24},{24,16},{1,9},{9,1},{17,25},{25,17},{2,10},{10... | collective-permute-start | bytes 12296 | tf_op jit(solution)/shard_map/ppermute | solution.py:435
  111.1 1.1 %own.1 = (f32[8,64]{1,0:T(8,128)S(1)}, f32[8,64]{1,0:T(8,128)S(1)}, f32[8,128]{1,0:T(8,128)S(1)}, f32[2,4,64]{2,1,0:T(4,128)}) custom-call(f32[8,512]{1,0:T(8,128)S(1)} %get-tuple-element.69.work_ref, f32[8,512]{1,0:T(8,128)S(1)} %get-tuple-element.70.vector_ref, f32[8,128]{1,0:T(8,128)S(1)} %get-tuple-element.57.refs_7_.refs_0_, ...), custom_call_target="tpu_custom_call" | custom-call | tf_op jit(solution)/shard_map/own/pallas_call | solution.py:399
  112.3 0.4 collective-permute-done.29.refs_2_
  112.7 0.7 collective-permute-done.28.refs_1_
  113.4 1.0 end.1
  (39 shorter events, 1.7 us)
Async XLA Ops:
  0.6 7.9 %copy-start.2 = (s32[16,16]{1,0:T(8,128)S(1)}, s32[16,16]{1,0:T(8,128)}, u32[]{:S(2)}) copy-start(s32[16,16]{1,0:T(8,128)} %mi_ref.1) | copy-start | bytes 3076
  0.6 11.9 %copy-start.1 = (bf16[4,512,512]{2,1,0:T(8,128)(2,1)S(1)}, bf16[4,512,512]{2,1,0:T(8,128)(2,1)}, u32[]{:S(2)}) copy-start(bf16[4,512,512]{2,1,0:T(8,128)(2,1)} %refs_10_.1) | copy-start | bytes 6291460
  1.6 1.4 %collective-permute-start = (f32[16,128]{1,0:T(8,128)S(1)}, f32[16,128]{1,0:T(8,128)S(1)}, u32[]{:S(2)}, u32[]{:S(2)}) collective-permute-start(f32[16,128]{1,0:T(8,128)S(1)} %begin.1.own_ref), channel_id=1, source_target_pairs={{0,1},{1,0},{2,3},{3,2},{4,5},{5,4},{6,7},{7,6},{8,9},{9,8},{10,11... | collective-permute-start | bytes 24584 | tf_op jit(solution)/shard_map/ppermute | solution.py:435
  3.0 6.6 %collective-permute-start.3 = (f32[32,128]{1,0:T(8,128)S(1)}, f32[32,128]{1,0:T(8,128)S(1)}, u32[]{:S(2)}, u32[]{:S(2)}) collective-permute-start(f32[32,128]{1,0:T(8,128)S(1)} %stack.1.refs_0_), channel_id=1, source_target_pairs={{0,6},{2,4},{4,2},{6,0},{1,7},{3,5},{5,3},{7,1},{8,14},{10,12},{12... | collective-permute-start | bytes 49160 | tf_op jit(solution)/shard_map/ppermute | solution.py:435
  7.9 4.6 %collective-permute-start.2 = (f32[32,128]{1,0:T(8,128)S(1)}, f32[32,128]{1,0:T(8,128)S(1)}, u32[]{:S(2)}, u32[]{:S(2)}) collective-permute-start(f32[32,128]{1,0:T(8,128)S(1)} %stack.1.refs_0_), channel_id=1, source_target_pairs={{0,4},{2,6},{4,0},{6,2},{1,5},{3,7},{5,1},{7,3},{8,12},{10,14},{12... | collective-permute-start | bytes 49160 | tf_op jit(solution)/shard_map/ppermute | solution.py:435
  7.9 4.6 %collective-permute-start.1 = (f32[32,128]{1,0:T(8,128)S(1)}, f32[32,128]{1,0:T(8,128)S(1)}, u32[]{:S(2)}, u32[]{:S(2)}) collective-permute-start(f32[32,128]{1,0:T(8,128)S(1)} %stack.1.refs_0_), channel_id=1, source_target_pairs={{0,2},{2,0},{4,6},{6,4},{1,3},{3,1},{5,7},{7,5},{8,10},{10,8},{12,... | collective-permute-start | bytes 49160 | tf_op jit(solution)/shard_map/ppermute | solution.py:435
  8.6 17.3 %slice-start = ((s8[16777216]{0:T(1024)(128)(4,1)}), s8[4194304]{0:T(1024)(128)(4,1)S(1)}, s32[]{:S(2)}) async-start(s8[16777216]{0:T(1024)(128)(4,1)} %bitcast.1), calls=%async_computation.3 | async-start | bytes 8388608
  8.9 17.0 %slice-start.1 = ((s8[16777216]{0:T(1024)(128)(4,1)}), s8[4194304]{0:T(1024)(128)(4,1)S(1)}, s32[]{:S(2)}) async-start(s8[16777216]{0:T(1024)(128)(4,1)} %bitcast.1), calls=%async_computation.4 | async-start | bytes 8388608
  8.9 17.0 %slice-start.2 = ((s8[16777216]{0:T(1024)(128)(4,1)}), s8[4194304]{0:T(1024)(128)(4,1)S(1)}, s32[]{:S(2)}) async-start(s8[16777216]{0:T(1024)(128)(4,1)} %bitcast.1), calls=%async_computation.5 | async-start | bytes 8388608
  9.0 17.0 %slice-start.3 = ((s8[16777216]{0:T(1024)(128)(4,1)}), s8[4194304]{0:T(1024)(128)(4,1)S(1)}, s32[]{:S(2)}) async-start(s8[16777216]{0:T(1024)(128)(4,1)} %bitcast.1), calls=%async_computation.6 | async-start | bytes 8388608
  25.5 2.8 %collective-permute-start.4 = (bf16[32,9,2,128]{3,2,1,0:T(2,128)(2,1)S(1)}, bf16[32,9,2,128]{3,2,1,0:T(2,128)(2,1)S(1)}, u32[]{:S(2)}, u32[]{:S(2)}) collective-permute-start(bf16[32,9,2,128]{3,2,1,0:T(2,128)(2,1)S(1)} %all_to_all.15.packet_ref.refs_1_), channel_id=1, source_target_pairs={{0,1},{1,0},{2,3},{3,2},{4,5},{5,4},{6,7},{7,6},{8,9},{9,8},{10,11... | collective-permute-start | bytes 442376 | tf_op jit(solution)/shard_map/ppermute | solution.py:435
  28.3 8.4 %copy-start = (bf16[4,512,512]{2,1,0:T(8,128)(2,1)S(1)}, bf16[4,512,512]{2,1,0:T(8,128)(2,1)}, u32[]{:S(2)}) copy-start(bf16[4,512,512]{2,1,0:T(8,128)(2,1)} %refs_4_.11) | copy-start | bytes 6291460
  30.9 13.7 %copy-start.3 = (f32[2]{0:T(128)S(1)}, f32[2]{0:T(128)}, u32[]{:S(2)}) copy-start(f32[2]{0:T(128)} %param.11) | copy-start | bytes 28
  30.9 4.7 %collective-permute-start.5 = (f32[8,512]{1,0:T(8,128)S(1)}, f32[8,512]{1,0:T(8,128)S(1)}, u32[]{:S(2)}, u32[]{:S(2)}) collective-permute-start(f32[8,512]{1,0:T(8,128)S(1)} %get-tuple-element.42), channel_id=1, source_target_pairs={{0,24},{8,16},{16,8},{24,0},{1,25},{9,17},{17,9},{25,1},{2,26},{10... | collective-permute-start | bytes 49160 | tf_op jit(solution)/shard_map/ppermute | solution.py:435
  31.6 4.0 %collective-permute-start.6 = (f32[8,512]{1,0:T(8,128)S(1)}, f32[8,512]{1,0:T(8,128)S(1)}, u32[]{:S(2)}, u32[]{:S(2)}) collective-permute-start(f32[8,512]{1,0:T(8,128)S(1)} %get-tuple-element.43), channel_id=1, source_target_pairs={{0,8},{8,0},{16,24},{24,16},{1,9},{9,1},{17,25},{25,17},{2,10},{10... | collective-permute-start | bytes 49160 | tf_op jit(solution)/shard_map/ppermute | solution.py:435
  32.9 3.7 %collective-permute-start.7 = (f32[8,512]{1,0:T(8,128)S(1)}, f32[8,512]{1,0:T(8,128)S(1)}, u32[]{:S(2)}, u32[]{:S(2)}) collective-permute-start(f32[8,512]{1,0:T(8,128)S(1)} %get-tuple-element.44), channel_id=1, source_target_pairs={{0,16},{8,24},{16,0},{24,8},{1,17},{9,25},{17,1},{25,9},{2,18},{10... | collective-permute-start | bytes 49160 | tf_op jit(solution)/shard_map/ppermute | solution.py:435
  37.3 1.2 %collective-permute-start.8 = (f32[8,512]{1,0:T(8,128)S(1)}, f32[8,512]{1,0:T(8,128)S(1)}, u32[]{:S(2)}, u32[]{:S(2)}) collective-permute-start(f32[8,512]{1,0:T(8,128)S(1)} %field.3.own_ref), channel_id=1, source_target_pairs={{0,1},{1,0},{2,3},{3,2},{4,5},{5,4},{6,7},{7,6},{8,9},{9,8},{10,11... | collective-permute-start | bytes 49160 | tf_op jit(solution)/shard_map/ppermute | solution.py:435
  38.5 5.4 %collective-permute-start.11 = (bf16[8,512]{1,0:T(8,128)(2,1)S(1)}, bf16[8,512]{1,0:T(8,128)(2,1)S(1)}, u32[]{:S(2)}, u32[]{:S(2)}) collective-permute-start(bf16[8,512]{1,0:T(8,128)(2,1)S(1)} %pair.3.refs_0_), channel_id=1, source_target_pairs={{0,6},{2,4},{4,2},{6,0},{1,7},{3,5},{5,3},{7,1},{8,14},{10,12},{12... | collective-permute-start | bytes 24584 | tf_op jit(solution)/shard_map/ppermute | solution.py:435
  39.7 4.5 %collective-permute-start.10 = (bf16[8,512]{1,0:T(8,128)(2,1)S(1)}, bf16[8,512]{1,0:T(8,128)(2,1)S(1)}, u32[]{:S(2)}, u32[]{:S(2)}) collective-permute-start(bf16[8,512]{1,0:T(8,128)(2,1)S(1)} %pair.3.refs_0_), channel_id=1, source_target_pairs={{0,4},{2,6},{4,0},{6,2},{1,5},{3,7},{5,1},{7,3},{8,12},{10,14},{12... | collective-permute-start | bytes 24584 | tf_op jit(solution)/shard_map/ppermute | solution.py:435
  40.6 4.0 %collective-permute-start.9 = (bf16[8,512]{1,0:T(8,128)(2,1)S(1)}, bf16[8,512]{1,0:T(8,128)(2,1)S(1)}, u32[]{:S(2)}, u32[]{:S(2)}) collective-permute-start(bf16[8,512]{1,0:T(8,128)(2,1)S(1)} %pair.3.refs_0_), channel_id=1, source_target_pairs={{0,2},{2,0},{4,6},{6,4},{1,3},{3,1},{5,7},{7,5},{8,10},{10,8},{12,... | collective-permute-start | bytes 24584 | tf_op jit(solution)/shard_map/ppermute | solution.py:435
  57.0 2.7 %collective-permute-start.12 = (bf16[32,9,2,128]{3,2,1,0:T(2,128)(2,1)S(1)}, bf16[32,9,2,128]{3,2,1,0:T(2,128)(2,1)S(1)}, u32[]{:S(2)}, u32[]{:S(2)}) collective-permute-start(bf16[32,9,2,128]{3,2,1,0:T(2,128)(2,1)S(1)} %all_to_all.16.packet_ref.refs_1_), channel_id=1, source_target_pairs={{0,1},{1,0},{2,3},{3,2},{4,5},{5,4},{6,7},{7,6},{8,9},{9,8},{10,11... | collective-permute-start | bytes 442376 | tf_op jit(solution)/shard_map/ppermute | solution.py:435
  62.3 4.7 %collective-permute-start.13 = (f32[8,512]{1,0:T(8,128)S(1)}, f32[8,512]{1,0:T(8,128)S(1)}, u32[]{:S(2)}, u32[]{:S(2)}) collective-permute-start(f32[8,512]{1,0:T(8,128)S(1)} %get-tuple-element.52), channel_id=1, source_target_pairs={{0,24},{8,16},{16,8},{24,0},{1,25},{9,17},{17,9},{25,1},{2,26},{10... | collective-permute-start | bytes 49160 | tf_op jit(solution)/shard_map/ppermute | solution.py:435
  63.0 4.0 %collective-permute-start.14 = (f32[8,512]{1,0:T(8,128)S(1)}, f32[8,512]{1,0:T(8,128)S(1)}, u32[]{:S(2)}, u32[]{:S(2)}) collective-permute-start(f32[8,512]{1,0:T(8,128)S(1)} %get-tuple-element.53), channel_id=1, source_target_pairs={{0,8},{8,0},{16,24},{24,16},{1,9},{9,1},{17,25},{25,17},{2,10},{10... | collective-permute-start | bytes 49160 | tf_op jit(solution)/shard_map/ppermute | solution.py:435
  64.3 3.7 %collective-permute-start.15 = (f32[8,512]{1,0:T(8,128)S(1)}, f32[8,512]{1,0:T(8,128)S(1)}, u32[]{:S(2)}, u32[]{:S(2)}) collective-permute-start(f32[8,512]{1,0:T(8,128)S(1)} %get-tuple-element.54), channel_id=1, source_target_pairs={{0,16},{8,24},{16,0},{24,8},{1,17},{9,25},{17,1},{25,9},{2,18},{10... | collective-permute-start | bytes 49160 | tf_op jit(solution)/shard_map/ppermute | solution.py:435
  68.7 1.2 %collective-permute-start.16 = (f32[8,512]{1,0:T(8,128)S(1)}, f32[8,512]{1,0:T(8,128)S(1)}, u32[]{:S(2)}, u32[]{:S(2)}) collective-permute-start(f32[8,512]{1,0:T(8,128)S(1)} %field.4.own_ref), channel_id=1, source_target_pairs={{0,1},{1,0},{2,3},{3,2},{4,5},{5,4},{6,7},{7,6},{8,9},{9,8},{10,11... | collective-permute-start | bytes 49160 | tf_op jit(solution)/shard_map/ppermute | solution.py:435
  69.9 5.4 %collective-permute-start.19 = (bf16[8,512]{1,0:T(8,128)(2,1)S(1)}, bf16[8,512]{1,0:T(8,128)(2,1)S(1)}, u32[]{:S(2)}, u32[]{:S(2)}) collective-permute-start(bf16[8,512]{1,0:T(8,128)(2,1)S(1)} %pair.4.refs_0_), channel_id=1, source_target_pairs={{0,6},{2,4},{4,2},{6,0},{1,7},{3,5},{5,3},{7,1},{8,14},{10,12},{12... | collective-permute-start | bytes 24584 | tf_op jit(solution)/shard_map/ppermute | solution.py:435
  71.1 4.5 %collective-permute-start.18 = (bf16[8,512]{1,0:T(8,128)(2,1)S(1)}, bf16[8,512]{1,0:T(8,128)(2,1)S(1)}, u32[]{:S(2)}, u32[]{:S(2)}) collective-permute-start(bf16[8,512]{1,0:T(8,128)(2,1)S(1)} %pair.4.refs_0_), channel_id=1, source_target_pairs={{0,4},{2,6},{4,0},{6,2},{1,5},{3,7},{5,1},{7,3},{8,12},{10,14},{12... | collective-permute-start | bytes 24584 | tf_op jit(solution)/shard_map/ppermute | solution.py:435
  72.0 4.0 %collective-permute-start.17 = (bf16[8,512]{1,0:T(8,128)(2,1)S(1)}, bf16[8,512]{1,0:T(8,128)(2,1)S(1)}, u32[]{:S(2)}, u32[]{:S(2)}) collective-permute-start(bf16[8,512]{1,0:T(8,128)(2,1)S(1)} %pair.4.refs_0_), channel_id=1, source_target_pairs={{0,2},{2,0},{4,6},{6,4},{1,3},{3,1},{5,7},{7,5},{8,10},{10,8},{12,... | collective-permute-start | bytes 24584 | tf_op jit(solution)/shard_map/ppermute | solution.py:435
  88.3 2.7 %collective-permute-start.20 = (bf16[32,9,2,128]{3,2,1,0:T(2,128)(2,1)S(1)}, bf16[32,9,2,128]{3,2,1,0:T(2,128)(2,1)S(1)}, u32[]{:S(2)}, u32[]{:S(2)}) collective-permute-start(bf16[32,9,2,128]{3,2,1,0:T(2,128)(2,1)S(1)} %all_to_all.17.packet_ref.refs_1_), channel_id=1, source_target_pairs={{0,1},{1,0},{2,3},{3,2},{4,5},{5,4},{6,7},{7,6},{8,9},{9,8},{10,11... | collective-permute-start | bytes 442376 | tf_op jit(solution)/shard_map/ppermute | solution.py:435
  93.6 4.7 %collective-permute-start.21 = (f32[8,512]{1,0:T(8,128)S(1)}, f32[8,512]{1,0:T(8,128)S(1)}, u32[]{:S(2)}, u32[]{:S(2)}) collective-permute-start(f32[8,512]{1,0:T(8,128)S(1)} %get-tuple-element.61), channel_id=1, source_target_pairs={{0,24},{8,16},{16,8},{24,0},{1,25},{9,17},{17,9},{25,1},{2,26},{10... | collective-permute-start | bytes 49160 | tf_op jit(solution)/shard_map/ppermute | solution.py:435
  94.3 4.0 %collective-permute-start.22 = (f32[8,512]{1,0:T(8,128)S(1)}, f32[8,512]{1,0:T(8,128)S(1)}, u32[]{:S(2)}, u32[]{:S(2)}) collective-permute-start(f32[8,512]{1,0:T(8,128)S(1)} %get-tuple-element.62), channel_id=1, source_target_pairs={{0,8},{8,0},{16,24},{24,16},{1,9},{9,1},{17,25},{25,17},{2,10},{10... | collective-permute-start | bytes 49160 | tf_op jit(solution)/shard_map/ppermute | solution.py:435
  95.7 3.7 %collective-permute-start.23 = (f32[8,512]{1,0:T(8,128)S(1)}, f32[8,512]{1,0:T(8,128)S(1)}, u32[]{:S(2)}, u32[]{:S(2)}) collective-permute-start(f32[8,512]{1,0:T(8,128)S(1)} %get-tuple-element.63), channel_id=1, source_target_pairs={{0,16},{8,24},{16,0},{24,8},{1,17},{9,25},{17,1},{25,9},{2,18},{10... | collective-permute-start | bytes 49160 | tf_op jit(solution)/shard_map/ppermute | solution.py:435
  100.1 1.2 %collective-permute-start.24 = (f32[8,512]{1,0:T(8,128)S(1)}, f32[8,512]{1,0:T(8,128)S(1)}, u32[]{:S(2)}, u32[]{:S(2)}) collective-permute-start(f32[8,512]{1,0:T(8,128)S(1)} %field.5.own_ref), channel_id=1, source_target_pairs={{0,1},{1,0},{2,3},{3,2},{4,5},{5,4},{6,7},{7,6},{8,9},{9,8},{10,11... | collective-permute-start | bytes 49160 | tf_op jit(solution)/shard_map/ppermute | solution.py:435
  101.3 5.4 %collective-permute-start.27 = (bf16[8,512]{1,0:T(8,128)(2,1)S(1)}, bf16[8,512]{1,0:T(8,128)(2,1)S(1)}, u32[]{:S(2)}, u32[]{:S(2)}) collective-permute-start(bf16[8,512]{1,0:T(8,128)(2,1)S(1)} %pair.5.refs_0_), channel_id=1, source_target_pairs={{0,6},{2,4},{4,2},{6,0},{1,7},{3,5},{5,3},{7,1},{8,14},{10,12},{12... | collective-permute-start | bytes 24584 | tf_op jit(solution)/shard_map/ppermute | solution.py:435
  102.4 4.5 %collective-permute-start.26 = (bf16[8,512]{1,0:T(8,128)(2,1)S(1)}, bf16[8,512]{1,0:T(8,128)(2,1)S(1)}, u32[]{:S(2)}, u32[]{:S(2)}) collective-permute-start(bf16[8,512]{1,0:T(8,128)(2,1)S(1)} %pair.5.refs_0_), channel_id=1, source_target_pairs={{0,4},{2,6},{4,0},{6,2},{1,5},{3,7},{5,1},{7,3},{8,12},{10,14},{12... | collective-permute-start | bytes 24584 | tf_op jit(solution)/shard_map/ppermute | solution.py:435
  103.3 4.0 %collective-permute-start.25 = (bf16[8,512]{1,0:T(8,128)(2,1)S(1)}, bf16[8,512]{1,0:T(8,128)(2,1)S(1)}, u32[]{:S(2)}, u32[]{:S(2)}) collective-permute-start(bf16[8,512]{1,0:T(8,128)(2,1)S(1)} %pair.5.refs_0_), channel_id=1, source_target_pairs={{0,2},{2,0},{4,6},{6,4},{1,3},{3,1},{5,7},{7,5},{8,10},{10,8},{12,... | collective-permute-start | bytes 24584 | tf_op jit(solution)/shard_map/ppermute | solution.py:435
  107.6 4.7 %collective-permute-start.30 = (f32[8,128]{1,0:T(8,128)S(1)}, f32[8,128]{1,0:T(8,128)S(1)}, u32[]{:S(2)}, u32[]{:S(2)}) collective-permute-start(f32[8,128]{1,0:T(8,128)S(1)} %get-tuple-element.68.refs_0_), channel_id=1, source_target_pairs={{0,24},{8,16},{16,8},{24,0},{1,25},{9,17},{17,9},{25,1},{2,26},{10... | collective-permute-start | bytes 12296 | tf_op jit(solution)/shard_map/ppermute | solution.py:435
  109.1 3.6 %collective-permute-start.29 = (f32[8,128]{1,0:T(8,128)S(1)}, f32[8,128]{1,0:T(8,128)S(1)}, u32[]{:S(2)}, u32[]{:S(2)}) collective-permute-start(f32[8,128]{1,0:T(8,128)S(1)} %get-tuple-element.68.refs_0_), channel_id=1, source_target_pairs={{0,16},{8,24},{16,0},{24,8},{1,17},{9,25},{17,1},{25,9},{2,18},{10... | collective-permute-start | bytes 12296 | tf_op jit(solution)/shard_map/ppermute | solution.py:435
  109.8 3.6 %collective-permute-start.28 = (f32[8,128]{1,0:T(8,128)S(1)}, f32[8,128]{1,0:T(8,128)S(1)}, u32[]{:S(2)}, u32[]{:S(2)}) collective-permute-start(f32[8,128]{1,0:T(8,128)S(1)} %get-tuple-element.68.refs_0_), channel_id=1, source_target_pairs={{0,8},{8,0},{16,24},{24,16},{1,9},{9,1},{17,25},{25,17},{2,10},{10... | collective-permute-start | bytes 12296 | tf_op jit(solution)/shard_map/ppermute | solution.py:435

commit v9 on v8

--- a/solution.py
+++ b/solution.py
@@ -66,10 +66,13 @@
 
 def stack_kernel(s, own_ref, other_ref, out_ref):
     core = lax.axis_index("core")
-    height = own_ref.shape[0]
+    half = own_ref.shape[1] // 2
+    levels = []
     for c in range(CORES):
         value = jnp.where(core == c, own_ref[...], other_ref[...])
-        out_ref[c * height : (c + 1) * height, :] = value
+        out_ref[c * s.rows : (c + 1) * s.rows, :] = value[: s.rows]
+        levels.append(value[s.rows :, :half])
+    out_ref[CORES * s.rows :, :] = jnp.concatenate(levels, axis=1)
 
 
 def pick_kernel(s, mi_ref, pick_ref):
@@ -101,13 +104,13 @@
     rows = s.rows
     width = refs[0].shape[1] // 2
     pieces = in_order(lax.axis_index("z"), [ref[...] for ref in refs[: s.chips]])
-    for ref, row, lane in ((vector_ref, 0, 0), (earlier_ref, 0, width), (levels_ref, rows, 0)):
+    for ref, lane in ((vector_ref, 0), (earlier_ref, width)):
         blocks = []
         for piece in pieces:
             for c in range(CORES):
-                at = 2 * rows * c + row
-                blocks.append(piece[at : at + rows, lane : lane + width])
+                blocks.append(piece[rows * c : rows * (c + 1), lane : lane + width])
         ref[...] = jnp.concatenate(blocks, axis=1)
+    levels_ref[...] = jnp.concatenate([piece[CORES * rows :] for piece in pieces], axis=1)
     high, low = project(s, vector_ref[...], right_ref)
     density_ref[...] = high + low
     send(s, high, jnp.zeros((rows, LANES), F32), packet_ref)
@@ -364,14 +367,13 @@
     field_ref[...] = jnp.dot(pick_ref[...], stacked, preferred_element_type=F32)
     mine = lax.axis_index("kpt")
     for a in range(s.groups):
-        out_refs[a][...] = field_ref[pl.ds(pl.multiple_of((mine ^ a) * rows, rows), rows), :]
+        at = pl.ds(pl.multiple_of((mine ^ a) * rows, rows), rows)
+        out_refs[a][...] = field_ref[at, :].astype(out_refs[a].dtype)
 
 
 def field_kernel(s, first, *refs):
     left_ref, out_ref = refs[-2:]
-    field = refs[0][...]
-    for ref in refs[1:-2]:
-        field = field + ref[...]
+    field = sum(ref[...].astype(F32) for ref in refs[:-2])
     parts = (field.astype(BF),) if first else high_low(field)
     stacked = jnp.concatenate([p.astype(F32) for p in parts], axis=0).astype(BF)
     rows = s.rows
@@ -462,7 +464,7 @@
     (start,) = call(
         functools.partial(stack_kernel, s),
         (start, across(start, "core", CORES, 1)),
-        [((CORES * 2 * s.rows, 2 * band_block), F32)],
+        [(((CORES + 1) * s.rows, 2 * band_block), F32)],
         "stack",
     )
     (pick,) = call(
@@ -490,7 +492,7 @@
             functools.partial(half_kernel, s), (got, screened), [image], "half", cost=COVER
         )
         args = (half, got, other) + (() if first else (before,)) + (screened, pick)
-        outs = [((s.rows, width), F32)] * groups
+        outs = [block] + [((s.rows, width), BF)] * (groups - 1)
         outs += [] if first else [((s.rows, LANES), F32)]
         outs += [image] if keep else []
         results = call(

time: 115 us -> 115 us (level)
  no operation moved by 1% of the time
where the time goes in v9:
time: 115 us; the launch traced here: 114 us
  blocking collectives  36.1 us (31%)
  starting transfers between devices  34.5 us (30%)
  Pallas kernels  22.2 us (19%)
  waiting for transfers between devices  20.5 us (18%)
    all_to_all x3, blocking collectives, exchange(): return lax.all_to_all(x, axes, 0, 0, tiled=True)  36.1 us
    ppermute x31, starting transfers between devices, across(): return lax.ppermute(x, axis, [(i, i ^ distance) for i in range(size)])  34.5 us
    pallas_call x21, Pallas kernels, call(): pl.pallas_call(body, out_shape=[jax.ShapeDtypeStruct(shape, dtype) for sh...  22.2 us
    ppermute x31, waiting for transfers between devices, across(): return lax.ppermute(x, axis, [(i, i ^ distance) for i in range(size)])  20.5 us
  transfers between devices with their start and end apart: 31, of which 23 were waited for; matrix products, arithmetic and copies ran while one was open for 0% of the time, Pallas kernels for 8%

profile of v9, /device:TPU:0, one launch (start us, length us, event | category | flops | bytes accessed | tf_op | source)
XLA Modules:
  0.0 114.3 jit_solution(18391418430969520156)
XLA Ops:
  0.7 1.0 begin.1.own_ref
  1.6 0.6 collective-permute-start
  2.2 0.8 collective-permute-done.other_ref
  3.1 4.9 %collective-permute-start.3 = (f32[24,128]{1,0:T(8,128)S(1)}, f32[24,128]{1,0:T(8,128)S(1)}, u32[]{:S(2)}, u32[]{:S(2)}) collective-permute-start(f32[24,128]{1,0:T(8,128)S(1)} %stack.1.refs_0_), channel_id=1, source_target_pairs={{0,6},{2,4},{4,2},{6,0},{1,7},{3,5},{5,3},{7,1},{8,14},{10,12},{12... | collective-permute-start | bytes 36872 | tf_op jit(solution)/shard_map/ppermute | solution.py:437
  8.0 0.6 collective-permute-start.1
  9.0 0.7 collective-permute-done.3.refs_3_
  9.7 2.9 %collective-permute-done.2.refs_2_ = f32[24,128]{1,0:T(8,128)S(1)} collective-permute-done((f32[24,128]{1,0:T(8,128)S(1)}, f32[24,128]{1,0:T(8,128)S(1)}, u32[]{:S(2)}, u32[]{:S(2)}) %collective-permute-start.2) | collective-permute-done | bytes 12320 | tf_op jit(solution)/shard_map/ppermute | solution.py:437
  12.6 0.5 unpack.1
  13.1 12.4 %all_to_all.15.packet_ref.refs_1_ = bf16[32,9,2,128]{3,2,1,0:T(2,128)(2,1)S(1)} all-to-all(bf16[32,9,2,128]{3,2,1,0:T(2,128)(2,1)S(1)} %get-tuple-element.41), channel_id=1, replica_groups=mesh['kpt'=4,'z'=4,'core'=2] {'kpt','z','core'}, dimensions={0} | all-to-all | bytes 294912 | tf_op jit(solution)/shard_map/all_to_all | solution.py:434
  25.6 0.4 collective-permute-start.4
  26.0 2.4 %half.3.refs_0_ = f32[4,32,512]{2,1,0:T(8,128)S(1)} custom-call(bf16[32,9,2,128]{3,2,1,0:T(2,128)(2,1)S(1)} %all_to_all.15.packet_ref.refs_1_, bf16[4,512,4096]{2,1,0:T(8,128)(2,1)S(1)} %bitcast.2), custom_call_target="tpu_custom_call" | custom-call | flops 10000000000 | bytes 39062500 | tf_op jit(solution)/shard_map/half/pallas_call | solution.py:401
  28.3 2.6 %screen.3 = (f32[8,512]{1,0:T(8,128)S(1)}, bf16[8,512]{1,0:T(8,128)(2,1)S(1)}, bf16[8,512]{1,0:T(8,128)(2,1)S(1)}, bf16[8,512]{1,0:T(8,128)(2,1)S(1)}, f32[4,32,512]{2,1,0:T(8,128)S(1)}) custom-call(f32[4,32,512]{2,1,0:T(8,128)S(1)} %half.3.refs_0_, bf16[32,9,2,128]{3,2,1,0:T(2,128)(2,1)S(1)} %all_to_all.15.packet_ref.refs_1_, ...), custom_call_target="tpu_custom_call" | custom-call | tf_op jit(solution)/shard_map/screen/pallas_call | solution.py:401
  30.9 0.7 collective-permute-start.5
  31.6 1.3 %collective-permute-start.6 = (bf16[8,512]{1,0:T(8,128)(2,1)S(1)}, bf16[8,512]{1,0:T(8,128)(2,1)S(1)}, u32[]{:S(2)}, u32[]{:S(2)}) collective-permute-start(bf16[8,512]{1,0:T(8,128)(2,1)S(1)} %get-tuple-element.43), channel_id=1, source_target_pairs={{0,8},{8,0},{16,24},{24,16},{1,9},{9,1},{17,25},{25,17},{2,10},{10... | collective-permute-start | bytes 24584 | tf_op jit(solution)/shard_map/ppermute | solution.py:437
  33.0 1.5 %collective-permute-start.7 = (bf16[8,512]{1,0:T(8,128)(2,1)S(1)}, bf16[8,512]{1,0:T(8,128)(2,1)S(1)}, u32[]{:S(2)}, u32[]{:S(2)}) collective-permute-start(bf16[8,512]{1,0:T(8,128)(2,1)S(1)} %get-tuple-element.44), channel_id=1, source_target_pairs={{0,16},{8,24},{16,0},{24,8},{1,17},{9,25},{17,1},{25,9},{2,18},{10... | collective-permute-start | bytes 24584 | tf_op jit(solution)/shard_map/ppermute | solution.py:437
  34.5 1.1 collective-permute-done.5.refs_0_
  35.5 1.1 collective-permute-done.7.refs_2_
  36.6 0.6 field.3.own_ref
  37.3 1.2 %collective-permute-done.8.other_ref = f32[8,512]{1,0:T(8,128)S(1)} collective-permute-done((f32[8,512]{1,0:T(8,128)S(1)}, f32[8,512]{1,0:T(8,128)S(1)}, u32[]{:S(2)}, u32[]{:S(2)}) %collective-permute-start.8) | collective-permute-done | bytes 16416 | tf_op jit(solution)/shard_map/ppermute | solution.py:437
  38.5 1.1 collective-permute-start.11
  39.6 0.9 collective-permute-start.10
  40.5 2.4 %collective-permute-start.9 = (bf16[8,512]{1,0:T(8,128)(2,1)S(1)}, bf16[8,512]{1,0:T(8,128)(2,1)S(1)}, u32[]{:S(2)}, u32[]{:S(2)}) collective-permute-start(bf16[8,512]{1,0:T(8,128)(2,1)S(1)} %pair.3.refs_0_), channel_id=1, source_target_pairs={{0,2},{2,0},{4,6},{6,4},{1,3},{3,1},{5,7},{7,5},{8,10},{10,8},{12,... | collective-permute-start | bytes 24584 | tf_op jit(solution)/shard_map/ppermute | solution.py:437
  42.9 1.1 collective-permute-done.11.refs_3_
  44.1 0.3 collective-permute-done.9.refs_1_
  44.5 0.6 apply.3
  45.1 11.8 %all_to_all.16.packet_ref.refs_1_ = bf16[32,9,2,128]{3,2,1,0:T(2,128)(2,1)S(1)} all-to-all(bf16[32,9,2,128]{3,2,1,0:T(2,128)(2,1)S(1)} %get-tuple-element.50), channel_id=1, replica_groups=mesh['kpt'=4,'z'=4,'core'=2] {'kpt','z','core'}, dimensions={0} | all-to-all | bytes 294912 | tf_op jit(solution)/shard_map/all_to_all | solution.py:434
  56.9 0.4 collective-permute-start.12
  57.3 2.4 %half.4.refs_0_ = f32[4,32,512]{2,1,0:T(8,128)S(1)} custom-call(bf16[32,9,2,128]{3,2,1,0:T(2,128)(2,1)S(1)} %all_to_all.16.packet_ref.refs_1_, bf16[4,512,4096]{2,1,0:T(8,128)(2,1)S(1)} %bitcast.2), custom_call_target="tpu_custom_call" | custom-call | flops 10000000000 | bytes 39062500 | tf_op jit(solution)/shard_map/half/pallas_call | solution.py:401
  59.7 2.6 %screen.4 = (f32[8,512]{1,0:T(8,128)S(1)}, bf16[8,512]{1,0:T(8,128)(2,1)S(1)}, bf16[8,512]{1,0:T(8,128)(2,1)S(1)}, bf16[8,512]{1,0:T(8,128)(2,1)S(1)}, f32[8,128]{1,0:T(8,128)S(1)}, /*index=5*/f32[4,32,512]{2,1,0:T(8,128)S(1)}) custom-call(f32[4,32,512]{2,1,0:T(8,128)S(1)} %half.4.refs_0_, bf16[32,9,2,128]{3,2,1,0:T(2,128)(2,1)S(1)} %all_to_all.16.packet_ref.refs_1_, ...), custom_call_target="tpu_custom_call" | custom-call | tf_op jit(solution)/shard_map/screen/pallas_call | solution.py:401
  62.2 0.7 collective-permute-start.13
  62.9 1.3 %collective-permute-start.14 = (bf16[8,512]{1,0:T(8,128)(2,1)S(1)}, bf16[8,512]{1,0:T(8,128)(2,1)S(1)}, u32[]{:S(2)}, u32[]{:S(2)}) collective-permute-start(bf16[8,512]{1,0:T(8,128)(2,1)S(1)} %get-tuple-element.53), channel_id=1, source_target_pairs={{0,8},{8,0},{16,24},{24,16},{1,9},{9,1},{17,25},{25,17},{2,10},{10... | collective-permute-start | bytes 24584 | tf_op jit(solution)/shard_map/ppermute | solution.py:437
  64.3 1.5 %collective-permute-start.15 = (bf16[8,512]{1,0:T(8,128)(2,1)S(1)}, bf16[8,512]{1,0:T(8,128)(2,1)S(1)}, u32[]{:S(2)}, u32[]{:S(2)}) collective-permute-start(bf16[8,512]{1,0:T(8,128)(2,1)S(1)} %get-tuple-element.54), channel_id=1, source_target_pairs={{0,16},{8,24},{16,0},{24,8},{1,17},{9,25},{17,1},{25,9},{2,18},{10... | collective-permute-start | bytes 24584 | tf_op jit(solution)/shard_map/ppermute | solution.py:437
  65.8 1.1 collective-permute-done.13.refs_0_
  66.8 1.1 collective-permute-done.15.refs_2_
  67.9 0.6 field.4.own_ref
  68.6 1.2 %collective-permute-done.16.other_ref = f32[8,512]{1,0:T(8,128)S(1)} collective-permute-done((f32[8,512]{1,0:T(8,128)S(1)}, f32[8,512]{1,0:T(8,128)S(1)}, u32[]{:S(2)}, u32[]{:S(2)}) %collective-permute-start.16) | collective-permute-done | bytes 16416 | tf_op jit(solution)/shard_map/ppermute | solution.py:437
  69.8 1.1 collective-permute-start.19
  70.9 0.9 collective-permute-start.18
  71.8 2.4 %collective-permute-start.17 = (bf16[8,512]{1,0:T(8,128)(2,1)S(1)}, bf16[8,512]{1,0:T(8,128)(2,1)S(1)}, u32[]{:S(2)}, u32[]{:S(2)}) collective-permute-start(bf16[8,512]{1,0:T(8,128)(2,1)S(1)} %pair.4.refs_0_), channel_id=1, source_target_pairs={{0,2},{2,0},{4,6},{6,4},{1,3},{3,1},{5,7},{7,5},{8,10},{10,8},{12,... | collective-permute-start | bytes 24584 | tf_op jit(solution)/shard_map/ppermute | solution.py:437
  74.2 1.1 collective-permute-done.19.refs_3_
  75.8 0.5 apply.4
  76.3 11.8 %all_to_all.17.packet_ref.refs_1_ = bf16[32,9,2,128]{3,2,1,0:T(2,128)(2,1)S(1)} all-to-all(bf16[32,9,2,128]{3,2,1,0:T(2,128)(2,1)S(1)} %get-tuple-element.59), channel_id=1, replica_groups=mesh['kpt'=4,'z'=4,'core'=2] {'kpt','z','core'}, dimensions={0} | all-to-all | bytes 294912 | tf_op jit(solution)/shard_map/all_to_all | solution.py:434
  88.2 0.4 collective-permute-start.20
  88.5 2.4 %half.5.refs_0_ = f32[4,32,512]{2,1,0:T(8,128)S(1)} custom-call(bf16[32,9,2,128]{3,2,1,0:T(2,128)(2,1)S(1)} %all_to_all.17.packet_ref.refs_1_, bf16[4,512,4096]{2,1,0:T(8,128)(2,1)S(1)} %bitcast.2), custom_call_target="tpu_custom_call" | custom-call | flops 10000000000 | bytes 39062500 | tf_op jit(solution)/shard_map/half/pallas_call | solution.py:401
  90.9 2.6 %screen.5 = (f32[8,512]{1,0:T(8,128)S(1)}, bf16[8,512]{1,0:T(8,128)(2,1)S(1)}, bf16[8,512]{1,0:T(8,128)(2,1)S(1)}, bf16[8,512]{1,0:T(8,128)(2,1)S(1)}, f32[8,128]{1,0:T(8,128)S(1)}) custom-call(f32[4,32,512]{2,1,0:T(8,128)S(1)} %half.5.refs_0_, bf16[32,9,2,128]{3,2,1,0:T(2,128)(2,1)S(1)} %all_to_all.17.packet_ref.refs_1_, ...), custom_call_target="tpu_custom_call" | custom-call | tf_op jit(solution)/shard_map/screen/pallas_call | solution.py:401
  93.5 0.7 collective-permute-start.21
  94.2 1.3 %collective-permute-start.22 = (bf16[8,512]{1,0:T(8,128)(2,1)S(1)}, bf16[8,512]{1,0:T(8,128)(2,1)S(1)}, u32[]{:S(2)}, u32[]{:S(2)}) collective-permute-start(bf16[8,512]{1,0:T(8,128)(2,1)S(1)} %get-tuple-element.62), channel_id=1, source_target_pairs={{0,8},{8,0},{16,24},{24,16},{1,9},{9,1},{17,25},{25,17},{2,10},{10... | collective-permute-start | bytes 24584 | tf_op jit(solution)/shard_map/ppermute | solution.py:437
  95.5 1.5 %collective-permute-start.23 = (bf16[8,512]{1,0:T(8,128)(2,1)S(1)}, bf16[8,512]{1,0:T(8,128)(2,1)S(1)}, u32[]{:S(2)}, u32[]{:S(2)}) collective-permute-start(bf16[8,512]{1,0:T(8,128)(2,1)S(1)} %get-tuple-element.63), channel_id=1, source_target_pairs={{0,16},{8,24},{16,0},{24,8},{1,17},{9,25},{17,1},{25,9},{2,18},{10... | collective-permute-start | bytes 24584 | tf_op jit(solution)/shard_map/ppermute | solution.py:437
  97.0 1.1 collective-permute-done.21.refs_0_
  98.1 1.1 collective-permute-done.23.refs_2_
  99.2 0.6 field.5.own_ref
  99.8 1.2 %collective-permute-done.24.other_ref = f32[8,512]{1,0:T(8,128)S(1)} collective-permute-done((f32[8,512]{1,0:T(8,128)S(1)}, f32[8,512]{1,0:T(8,128)S(1)}, u32[]{:S(2)}, u32[]{:S(2)}) %collective-permute-start.24) | collective-permute-done | bytes 16416 | tf_op jit(solution)/shard_map/ppermute | solution.py:437
  101.0 1.1 collective-permute-start.27
  102.1 0.9 collective-permute-start.26
  103.0 2.4 %collective-permute-start.25 = (bf16[8,512]{1,0:T(8,128)(2,1)S(1)}, bf16[8,512]{1,0:T(8,128)(2,1)S(1)}, u32[]{:S(2)}, u32[]{:S(2)}) collective-permute-start(bf16[8,512]{1,0:T(8,128)(2,1)S(1)} %pair.5.refs_0_), channel_id=1, source_target_pairs={{0,2},{2,0},{4,6},{6,4},{1,3},{3,1},{5,7},{7,5},{8,10},{10,8},{12,... | collective-permute-start | bytes 24584 | tf_op jit(solution)/shard_map/ppermute | solution.py:437
  105.4 1.1 collective-permute-done.27.refs_3_
  106.7 0.3 collective-permute-done.25.refs_1_
  107.4 1.5 %collective-permute-start.30 = (f32[8,128]{1,0:T(8,128)S(1)}, f32[8,128]{1,0:T(8,128)S(1)}, u32[]{:S(2)}, u32[]{:S(2)}) collective-permute-start(f32[8,128]{1,0:T(8,128)S(1)} %get-tuple-element.68.refs_0_), channel_id=1, source_target_pairs={{0,24},{8,16},{16,8},{24,0},{1,25},{9,17},{17,9},{25,1},{2,26},{10... | collective-permute-start | bytes 12296 | tf_op jit(solution)/shard_map/ppermute | solution.py:437
  108.8 0.7 collective-permute-start.29
  109.6 1.3 %collective-permute-start.28 = (f32[8,128]{1,0:T(8,128)S(1)}, f32[8,128]{1,0:T(8,128)S(1)}, u32[]{:S(2)}, u32[]{:S(2)}) collective-permute-start(f32[8,128]{1,0:T(8,128)S(1)} %get-tuple-element.68.refs_0_), channel_id=1, source_target_pairs={{0,8},{8,0},{16,24},{24,16},{1,9},{9,1},{17,25},{25,17},{2,10},{10... | collective-permute-start | bytes 12296 | tf_op jit(solution)/shard_map/ppermute | solution.py:437
  110.9 1.1 %own.1 = (f32[8,64]{1,0:T(8,128)S(1)}, f32[8,64]{1,0:T(8,128)S(1)}, f32[8,128]{1,0:T(8,128)S(1)}, f32[2,4,64]{2,1,0:T(4,128)}) custom-call(f32[8,512]{1,0:T(8,128)S(1)} %get-tuple-element.69.work_ref, f32[8,512]{1,0:T(8,128)S(1)} %get-tuple-element.70.vector_ref, f32[8,128]{1,0:T(8,128)S(1)} %get-tuple-element.57.refs_7_.refs_0_, ...), custom_call_target="tpu_custom_call" | custom-call | tf_op jit(solution)/shard_map/own/pallas_call | solution.py:401
  112.1 0.4 collective-permute-done.29.refs_2_
  112.4 0.7 collective-permute-done.28.refs_1_
  113.2 1.0 end.1
  (39 shorter events, 1.8 us)
Async XLA Ops:
  0.6 8.0 %copy-start.2 = (s32[16,16]{1,0:T(8,128)S(1)}, s32[16,16]{1,0:T(8,128)}, u32[]{:S(2)}) copy-start(s32[16,16]{1,0:T(8,128)} %mi_ref.1) | copy-start | bytes 3076
  0.6 12.0 %copy-start.1 = (bf16[4,512,512]{2,1,0:T(8,128)(2,1)S(1)}, bf16[4,512,512]{2,1,0:T(8,128)(2,1)}, u32[]{:S(2)}) copy-start(bf16[4,512,512]{2,1,0:T(8,128)(2,1)} %refs_10_.1) | copy-start | bytes 6291460
  1.6 1.4 %collective-permute-start = (f32[16,128]{1,0:T(8,128)S(1)}, f32[16,128]{1,0:T(8,128)S(1)}, u32[]{:S(2)}, u32[]{:S(2)}) collective-permute-start(f32[16,128]{1,0:T(8,128)S(1)} %begin.1.own_ref), channel_id=1, source_target_pairs={{0,1},{1,0},{2,3},{3,2},{4,5},{5,4},{6,7},{7,6},{8,9},{9,8},{10,11... | collective-permute-start | bytes 24584 | tf_op jit(solution)/shard_map/ppermute | solution.py:437
  3.1 6.6 %collective-permute-start.3 = (f32[24,128]{1,0:T(8,128)S(1)}, f32[24,128]{1,0:T(8,128)S(1)}, u32[]{:S(2)}, u32[]{:S(2)}) collective-permute-start(f32[24,128]{1,0:T(8,128)S(1)} %stack.1.refs_0_), channel_id=1, source_target_pairs={{0,6},{2,4},{4,2},{6,0},{1,7},{3,5},{5,3},{7,1},{8,14},{10,12},{12... | collective-permute-start | bytes 36872 | tf_op jit(solution)/shard_map/ppermute | solution.py:437
  8.0 4.6 %collective-permute-start.2 = (f32[24,128]{1,0:T(8,128)S(1)}, f32[24,128]{1,0:T(8,128)S(1)}, u32[]{:S(2)}, u32[]{:S(2)}) collective-permute-start(f32[24,128]{1,0:T(8,128)S(1)} %stack.1.refs_0_), channel_id=1, source_target_pairs={{0,4},{2,6},{4,0},{6,2},{1,5},{3,7},{5,1},{7,3},{8,12},{10,14},{12... | collective-permute-start | bytes 36872 | tf_op jit(solution)/shard_map/ppermute | solution.py:437
  8.0 4.6 %collective-permute-start.1 = (f32[24,128]{1,0:T(8,128)S(1)}, f32[24,128]{1,0:T(8,128)S(1)}, u32[]{:S(2)}, u32[]{:S(2)}) collective-permute-start(f32[24,128]{1,0:T(8,128)S(1)} %stack.1.refs_0_), channel_id=1, source_target_pairs={{0,2},{2,0},{4,6},{6,4},{1,3},{3,1},{5,7},{7,5},{8,10},{10,8},{12,... | collective-permute-start | bytes 36872 | tf_op jit(solution)/shard_map/ppermute | solution.py:437
  8.6 17.3 %slice-start = ((s8[16777216]{0:T(1024)(128)(4,1)}), s8[4194304]{0:T(1024)(128)(4,1)S(1)}, s32[]{:S(2)}) async-start(s8[16777216]{0:T(1024)(128)(4,1)} %bitcast.1), calls=%async_computation.3 | async-start | bytes 8388608
  8.9 17.0 %slice-start.1 = ((s8[16777216]{0:T(1024)(128)(4,1)}), s8[4194304]{0:T(1024)(128)(4,1)S(1)}, s32[]{:S(2)}) async-start(s8[16777216]{0:T(1024)(128)(4,1)} %bitcast.1), calls=%async_computation.4 | async-start | bytes 8388608
  8.9 17.0 %slice-start.2 = ((s8[16777216]{0:T(1024)(128)(4,1)}), s8[4194304]{0:T(1024)(128)(4,1)S(1)}, s32[]{:S(2)}) async-start(s8[16777216]{0:T(1024)(128)(4,1)} %bitcast.1), calls=%async_computation.5 | async-start | bytes 8388608
  9.0 17.0 %slice-start.3 = ((s8[16777216]{0:T(1024)(128)(4,1)}), s8[4194304]{0:T(1024)(128)(4,1)S(1)}, s32[]{:S(2)}) async-start(s8[16777216]{0:T(1024)(128)(4,1)} %bitcast.1), calls=%async_computation.6 | async-start | bytes 8388608
  25.6 2.8 %collective-permute-start.4 = (bf16[32,9,2,128]{3,2,1,0:T(2,128)(2,1)S(1)}, bf16[32,9,2,128]{3,2,1,0:T(2,128)(2,1)S(1)}, u32[]{:S(2)}, u32[]{:S(2)}) collective-permute-start(bf16[32,9,2,128]{3,2,1,0:T(2,128)(2,1)S(1)} %all_to_all.15.packet_ref.refs_1_), channel_id=1, source_target_pairs={{0,1},{1,0},{2,3},{3,2},{4,5},{5,4},{6,7},{7,6},{8,9},{9,8},{10,11... | collective-permute-start | bytes 442376 | tf_op jit(solution)/shard_map/ppermute | solution.py:437
  28.3 8.3 %copy-start = (bf16[4,512,512]{2,1,0:T(8,128)(2,1)S(1)}, bf16[4,512,512]{2,1,0:T(8,128)(2,1)}, u32[]{:S(2)}) copy-start(bf16[4,512,512]{2,1,0:T(8,128)(2,1)} %refs_4_.11) | copy-start | bytes 6291460
  30.9 13.6 %copy-start.3 = (f32[2]{0:T(128)S(1)}, f32[2]{0:T(128)}, u32[]{:S(2)}) copy-start(f32[2]{0:T(128)} %param.11) | copy-start | bytes 28
  30.9 4.6 %collective-permute-start.5 = (bf16[8,512]{1,0:T(8,128)(2,1)S(1)}, bf16[8,512]{1,0:T(8,128)(2,1)S(1)}, u32[]{:S(2)}, u32[]{:S(2)}) collective-permute-start(bf16[8,512]{1,0:T(8,128)(2,1)S(1)} %get-tuple-element.42), channel_id=1, source_target_pairs={{0,24},{8,16},{16,8},{24,0},{1,25},{9,17},{17,9},{25,1},{2,26},{10... | collective-permute-start | bytes 24584 | tf_op jit(solution)/shard_map/ppermute | solution.py:437
  31.6 3.9 %collective-permute-start.6 = (bf16[8,512]{1,0:T(8,128)(2,1)S(1)}, bf16[8,512]{1,0:T(8,128)(2,1)S(1)}, u32[]{:S(2)}, u32[]{:S(2)}) collective-permute-start(bf16[8,512]{1,0:T(8,128)(2,1)S(1)} %get-tuple-element.43), channel_id=1, source_target_pairs={{0,8},{8,0},{16,24},{24,16},{1,9},{9,1},{17,25},{25,17},{2,10},{10... | collective-permute-start | bytes 24584 | tf_op jit(solution)/shard_map/ppermute | solution.py:437
  33.0 3.7 %collective-permute-start.7 = (bf16[8,512]{1,0:T(8,128)(2,1)S(1)}, bf16[8,512]{1,0:T(8,128)(2,1)S(1)}, u32[]{:S(2)}, u32[]{:S(2)}) collective-permute-start(bf16[8,512]{1,0:T(8,128)(2,1)S(1)} %get-tuple-element.44), channel_id=1, source_target_pairs={{0,16},{8,24},{16,0},{24,8},{1,17},{9,25},{17,1},{25,9},{2,18},{10... | collective-permute-start | bytes 24584 | tf_op jit(solution)/shard_map/ppermute | solution.py:437
  37.3 1.2 %collective-permute-start.8 = (f32[8,512]{1,0:T(8,128)S(1)}, f32[8,512]{1,0:T(8,128)S(1)}, u32[]{:S(2)}, u32[]{:S(2)}) collective-permute-start(f32[8,512]{1,0:T(8,128)S(1)} %field.3.own_ref), channel_id=1, source_target_pairs={{0,1},{1,0},{2,3},{3,2},{4,5},{5,4},{6,7},{7,6},{8,9},{9,8},{10,11... | collective-permute-start | bytes 49160 | tf_op jit(solution)/shard_map/ppermute | solution.py:437
  38.5 5.4 %collective-permute-start.11 = (bf16[8,512]{1,0:T(8,128)(2,1)S(1)}, bf16[8,512]{1,0:T(8,128)(2,1)S(1)}, u32[]{:S(2)}, u32[]{:S(2)}) collective-permute-start(bf16[8,512]{1,0:T(8,128)(2,1)S(1)} %pair.3.refs_0_), channel_id=1, source_target_pairs={{0,6},{2,4},{4,2},{6,0},{1,7},{3,5},{5,3},{7,1},{8,14},{10,12},{12... | collective-permute-start | bytes 24584 | tf_op jit(solution)/shard_map/ppermute | solution.py:437
  39.6 4.5 %collective-permute-start.10 = (bf16[8,512]{1,0:T(8,128)(2,1)S(1)}, bf16[8,512]{1,0:T(8,128)(2,1)S(1)}, u32[]{:S(2)}, u32[]{:S(2)}) collective-permute-start(bf16[8,512]{1,0:T(8,128)(2,1)S(1)} %pair.3.refs_0_), channel_id=1, source_target_pairs={{0,4},{2,6},{4,0},{6,2},{1,5},{3,7},{5,1},{7,3},{8,12},{10,14},{12... | collective-permute-start | bytes 24584 | tf_op jit(solution)/shard_map/ppermute | solution.py:437
  40.5 4.0 %collective-permute-start.9 = (bf16[8,512]{1,0:T(8,128)(2,1)S(1)}, bf16[8,512]{1,0:T(8,128)(2,1)S(1)}, u32[]{:S(2)}, u32[]{:S(2)}) collective-permute-start(bf16[8,512]{1,0:T(8,128)(2,1)S(1)} %pair.3.refs_0_), channel_id=1, source_target_pairs={{0,2},{2,0},{4,6},{6,4},{1,3},{3,1},{5,7},{7,5},{8,10},{10,8},{12,... | collective-permute-start | bytes 24584 | tf_op jit(solution)/shard_map/ppermute | solution.py:437
  56.9 2.7 %collective-permute-start.12 = (bf16[32,9,2,128]{3,2,1,0:T(2,128)(2,1)S(1)}, bf16[32,9,2,128]{3,2,1,0:T(2,128)(2,1)S(1)}, u32[]{:S(2)}, u32[]{:S(2)}) collective-permute-start(bf16[32,9,2,128]{3,2,1,0:T(2,128)(2,1)S(1)} %all_to_all.16.packet_ref.refs_1_), channel_id=1, source_target_pairs={{0,1},{1,0},{2,3},{3,2},{4,5},{5,4},{6,7},{7,6},{8,9},{9,8},{10,11... | collective-permute-start | bytes 442376 | tf_op jit(solution)/shard_map/ppermute | solution.py:437
  62.2 4.6 %collective-permute-start.13 = (bf16[8,512]{1,0:T(8,128)(2,1)S(1)}, bf16[8,512]{1,0:T(8,128)(2,1)S(1)}, u32[]{:S(2)}, u32[]{:S(2)}) collective-permute-start(bf16[8,512]{1,0:T(8,128)(2,1)S(1)} %get-tuple-element.52), channel_id=1, source_target_pairs={{0,24},{8,16},{16,8},{24,0},{1,25},{9,17},{17,9},{25,1},{2,26},{10... | collective-permute-start | bytes 24584 | tf_op jit(solution)/shard_map/ppermute | solution.py:437
  62.9 3.9 %collective-permute-start.14 = (bf16[8,512]{1,0:T(8,128)(2,1)S(1)}, bf16[8,512]{1,0:T(8,128)(2,1)S(1)}, u32[]{:S(2)}, u32[]{:S(2)}) collective-permute-start(bf16[8,512]{1,0:T(8,128)(2,1)S(1)} %get-tuple-element.53), channel_id=1, source_target_pairs={{0,8},{8,0},{16,24},{24,16},{1,9},{9,1},{17,25},{25,17},{2,10},{10... | collective-permute-start | bytes 24584 | tf_op jit(solution)/shard_map/ppermute | solution.py:437
  64.3 3.7 %collective-permute-start.15 = (bf16[8,512]{1,0:T(8,128)(2,1)S(1)}, bf16[8,512]{1,0:T(8,128)(2,1)S(1)}, u32[]{:S(2)}, u32[]{:S(2)}) collective-permute-start(bf16[8,512]{1,0:T(8,128)(2,1)S(1)} %get-tuple-element.54), channel_id=1, source_target_pairs={{0,16},{8,24},{16,0},{24,8},{1,17},{9,25},{17,1},{25,9},{2,18},{10... | collective-permute-start | bytes 24584 | tf_op jit(solution)/shard_map/ppermute | solution.py:437
  68.6 1.2 %collective-permute-start.16 = (f32[8,512]{1,0:T(8,128)S(1)}, f32[8,512]{1,0:T(8,128)S(1)}, u32[]{:S(2)}, u32[]{:S(2)}) collective-permute-start(f32[8,512]{1,0:T(8,128)S(1)} %field.4.own_ref), channel_id=1, source_target_pairs={{0,1},{1,0},{2,3},{3,2},{4,5},{5,4},{6,7},{7,6},{8,9},{9,8},{10,11... | collective-permute-start | bytes 49160 | tf_op jit(solution)/shard_map/ppermute | solution.py:437
  69.8 5.4 %collective-permute-start.19 = (bf16[8,512]{1,0:T(8,128)(2,1)S(1)}, bf16[8,512]{1,0:T(8,128)(2,1)S(1)}, u32[]{:S(2)}, u32[]{:S(2)}) collective-permute-start(bf16[8,512]{1,0:T(8,128)(2,1)S(1)} %pair.4.refs_0_), channel_id=1, source_target_pairs={{0,6},{2,4},{4,2},{6,0},{1,7},{3,5},{5,3},{7,1},{8,14},{10,12},{12... | collective-permute-start | bytes 24584 | tf_op jit(solution)/shard_map/ppermute | solution.py:437
  70.9 4.5 %collective-permute-start.18 = (bf16[8,512]{1,0:T(8,128)(2,1)S(1)}, bf16[8,512]{1,0:T(8,128)(2,1)S(1)}, u32[]{:S(2)}, u32[]{:S(2)}) collective-permute-start(bf16[8,512]{1,0:T(8,128)(2,1)S(1)} %pair.4.refs_0_), channel_id=1, source_target_pairs={{0,4},{2,6},{4,0},{6,2},{1,5},{3,7},{5,1},{7,3},{8,12},{10,14},{12... | collective-permute-start | bytes 24584 | tf_op jit(solution)/shard_map/ppermute | solution.py:437
  71.8 4.0 %collective-permute-start.17 = (bf16[8,512]{1,0:T(8,128)(2,1)S(1)}, bf16[8,512]{1,0:T(8,128)(2,1)S(1)}, u32[]{:S(2)}, u32[]{:S(2)}) collective-permute-start(bf16[8,512]{1,0:T(8,128)(2,1)S(1)} %pair.4.refs_0_), channel_id=1, source_target_pairs={{0,2},{2,0},{4,6},{6,4},{1,3},{3,1},{5,7},{7,5},{8,10},{10,8},{12,... | collective-permute-start | bytes 24584 | tf_op jit(solution)/shard_map/ppermute | solution.py:437
  88.2 2.7 %collective-permute-start.20 = (bf16[32,9,2,128]{3,2,1,0:T(2,128)(2,1)S(1)}, bf16[32,9,2,128]{3,2,1,0:T(2,128)(2,1)S(1)}, u32[]{:S(2)}, u32[]{:S(2)}) collective-permute-start(bf16[32,9,2,128]{3,2,1,0:T(2,128)(2,1)S(1)} %all_to_all.17.packet_ref.refs_1_), channel_id=1, source_target_pairs={{0,1},{1,0},{2,3},{3,2},{4,5},{5,4},{6,7},{7,6},{8,9},{9,8},{10,11... | collective-permute-start | bytes 442376 | tf_op jit(solution)/shard_map/ppermute | solution.py:437
  93.5 4.6 %collective-permute-start.21 = (bf16[8,512]{1,0:T(8,128)(2,1)S(1)}, bf16[8,512]{1,0:T(8,128)(2,1)S(1)}, u32[]{:S(2)}, u32[]{:S(2)}) collective-permute-start(bf16[8,512]{1,0:T(8,128)(2,1)S(1)} %get-tuple-element.61), channel_id=1, source_target_pairs={{0,24},{8,16},{16,8},{24,0},{1,25},{9,17},{17,9},{25,1},{2,26},{10... | collective-permute-start | bytes 24584 | tf_op jit(solution)/shard_map/ppermute | solution.py:437
  94.2 3.9 %collective-permute-start.22 = (bf16[8,512]{1,0:T(8,128)(2,1)S(1)}, bf16[8,512]{1,0:T(8,128)(2,1)S(1)}, u32[]{:S(2)}, u32[]{:S(2)}) collective-permute-start(bf16[8,512]{1,0:T(8,128)(2,1)S(1)} %get-tuple-element.62), channel_id=1, source_target_pairs={{0,8},{8,0},{16,24},{24,16},{1,9},{9,1},{17,25},{25,17},{2,10},{10... | collective-permute-start | bytes 24584 | tf_op jit(solution)/shard_map/ppermute | solution.py:437
  95.5 3.7 %collective-permute-start.23 = (bf16[8,512]{1,0:T(8,128)(2,1)S(1)}, bf16[8,512]{1,0:T(8,128)(2,1)S(1)}, u32[]{:S(2)}, u32[]{:S(2)}) collective-permute-start(bf16[8,512]{1,0:T(8,128)(2,1)S(1)} %get-tuple-element.63), channel_id=1, source_target_pairs={{0,16},{8,24},{16,0},{24,8},{1,17},{9,25},{17,1},{25,9},{2,18},{10... | collective-permute-start | bytes 24584 | tf_op jit(solution)/shard_map/ppermute | solution.py:437
  99.8 1.2 %collective-permute-start.24 = (f32[8,512]{1,0:T(8,128)S(1)}, f32[8,512]{1,0:T(8,128)S(1)}, u32[]{:S(2)}, u32[]{:S(2)}) collective-permute-start(f32[8,512]{1,0:T(8,128)S(1)} %field.5.own_ref), channel_id=1, source_target_pairs={{0,1},{1,0},{2,3},{3,2},{4,5},{5,4},{6,7},{7,6},{8,9},{9,8},{10,11... | collective-permute-start | bytes 49160 | tf_op jit(solution)/shard_map/ppermute | solution.py:437
  101.0 5.4 %collective-permute-start.27 = (bf16[8,512]{1,0:T(8,128)(2,1)S(1)}, bf16[8,512]{1,0:T(8,128)(2,1)S(1)}, u32[]{:S(2)}, u32[]{:S(2)}) collective-permute-start(bf16[8,512]{1,0:T(8,128)(2,1)S(1)} %pair.5.refs_0_), channel_id=1, source_target_pairs={{0,6},{2,4},{4,2},{6,0},{1,7},{3,5},{5,3},{7,1},{8,14},{10,12},{12... | collective-permute-start | bytes 24584 | tf_op jit(solution)/shard_map/ppermute | solution.py:437
  102.1 4.5 %collective-permute-start.26 = (bf16[8,512]{1,0:T(8,128)(2,1)S(1)}, bf16[8,512]{1,0:T(8,128)(2,1)S(1)}, u32[]{:S(2)}, u32[]{:S(2)}) collective-permute-start(bf16[8,512]{1,0:T(8,128)(2,1)S(1)} %pair.5.refs_0_), channel_id=1, source_target_pairs={{0,4},{2,6},{4,0},{6,2},{1,5},{3,7},{5,1},{7,3},{8,12},{10,14},{12... | collective-permute-start | bytes 24584 | tf_op jit(solution)/shard_map/ppermute | solution.py:437
  103.0 4.0 %collective-permute-start.25 = (bf16[8,512]{1,0:T(8,128)(2,1)S(1)}, bf16[8,512]{1,0:T(8,128)(2,1)S(1)}, u32[]{:S(2)}, u32[]{:S(2)}) collective-permute-start(bf16[8,512]{1,0:T(8,128)(2,1)S(1)} %pair.5.refs_0_), channel_id=1, source_target_pairs={{0,2},{2,0},{4,6},{6,4},{1,3},{3,1},{5,7},{7,5},{8,10},{10,8},{12,... | collective-permute-start | bytes 24584 | tf_op jit(solution)/shard_map/ppermute | solution.py:437
  107.4 4.7 %collective-permute-start.30 = (f32[8,128]{1,0:T(8,128)S(1)}, f32[8,128]{1,0:T(8,128)S(1)}, u32[]{:S(2)}, u32[]{:S(2)}) collective-permute-start(f32[8,128]{1,0:T(8,128)S(1)} %get-tuple-element.68.refs_0_), channel_id=1, source_target_pairs={{0,24},{8,16},{16,8},{24,0},{1,25},{9,17},{17,9},{25,1},{2,26},{10... | collective-permute-start | bytes 12296 | tf_op jit(solution)/shard_map/ppermute | solution.py:437
  108.8 3.6 %collective-permute-start.29 = (f32[8,128]{1,0:T(8,128)S(1)}, f32[8,128]{1,0:T(8,128)S(1)}, u32[]{:S(2)}, u32[]{:S(2)}) collective-permute-start(f32[8,128]{1,0:T(8,128)S(1)} %get-tuple-element.68.refs_0_), channel_id=1, source_target_pairs={{0,16},{8,24},{16,0},{24,8},{1,17},{9,25},{17,1},{25,9},{2,18},{10... | collective-permute-start | bytes 12296 | tf_op jit(solution)/shard_map/ppermute | solution.py:437
  109.6 3.6 %collective-permute-start.28 = (f32[8,128]{1,0:T(8,128)S(1)}, f32[8,128]{1,0:T(8,128)S(1)}, u32[]{:S(2)}, u32[]{:S(2)}) collective-permute-start(f32[8,128]{1,0:T(8,128)S(1)} %get-tuple-element.68.refs_0_), channel_id=1, source_target_pairs={{0,8},{8,0},{16,24},{24,16},{1,9},{9,1},{17,25},{25,17},{2,10},{10... | collective-permute-start | bytes 12296 | tf_op jit(solution)/shard_map/ppermute | solution.py:437
